TPU v7x, 32 devices: a whole 2x2x4 slice. The times are simulated.
32 devices in a mesh: space: 8 (over z, y), slab: 4 (over x, core).
Axes of the slice: x: 2, y: 2, z: 4, core: 2. Of those that a mesh axis runs over, the one named last changes fastest.
Arguments:
- displacement: float32 [3, 128, 32, 256], P(None, 'space', 'slab'), may hold values from -0.1 to 0.1
- velocity: float32 [3, 128, 32, 256], P(None, 'space', 'slab'), may hold values from -6 to 6
- stress: float32 [6, 128, 32, 256], P(None, 'space', 'slab'), may hold values from -6 to 6
- hourglass: float32 [128, 32, 256], P('space', 'slab'), may hold values from 0.02 to 0.2
- mass: float32 [128, 32, 256], P('space', 'slab'), may hold values from 1 to 4
- contact_route: int32 [8192], P(('space', 'slab')), may hold values from 0 to 383, as said below
- pair_nodes: int32 [5, 32768], P(None, ('space', 'slab')), may hold values from 0 to 383, as said below
- pair_diagonals: float32 [6, 32768], P(None, ('space', 'slab')), may hold values from -5 to 5
- pair_gap: float32 [32768], P(('space', 'slab')), may hold values from -0.3 to 0.3
- pair_stiffness: float32 [32768], P(('space', 'slab')), may hold values from 1 to 10
Outputs:
- velocity_new: float32 [3, 128, 32, 256], P(None, 'space', 'slab')
Inputs may be any that keep to these rules, and one draw needn't show every extreme that they name: `contact_route`: values of one device are distinct; value // 48 is the space index of the contact owner (same slab index), value % 48 the slot. In every draw one owner receives all 48 slots from every device of its group, and every owner receives a slot from the device of its own indices. `pair_nodes`: entries of the pairs of one owner name slots that are filled at that owner; entries of one pair need not differ.
All inputs are finite; a program needn't handle non-finite values.
Results may differ from a plain program's by a relative error of at most 0.0003.
Values sent between devices are 32-bit elements; how exact they have to be, the bound alone decides.
No kernel may reach another device: no remote copies, remote signals or barrier semaphores. Data moves between devices by JAX's collectives and lax.ppermute only.
A program may use at most 64 MiB of HBM per device.

v0:
```python
import functools

import jax
import jax.numpy as jnp
from jax import lax
from jax.experimental import pallas as pl
from jax.experimental.pallas import tpu as pltpu
from jax.sharding import PartitionSpec as P


time_step = 0.5
LANES = 128
VOIGT = [[0, 5, 4], [5, 1, 3], [4, 3, 2]]


def shifted(value, axis, steps):
    count = lax.axis_size(axis)
    return lax.ppermute(value, axis, [(at, (at + steps) % count) for at in range(count)])


def exchanged(value):
    return lax.all_to_all(value, "space", split_axis=0, concat_axis=0, tiled=True)


def kernel_call(body, inputs, outs, scratch=(), hbm_inputs=0, final=False):
    vmem = pl.BlockSpec(memory_space=pltpu.VMEM)
    hbm = pl.BlockSpec(memory_space=pltpu.HBM)
    spaces = [pltpu.HBM if at < hbm_inputs else pltpu.VMEM for at in range(len(inputs))]
    inputs = [pltpu.with_memory_space_constraint(*pair) for pair in zip(inputs, spaces)]
    space = pltpu.HBM if final else pltpu.VMEM
    return pl.pallas_call(
        body,
        out_shape=jax.tree.map(lambda out: space(out.shape, out.dtype), outs),
        in_specs=[pl.BlockSpec(memory_space=one) for one in spaces],
        out_specs=jax.tree.map(lambda _: hbm if final else vmem, outs),
        scratch_shapes=list(scratch),
        compiler_params=pltpu.CompilerParams(vmem_limit_bytes=16 << 20),
    )(*inputs)


def contract_lanes(lhs, rhs):
    return lax.dot_general(lhs, rhs, (((1,), (1,)), ((), ())), preferred_element_type=jnp.float32)


def layout(nspace, surf_count):
    capacity = max(2, (3 * surf_count // 2 + nspace - 1) // nspace)
    pack = max(1, min(LANES // capacity, nspace // 8))
    while nspace % pack:
        pack -= 1
    return capacity, pack, nspace // pack


def block_of(slots, width, blocks):
    block = jnp.zeros_like(slots)
    for b in range(1, blocks):
        block = block + jnp.where(slots >= b * width, 1, 0)
    return block, slots - block * width


def parts_of(rows):
    high = rows.astype(jnp.bfloat16).astype(jnp.float32)
    rest = rows - high
    middle = rest.astype(jnp.bfloat16).astype(jnp.float32)
    return [high, middle, rest - middle]


def places(place, width):
    rows = (width + 15) // 16 * 16
    count = place.shape[1]
    at = lax.broadcasted_iota(jnp.int32, (rows, count), 0)
    return jnp.where(at == place, 1.0, 0.0).astype(jnp.bfloat16)


def spread(parts, block, blocks):
    return [
        jnp.where(block == b, part, 0.0).astype(jnp.bfloat16)
        for part in parts
        for b in range(blocks)
    ]


def write_messages(out_ref, got, pack, blocks):
    for b in range(blocks):
        at = [(part * blocks + b) * 8 for part in range(3)]
        total = got[at[0] : at[0] + 8] + got[at[1] : at[1] + 8] + got[at[2] : at[2] + 8]
        for q in range(pack):
            out_ref[b * pack + q, :, 0 : total.shape[1]] = total


def first_body(
    capacity, pack, blocks, u_hbm, v_hbm, stress_hbm, hour_hbm, mass_hbm, route_hbm,
    out_ref, ydn, yup, sides_ref, u_ref, v_ref, stress_ref, hour_ref, mass_ref, rows_ref, route_ref, sems,
):
    copies = [
        pltpu.make_async_copy(source, target, sems.at[at])
        for at, (source, target) in enumerate(
            (
                (u_hbm, u_ref),
                (route_hbm, route_ref),
                (v_hbm, v_ref),
                (stress_hbm, stress_ref),
                (hour_hbm, hour_ref),
                (mass_hbm, mass_ref),
            )
        )
    ]
    for copy in copies:
        copy.start()
    out_ref[...] = jnp.zeros(out_ref.shape, jnp.float32)
    rows_ref[...] = jnp.zeros(rows_ref.shape, jnp.float32)
    copies[0].wait()
    copies[1].wait()
    planes, columns, depth = u_ref.shape[1:]
    side = planes * columns
    lane = lax.broadcasted_iota(jnp.int32, (side, LANES), 1)
    for c in range(3):
        bottom = u_ref[c, :, :, 0:LANES].reshape(side, LANES)
        top = u_ref[c, :, :, depth - LANES : depth].reshape(side, LANES)
        both = jnp.where(lane == LANES - 1, top, bottom).T
        rows_ref[c : c + 1, 0:side] = both[0:1]
        rows_ref[c : c + 1, side : 2 * side] = both[LANES - 1 : LANES]
    width = pack * capacity
    route = route_ref[...]
    sides_ref[0:1, :] = route[:, 0:side]
    sides_ref[1:2, :] = route[:, side : 2 * side]
    block, place = block_of(route, width, blocks)
    entries = spread(parts_of(rows_ref[...]), block, blocks)
    got = contract_lanes(jnp.concatenate(entries, 0), places(place, width))
    write_messages(out_ref, got, pack, blocks)
    for copy in copies[2:]:
        copy.wait()
    for c in range(13):
        ref = component(u_ref, v_ref, stress_ref, hour_ref, c)
        yup[c] = ref[:, columns - 1, :]
        if c < 6:
            ydn[c] = ref[:, 0, :]


def component(u_ref, v_ref, stress_ref, hour_ref, c):
    if c < 3:
        return u_ref.at[c]
    if c < 6:
        return v_ref.at[c - 3]
    if c < 12:
        return stress_ref.at[c - 6]
    return hour_ref


def second_body(u_ref, v_ref, stress_ref, hour_ref, yu, yd, xdn, xup):
    planes, columns = u_ref.shape[1:3]
    base = 13 * columns
    for c in range(13):
        ref = component(u_ref, v_ref, stress_ref, hour_ref, c)
        xup[c * columns : (c + 1) * columns, :] = ref[planes - 1]
        xup[base + c : base + c + 1, :] = yd[c, planes - 1 : planes, :]
    for c in range(6):
        ref = component(u_ref, v_ref, stress_ref, hour_ref, c)
        xup[base + 13 + c : base + 14 + c, :] = yu[c, planes - 1 : planes, :]
        xdn[c * columns : (c + 1) * columns, :] = ref[0]
        at = 6 * columns + c
        xdn[at : at + 1, :] = yd[c, 0:1, :]
        xdn[at + 6 : at + 7, :] = yu[c, 0:1, :]


def places_body(
    width, blocks, nodes_hbm, diag_hbm, gap_hbm, stiff_hbm,
    place_ref, block_ref, lines_ref, diag_lines_ref, gap_ref, stiff_ref, nodes_ref, diag_ref, sems,
):
    copies = [
        pltpu.make_async_copy(source, target, sems.at[at])
        for at, (source, target) in enumerate(
            (
                (nodes_hbm, nodes_ref),
                (diag_hbm, diag_ref),
                (gap_hbm, gap_ref),
                (stiff_hbm, stiff_ref),
            )
        )
    ]
    for copy in copies:
        copy.start()
    for copy in copies:
        copy.wait()
    pairs = nodes_ref.shape[1]
    for j in range(5):
        nodes = nodes_ref[j : j + 1, :]
        block, place = block_of(nodes, width, blocks)
        block_ref[j : j + 1, :] = block
        place_ref[:, j * pairs : (j + 1) * pairs] = places(place, width)
        for r in range(pairs // LANES):
            lines_ref[j, r : r + 1, :] = nodes[:, r * LANES : (r + 1) * LANES]
    for c in range(6):
        for r in range(pairs // LANES):
            diag_lines_ref[c, r : r + 1, :] = diag_ref[c : c + 1, r * LANES : (r + 1) * LANES]


def looked_up(table_ref, slots, capacity, offset, count):
    shape = slots[0].shape

    def step(s, found):
        shift = s * capacity - offset
        result = []
        for slot, old in zip(slots, found):
            here = (slot >= s * capacity) & (slot < (s + 1) * capacity)
            index = (slot - shift) & (LANES - 1)
            new = []
            for c in range(3):
                row = jnp.broadcast_to(table_ref[s, c : c + 1, :], shape)
                new.append(jnp.where(here, jnp.take_along_axis(row, index, axis=1), old[c]))
            result.append(tuple(new))
        return tuple(result)

    zero = jnp.zeros(shape, jnp.float32)
    found = tuple((zero, zero, zero) for _ in slots)
    if count <= 16:
        for s in range(count):
            found = step(s, found)
        return found
    return lax.fori_loop(0, count, step, found)


def pair_body(
    nspace, capacity, pack, blocks, table_ref, nodes_ref, diag_ref, gap_ref, stiff_ref, place_ref,
    block_ref, out_ref, rows_ref, entry_ref,
):
    offset = (lax.axis_index("space") % pack) * capacity
    picked = looked_up(table_ref, [nodes_ref[j] for j in range(5)], capacity, offset, nspace)
    slave = picked[0]
    first = [diag_ref[c] + picked[3][c] - picked[1][c] for c in range(3)]
    second = [diag_ref[3 + c] + picked[4][c] - picked[2][c] for c in range(3)]
    normal = [
        first[(c + 1) % 3] * second[(c + 2) % 3] - first[(c + 2) % 3] * second[(c + 1) % 3]
        for c in range(3)
    ]
    gap = gap_ref[...]
    for c in range(3):
        centre = (picked[1][c] + picked[2][c] + picked[3][c] + picked[4][c]) * 0.25
        gap = gap + (slave[c] - centre) * normal[c]
    push = stiff_ref[...] * jnp.maximum(-gap, 0.0)
    pairs = rows_ref.shape[1]
    rows_ref[...] = jnp.zeros(rows_ref.shape, jnp.float32)
    for c in range(3):
        force = push * normal[c]
        for r in range(force.shape[0]):
            rows_ref[c : c + 1, r * LANES : (r + 1) * LANES] = force[r : r + 1]
    parts = parts_of(rows_ref[...])
    fourth = [part * -0.25 for part in parts]
    for j in range(5):
        entries = spread(fourth if j else parts, block_ref[j : j + 1, :], blocks)
        entry_ref[:, j * pairs : (j + 1) * pairs] = jnp.concatenate(entries, 0)
    out_ref[...] = jnp.zeros(out_ref.shape, jnp.float32)
    got = contract_lanes(entry_ref[...], place_ref[...])
    write_messages(out_ref, got, pack, blocks)


def split(value):
    return jnp.stack([value[:, at : at + LANES] for at in range(0, value.shape[1], LANES)])


def z_pair(f):
    lane = lax.broadcasted_iota(jnp.int32, f.shape, 2)
    turned = pltpu.roll(f, LANES - 1, 2)
    after = jnp.concatenate([turned[1:], turned[:1]], 0)
    upper = jnp.where(lane == LANES - 1, after, turned)
    return f + upper, upper - f


def node_terms(sums, diffs, sums_next, diffs_next):
    result = []
    for c in range(6):
        s0, s1, d0, d1 = sums[c], sums_next[c], diffs[c], diffs_next[c]
        if c < 3:
            result.append((s0 + s1, s1 - s0, d0 + d1))
        else:
            result.append((d1 - d0, d0 + d1, s1 - s0))
    return result


def element_terms(lower, upper, stress, hour):
    eight = []
    for m in range(3):
        row = [
            upper[m][0] - lower[m][0],
            lower[m][1] + upper[m][1],
            lower[m][2] + upper[m][2],
        ]
        row[m] = row[m] + 4.0
        eight.append(row)
    cof = [
        [
            eight[(m + 1) % 3][(n + 1) % 3] * eight[(m + 2) % 3][(n + 2) % 3]
            - eight[(m + 1) % 3][(n + 2) % 3] * eight[(m + 2) % 3][(n + 1) % 3]
            for n in range(3)
        ]
        for m in range(3)
    ]
    hour = hour * 64.0
    result = []
    for m in range(3):
        line = [
            stress[VOIGT[m][0]] * cof[0][n]
            + stress[VOIGT[m][1]] * cof[1][n]
            + stress[VOIGT[m][2]] * cof[2][n]
            for n in range(3)
        ]
        low, up = lower[3 + m], upper[3 + m]
        line.append(hour * (low[0] + up[0]))
        line.append(hour * (up[1] - low[1]))
        line.append(hour * (up[2] - low[2]))
        line.append(hour * (up[0] - low[0]))
        result.append(line)
    return result


def gathered_x(before, after):
    result = []
    for m in range(3):
        p, n = before[m], after[m]
        result.append(
            (
                p[0] - n[0],
                (p[1] + n[1]) + (p[5] - n[5]),
                (p[2] + n[2]) + (p[4] - n[4]),
                (p[3] + n[3]) + (p[6] - n[6]),
            )
        )
    return result


def element_body(
    u_ref, v_ref, stress_ref, hour_ref, mass_ref, ydn, yu, yd, xu, xd,
    out_ref, row_ref, halo_s, halo_d, edge_ref, node_ref, elem_ref,
):
    planes, columns, depth = u_ref.shape[1:]
    nb = depth // LANES
    rows = row_ref.shape[0]

    def below(c):
        return xd[c * columns : (c + 1) * columns, :]

    def above(c):
        return xu[c * columns : (c + 1) * columns, :]

    def assembled(first, middle, last):
        row_ref[0:1, :] = first
        row_ref[1 : planes + 1, :] = middle
        if last is not None:
            row_ref[planes + 1 : planes + 2, :] = last
        return split(row_ref[...])

    def line(ref, at):
        return ref[at : at + 1, :]

    row_ref[...] = jnp.zeros(row_ref.shape, jnp.float32)
    base = 13 * columns
    left_s, left_d, mid_s, mid_d = [], [], [], []
    for c in range(6):
        right = assembled(line(xd, base + 13 + c), yu[c], line(xu, 6 * columns + 6 + c))
        s, d = z_pair(right)
        halo_s[c] = s
        halo_d[c] = d
        s, d = z_pair(assembled(line(xd, base + c), yd[c], line(xu, 6 * columns + c)))
        left_s.append(s)
        left_d.append(d)
        s, d = z_pair(assembled(line(xd, c * columns), ydn[c], line(xu, c * columns)))
        mid_s.append(s)
        mid_d.append(d)
    side = node_terms(left_s, left_d, mid_s, mid_d)
    stress = [assembled(line(xd, base + 6 + c), yd[6 + c], None) for c in range(6)]
    hour = assembled(line(xd, base + 12), yd[12], None)
    next_side = [tuple(pltpu.roll(q, rows - 1, 1) for q in terms) for terms in side]
    factors = element_terms(side, next_side, stress, hour)
    upper = [[pltpu.roll(q, rows - 1, 1) for q in terms] for terms in factors]
    for m, (a, b, c, e) in enumerate(gathered_x(factors, upper)):
        edge_ref[m, 0] = a + b
        edge_ref[m, 1] = c + e

    row = lax.broadcasted_iota(jnp.int32, (nb, columns, LANES), 1)
    lane = lax.broadcasted_iota(jnp.int32, (nb, columns, LANES), 2)
    block = lax.broadcasted_iota(jnp.int32, (nb, columns, LANES), 0)

    def node_plane(values, at):
        sums, diffs, sums_next, diffs_next = [], [], [], []
        for c in range(6):
            s, d = z_pair(values[c])
            sums.append(s)
            diffs.append(d)
            hs = halo_s[c, :, pl.ds(at, 1), :]
            hd = halo_d[c, :, pl.ds(at, 1), :]
            sums_next.append(jnp.where(row == columns - 1, hs, pltpu.roll(s, columns - 1, 1)))
            diffs_next.append(jnp.where(row == columns - 1, hd, pltpu.roll(d, columns - 1, 1)))
        return node_terms(sums, diffs, sums_next, diffs_next)

    def keep_nodes(terms):
        for c in range(6):
            for t in range(3):
                node_ref[c, t] = terms[c][t]

    def kept_nodes():
        return [tuple(node_ref[c, t] for t in range(3)) for c in range(6)]

    def keep_elements(factors):
        for m in range(3):
            for t in range(7):
                elem_ref[m, t] = factors[m][t]

    def kept_elements():
        return [[elem_ref[m, t] for t in range(7)] for m in range(3)]

    def write_plane(before, after, i):
        weight = (time_step / 64.0) / split(mass_ref[i])
        for m, (a, b, c, e) in enumerate(gathered_x(before, after)):
            ab = edge_ref[m, 0, :, pl.ds(i, 1), :]
            ce = edge_ref[m, 1, :, pl.ds(i, 1), :]
            p = (a - b) + jnp.where(row == 0, ab, pltpu.roll(a + b, 1, 1))
            r = (c - e) + jnp.where(row == 0, ce, pltpu.roll(c + e, 1, 1))
            up = pltpu.roll(p + r, 1, 2)
            before_up = jnp.concatenate([jnp.zeros_like(up[:1]), up[:-1]], 0)
            force = jnp.where(lane == 0, before_up, up)
            last = (lane == LANES - 1) & (block == nb - 1)
            force = force + jnp.where(last, 0.0, p - r)
            result = split(v_ref[m, i]) - force * weight
            for k in range(nb):
                out_ref[m, i, :, k * LANES : (k + 1) * LANES] = result[k]

    def own_nodes(i):
        return [split(u_ref[c, i]) for c in range(3)] + [split(v_ref[c, i]) for c in range(3)]

    keep_nodes(node_plane([split(below(c)) for c in range(6)], 0))
    current = node_plane(own_nodes(0), 1)
    keep_elements(
        element_terms(
            kept_nodes(), current, [split(below(6 + c)) for c in range(6)], split(below(12))
        )
    )
    keep_nodes(current)

    def step(i, upper):
        factors = element_terms(
            kept_nodes(), upper, [split(stress_ref[c, i - 1]) for c in range(6)], split(hour_ref[i - 1])
        )
        write_plane(kept_elements(), factors, i - 1)
        keep_elements(factors)
        keep_nodes(upper)

    def loop(i, carry):
        step(i, node_plane(own_nodes(i), i + 1))
        return carry

    lax.fori_loop(1, planes, loop, 0)
    step(planes, node_plane([split(above(c)) for c in range(6)], planes + 1))


def final_body(
    nspace, capacity, pack, base_ref, mass_ref, table_ref, route_ref, out_hbm, rows_ref, out_ref, sems
):
    planes, columns, depth = base_ref.shape[1:]
    offset = (lax.axis_index("space") % pack) * capacity
    (contact,) = looked_up(table_ref, [route_ref[...]], capacity, offset, nspace)
    rows_ref[...] = jnp.zeros(rows_ref.shape, jnp.float32)
    lane = lax.broadcasted_iota(jnp.int32, (planes, columns, LANES), 2)
    low_weight = jnp.where(lane == 0, time_step / mass_ref[:, :, 0:LANES], 0.0)
    high_weight = jnp.where(
        lane == LANES - 1, time_step / mass_ref[:, :, depth - LANES : depth], 0.0
    )
    copies = []
    for m in range(3):
        rows_ref[m, 0:1, :] = contact[m][0:1]
        rows_ref[m, LANES - 1 : LANES, :] = contact[m][1:2]
        turned = rows_ref[m].T.reshape(planes, columns, LANES)
        for k in range(0, depth, LANES):
            value = base_ref[m, :, :, k : k + LANES]
            if k == 0:
                value = value + low_weight * turned
            if k == depth - LANES:
                value = value + high_weight * turned
            out_ref[m, :, :, k : k + LANES] = value
        copies.append(pltpu.make_async_copy(out_ref.at[m], out_hbm.at[m], sems.at[m]))
        copies[m].start()
    for copy in copies:
        copy.wait()


def local(
    displacement,
    velocity,
    stress,
    hourglass,
    mass,
    contact_route,
    pair_nodes,
    pair_diagonals,
    pair_gap,
    pair_stiffness,
):
    planes, columns, depth = displacement.shape[1:]
    nspace = lax.axis_size("space")
    surf_count = 2 * planes * columns
    pairs = pair_nodes.shape[1]
    capacity, pack, blocks = layout(nspace, surf_count)
    f32 = jnp.float32
    lines = pairs // LANES

    def sized(*shape):
        return jax.ShapeDtypeStruct(shape, f32)

    message = sized(nspace, 8, LANES)
    width = pack * capacity
    whole = jax.ShapeDtypeStruct((5, pairs), jnp.int32)
    place, block, nodes, diagonals, gap, stiffness = kernel_call(
        functools.partial(places_body, width, blocks),
        (
            pair_nodes,
            pair_diagonals,
            pair_gap.reshape(lines, LANES),
            pair_stiffness.reshape(lines, LANES),
        ),
        (
            jax.ShapeDtypeStruct(((width + 15) // 16 * 16, 5 * pairs), jnp.bfloat16),
            whole,
            jax.ShapeDtypeStruct((5, lines, LANES), jnp.int32),
            sized(6, lines, LANES),
            sized(lines, LANES),
            sized(lines, LANES),
        ),
        [
            pltpu.VMEM(whole.shape, jnp.int32),
            pltpu.VMEM((6, pairs), f32),
            pltpu.SemaphoreType.DMA((4,)),
        ],
        hbm_inputs=4,
    )
    fields = (displacement, velocity, stress, hourglass, mass)
    outgoing, ydn, yup, sides, *fields = kernel_call(
        functools.partial(first_body, capacity, pack, blocks),
        (*fields, contact_route.reshape(1, surf_count)),
        (
            message,
            sized(6, planes, depth),
            sized(13, planes, depth),
            jax.ShapeDtypeStruct((2, surf_count // 2), jnp.int32),
            *(sized(*field.shape) for field in fields),
        ),
        [
            pltpu.VMEM((8, surf_count), f32),
            pltpu.VMEM((1, surf_count), jnp.int32),
            pltpu.SemaphoreType.DMA((6,)),
        ],
        hbm_inputs=6,
    )
    yu = shifted(ydn, "slab", -1)
    yd = shifted(yup, "slab", 1)
    received = exchanged(outgoing)
    xdn, xup = kernel_call(
        second_body,
        (*fields[:4], yu, yd),
        (
            sized((6 * columns + 12 + 7) // 8 * 8, depth),
            sized((13 * columns + 19 + 7) // 8 * 8, depth),
        ),
    )
    xu = shifted(xdn, "space", -1)
    xd = shifted(xup, "space", 1)
    slot_force = kernel_call(
        functools.partial(pair_body, nspace, capacity, pack, blocks),
        (
            received,
            nodes,
            diagonals,
            gap,
            stiffness,
            place,
            block,
        ),
        message,
        [pltpu.VMEM((8, pairs), f32), pltpu.VMEM((24 * blocks, 5 * pairs), jnp.bfloat16)],
    )
    returned = exchanged(slot_force)

    nb = depth // LANES
    rows = (planes + 2 + 7) // 8 * 8
    base = kernel_call(
        element_body,
        (*fields, ydn, yu, yd, xu, xd),
        sized(*displacement.shape),
        [
            pltpu.VMEM((rows, depth), f32),
            pltpu.VMEM((6, nb, rows, LANES), f32),
            pltpu.VMEM((6, nb, rows, LANES), f32),
            pltpu.VMEM((3, 2, nb, rows, LANES), f32),
            pltpu.VMEM((6, 3, nb, columns, LANES), f32),
            pltpu.VMEM((3, 7, nb, columns, LANES), f32),
        ],
    )

    return kernel_call(
        functools.partial(final_body, nspace, capacity, pack),
        (base, fields[4], returned, sides),
        sized(*displacement.shape),
        [
            pltpu.VMEM((3, LANES, LANES), f32),
            pltpu.VMEM(displacement.shape, f32),
            pltpu.SemaphoreType.DMA((3,)),
        ],
        final=True,
    )


def solution(mesh):
    in_specs = (
        P(None, "space", "slab", None),
        P(None, "space", "slab", None),
        P(None, "space", "slab", None),
        P("space", "slab", None),
        P("space", "slab", None),
        P(("space", "slab")),
        P(None, ("space", "slab")),
        P(None, ("space", "slab")),
        P(("space", "slab")),
        P(("space", "slab")),
    )
    out_specs = P(None, "space", "slab", None)
    return jax.shard_map(local, mesh=mesh, in_specs=in_specs, out_specs=out_specs, check_vma=False)
```

profile of v0, /device:TPU:0, one launch (start us, length us, event | category | flops | bytes accessed | tf_op | source)
XLA Modules:
  0.0 35.6 jit_solution(13659795109477530419)
XLA Ops:
  0.0 2.2 %shard_map.100 = (f32[8,8,128]{2,1,0:T(8,128)}, f32[6,16,256]{2,1,0:T(8,128)S(1)}, f32[13,16,256]{2,1,0:T(8,128)S(1)}, s32[2,128]{1,0:T(2,128)S(1)}, f32[3,16,8,...) custom-call(f32[3,16,8,256]{3,2,1,0:T(8,128)} %u_hbm.1, ...), custom_call_target="tpu_custom_call" | custom-call | tf_op jit(solution)/shard_map/pallas_call | solution.py:31
  2.2 0.5 %collective-permute-start.1 = (f32[13,16,256]{2,1,0:T(8,128)S(1)}, f32[13,16,256]{2,1,0:T(8,128)S(1)}, u32[]{:S(2)}, u32[]{:S(2)}) collective-permute-start(f32[13,16,256]{2,1,0:T(8,128)S(1)} %get-tuple-element.28), channel_id=1, source_target_pairs={{0,1},{1,2},{2,3},{3,0},{4,5},{5,6},{6,7},{7,4},{8,9},{9,10},{10,1... | collective-permute-start | bytes 638984 | tf_op jit(solution)/shard_map/ppermute | solution.py:18
  2.7 2.0 %collective-permute-start = (f32[6,16,256]{2,1,0:T(8,128)S(1)}, f32[6,16,256]{2,1,0:T(8,128)S(1)}, u32[]{:S(2)}, u32[]{:S(2)}) collective-permute-start(f32[6,16,256]{2,1,0:T(8,128)S(1)} %get-tuple-element.27.ydn), channel_id=1, source_target_pairs={{0,3},{1,0},{2,1},{3,2},{4,7},{5,4},{6,5},{7,6},{8,11},{9,8},{10,9... | collective-permute-start | bytes 294920 | tf_op jit(solution)/shard_map/ppermute | solution.py:18
  4.7 3.2 %collective-permute-done.yu = f32[6,16,256]{2,1,0:T(8,128)S(1)} collective-permute-done((f32[6,16,256]{2,1,0:T(8,128)S(1)}, f32[6,16,256]{2,1,0:T(8,128)S(1)}, u32[]{:S(2)}, u32[]{:S(2)}) %collective-permute-start) | collective-permute-done | bytes 98336 | tf_op jit(solution)/shard_map/ppermute | solution.py:18
  7.9 0.3 collective-permute-done.1.yd
  8.2 2.9 %collective-permute-start.3 = (f32[128,256]{1,0:T(8,128)S(1)}, f32[128,256]{1,0:T(8,128)S(1)}, u32[]{:S(2)}, u32[]{:S(2)}) collective-permute-start(f32[128,256]{1,0:T(8,128)S(1)} %get-tuple-element.30), channel_id=1, source_target_pairs={{0,4},{4,8},{8,12},{12,16},{16,20},{20,24},{24,28},{28,0},{1,5},{5... | collective-permute-start | bytes 393224 | tf_op jit(solution)/shard_map/ppermute | solution.py:18
  11.1 4.9 %all-to-all-start = ((f32[8,8,128]{2,1,0:T(8,128)}), f32[8,8,128]{2,1,0:T(8,128)S(1)}, u32[]{:S(2)}, u32[]{:S(2)}) async-start(f32[8,8,128]{2,1,0:T(8,128)} %get-tuple-element.31), calls=%async_computation | async-start | bytes 65536 | tf_op jit(solution)/shard_map/all_to_all | solution.py:22
  16.0 4.7 %collective-permute-start.2 = (f32[64,256]{1,0:T(8,128)S(1)}, f32[64,256]{1,0:T(8,128)S(1)}, u32[]{:S(2)}, u32[]{:S(2)}) collective-permute-start(f32[64,256]{1,0:T(8,128)S(1)} %get-tuple-element.29), channel_id=1, source_target_pairs={{0,28},{4,0},{8,4},{12,8},{16,12},{20,16},{24,20},{28,24},{1,29},{... | collective-permute-start | bytes 196616 | tf_op jit(solution)/shard_map/ppermute | solution.py:18
  20.7 0.9 %shard_map.103 = (bf16[48,5120]{1,0:T(8,128)(2,1)S(1)}, s32[5,1024]{1,0:T(8,128)S(1)}, s32[5,8,128]{2,1,0:T(8,128)S(1)}, f32[6,8,128]{2,1,0:T(8,128)S(1)}, f32[8,128]{1,0:T(8,128)S(1)}, /*index=5*/f32[8,128]{1,0:T(8,128)S(1)}) custom-call(s32[5,1024]{1,0:T(8,128)} %nodes_hbm.1, f32[6,1024]{1,0:T(8,128)} %diag_hbm.1, f32[8,128]{1,0:T(8,128)} %bitcast.3, ...), custom_call_target="tpu_custom_call" | custom-call | tf_op jit(solution)/shard_map/pallas_call | solution.py:31
  21.6 1.0 %all-to-all-done.table_ref = f32[8,8,128]{2,1,0:T(8,128)S(1)} async-done(((f32[8,8,128]{2,1,0:T(8,128)}), f32[8,8,128]{2,1,0:T(8,128)S(1)}, u32[]{:S(2)}, u32[]{:S(2)}) %all-to-all-start) | async-done | bytes 32800 | tf_op jit(solution)/shard_map/all_to_all | solution.py:22
  22.6 2.0 %shard_map.104 = f32[8,8,128]{2,1,0:T(8,128)} custom-call(f32[8,8,128]{2,1,0:T(8,128)S(1)} %all-to-all-done.table_ref, s32[5,8,128]{2,1,0:T(8,128)S(1)} %get-tuple-element.32.nodes_ref, f32[6,8,128]{2,1,0:T(8,128)S(1)} %get-tuple-element.33.diag_ref, f32[8,128]{1,0:T(8,128)S(1)} %get-tuple-element.34.gap_ref, f32[8,128]{1,0:T(8,128)S(1)} %get-tuple-element.35.stiff_ref, ...), custom_call_target="tpu_custom_call" | custom-call | tf_op jit(solution)/shard_map/pallas_call | solution.py:31
  24.7 3.3 %all-to-all-start.1 = ((f32[8,8,128]{2,1,0:T(8,128)}), f32[8,8,128]{2,1,0:T(8,128)S(1)}, u32[]{:S(2)}, u32[]{:S(2)}) async-start(f32[8,8,128]{2,1,0:T(8,128)} %shard_map.104), calls=%async_computation.1 | async-start | bytes 65536 | tf_op jit(solution)/shard_map/all_to_all | solution.py:22
  28.0 0.0 collective-permute-done.2.xu
  28.0 0.0 collective-permute-done.3.xd
  28.0 3.9 %shard_map.102.base_ref = f32[3,16,8,256]{3,2,1,0:T(8,128)S(1)} custom-call(f32[3,16,8,256]{3,2,1,0:T(8,128)S(1)} %get-tuple-element.22.u_ref, f32[3,16,8,256]{3,2,1,0:T(8,128)S(1)} %get-tuple-element.23.v_ref, f32[6,16,8,256]{3,2,1,0:T(8,128)S(1)} %get-tuple-element.24.stress_ref, f32[16,8,256]{2,1,0:T(8,128)S(1)} %get-tuple-element.25.hour_ref, ...), custom_call_target="tpu_custom_call" | custom-call | tf_op jit(solution)/shard_map/pallas_call | solution.py:31
  31.9 2.7 %all-to-all-done.1.table_ref = f32[8,8,128]{2,1,0:T(8,128)S(1)} async-done(((f32[8,8,128]{2,1,0:T(8,128)}), f32[8,8,128]{2,1,0:T(8,128)S(1)}, u32[]{:S(2)}, u32[]{:S(2)}) %all-to-all-start.1) | async-done | bytes 32800 | tf_op jit(solution)/shard_map/all_to_all | solution.py:22
  34.6 1.0 %shard_map.105 = f32[3,16,8,256]{3,2,1,0:T(8,128)} custom-call(f32[3,16,8,256]{3,2,1,0:T(8,128)S(1)} %shard_map.102.base_ref, f32[16,8,256]{2,1,0:T(8,128)S(1)} %get-tuple-element.26.mass_ref, f32[8,8,128]{2,1,0:T(8,128)S(1)} %all-to-all-done.1.table_ref, s32[2,128]{1,0:T(2,128)S(1)} %get-tuple-element.38.route_ref), custom_call_target="tpu_custom_call" | custom-call | tf_op jit(solution)/shard_map/pallas_call | solution.py:31
  (1 shorter events, 0.0 us)
Async XLA Ops:
  2.2 6.0 %collective-permute-start.1 = (f32[13,16,256]{2,1,0:T(8,128)S(1)}, f32[13,16,256]{2,1,0:T(8,128)S(1)}, u32[]{:S(2)}, u32[]{:S(2)}) collective-permute-start(f32[13,16,256]{2,1,0:T(8,128)S(1)} %get-tuple-element.28), channel_id=1, source_target_pairs={{0,1},{1,2},{2,3},{3,0},{4,5},{5,6},{6,7},{7,4},{8,9},{9,10},{10,1... | collective-permute-start | bytes 638984 | tf_op jit(solution)/shard_map/ppermute | solution.py:18
  2.7 5.2 %collective-permute-start = (f32[6,16,256]{2,1,0:T(8,128)S(1)}, f32[6,16,256]{2,1,0:T(8,128)S(1)}, u32[]{:S(2)}, u32[]{:S(2)}) collective-permute-start(f32[6,16,256]{2,1,0:T(8,128)S(1)} %get-tuple-element.27.ydn), channel_id=1, source_target_pairs={{0,3},{1,0},{2,1},{3,2},{4,7},{5,4},{6,5},{7,6},{8,11},{9,8},{10,9... | collective-permute-start | bytes 294920 | tf_op jit(solution)/shard_map/ppermute | solution.py:18
  8.2 19.8 %collective-permute-start.3 = (f32[128,256]{1,0:T(8,128)S(1)}, f32[128,256]{1,0:T(8,128)S(1)}, u32[]{:S(2)}, u32[]{:S(2)}) collective-permute-start(f32[128,256]{1,0:T(8,128)S(1)} %get-tuple-element.30), channel_id=1, source_target_pairs={{0,4},{4,8},{8,12},{12,16},{16,20},{20,24},{24,28},{28,0},{1,5},{5... | collective-permute-start | bytes 393224 | tf_op jit(solution)/shard_map/ppermute | solution.py:18
  11.1 11.6 %all-to-all-start = ((f32[8,8,128]{2,1,0:T(8,128)}), f32[8,8,128]{2,1,0:T(8,128)S(1)}, u32[]{:S(2)}, u32[]{:S(2)}) async-start(f32[8,8,128]{2,1,0:T(8,128)} %get-tuple-element.31), calls=%async_computation | async-start | bytes 65536 | tf_op jit(solution)/shard_map/all_to_all | solution.py:22
  16.0 12.0 %collective-permute-start.2 = (f32[64,256]{1,0:T(8,128)S(1)}, f32[64,256]{1,0:T(8,128)S(1)}, u32[]{:S(2)}, u32[]{:S(2)}) collective-permute-start(f32[64,256]{1,0:T(8,128)S(1)} %get-tuple-element.29), channel_id=1, source_target_pairs={{0,28},{4,0},{8,4},{12,8},{16,12},{20,16},{24,20},{28,24},{1,29},{... | collective-permute-start | bytes 196616 | tf_op jit(solution)/shard_map/ppermute | solution.py:18
  24.7 10.0 %all-to-all-start.1 = ((f32[8,8,128]{2,1,0:T(8,128)}), f32[8,8,128]{2,1,0:T(8,128)S(1)}, u32[]{:S(2)}, u32[]{:S(2)}) async-start(f32[8,8,128]{2,1,0:T(8,128)} %shard_map.104), calls=%async_computation.1 | async-start | bytes 65536 | tf_op jit(solution)/shard_map/all_to_all | solution.py:22
where the time goes:
time: 36 us; the launch traced here: 35.6 us
  starting transfers between devices  18.3 us (51%)
  Pallas kernels  10 us (28%)
  waiting for transfers between devices  7.21 us (20%)
    ppermute x4, starting transfers between devices, shifted(): lax.ppermute(value, axis, [(at, (at + steps) % count) for at in range(cou...  10.1 us
    pallas_call x6, Pallas kernels, kernel_call(): pl.pallas_call(body, out_shape=jax.tree.map(lambda out: space(out.shape,...  10 us
    all_to_all x2, starting transfers between devices, exchanged(): lax.all_to_all(value, 'space', split_axis=0, concat_axis=0, tiled=True)  8.22 us
    all_to_all x2, waiting for transfers between devices, exchanged(): lax.all_to_all(value, 'space', split_axis=0, concat_axis=0, tiled=True)  3.74 us
    ppermute x4, waiting for transfers between devices, shifted(): lax.ppermute(value, axis, [(at, (at + steps) % count) for at in range(cou...  3.47 us
  transfers between devices with their start and end apart: 6, of which 4 were waited for; matrix products, arithmetic and copies ran while one was open for 0% of the time, Pallas kernels for 19%

commit v1 on v0

--- a/solution.py
+++ b/solution.py
@@ -22,17 +22,21 @@
     return lax.all_to_all(value, "space", split_axis=0, concat_axis=0, tiled=True)
 
 
-def kernel_call(body, inputs, outs, scratch=(), hbm_inputs=0, final=False):
-    vmem = pl.BlockSpec(memory_space=pltpu.VMEM)
-    hbm = pl.BlockSpec(memory_space=pltpu.HBM)
+def kernel_call(body, inputs, outs, scratch=(), hbm_inputs=0):
     spaces = [pltpu.HBM if at < hbm_inputs else pltpu.VMEM for at in range(len(inputs))]
     inputs = [pltpu.with_memory_space_constraint(*pair) for pair in zip(inputs, spaces)]
-    space = pltpu.HBM if final else pltpu.VMEM
+
+    def placed(out):
+        if isinstance(out, jax.ShapeDtypeStruct):
+            return pltpu.VMEM(out.shape, out.dtype)
+        return out
+
+    outs = tuple(placed(out) for out in outs) if isinstance(outs, tuple) else placed(outs)
     return pl.pallas_call(
         body,
-        out_shape=jax.tree.map(lambda out: space(out.shape, out.dtype), outs),
+        out_shape=outs,
         in_specs=[pl.BlockSpec(memory_space=one) for one in spaces],
-        out_specs=jax.tree.map(lambda _: hbm if final else vmem, outs),
+        out_specs=jax.tree.map(lambda out: pl.BlockSpec(memory_space=out.memory_space), outs),
         scratch_shapes=list(scratch),
         compiler_params=pltpu.CompilerParams(vmem_limit_bytes=16 << 20),
     )(*inputs)
@@ -88,21 +92,15 @@
 
 
 def first_body(
-    capacity, pack, blocks, u_hbm, v_hbm, stress_hbm, hour_hbm, mass_hbm, route_hbm,
-    out_ref, ydn, yup, sides_ref, u_ref, v_ref, stress_ref, hour_ref, mass_ref, rows_ref, route_ref, sems,
+    capacity, pack, blocks, u_hbm, route_hbm, v_hbm, *rest,
 ):
+    hbm, rest = (u_hbm, route_hbm, v_hbm) + rest[:7], rest[7:]
+    message_hbm, ydn, sides_ref, u_ref, v_ref = rest[:5]
+    out_ref, rows_ref, route_ref, sems, message_sem = rest[-5:]
+    targets = (u_ref, route_ref, v_ref) + rest[5:-5]
     copies = [
         pltpu.make_async_copy(source, target, sems.at[at])
-        for at, (source, target) in enumerate(
-            (
-                (u_hbm, u_ref),
-                (route_hbm, route_ref),
-                (v_hbm, v_ref),
-                (stress_hbm, stress_ref),
-                (hour_hbm, hour_ref),
-                (mass_hbm, mass_ref),
-            )
-        )
+        for at, (source, target) in enumerate(zip(hbm, targets))
     ]
     for copy in copies:
         copy.start()
@@ -121,19 +119,22 @@
         rows_ref[c : c + 1, side : 2 * side] = both[LANES - 1 : LANES]
     width = pack * capacity
     route = route_ref[...]
-    sides_ref[0:1, :] = route[:, 0:side]
-    sides_ref[1:2, :] = route[:, side : 2 * side]
     block, place = block_of(route, width, blocks)
     entries = spread(parts_of(rows_ref[...]), block, blocks)
     got = contract_lanes(jnp.concatenate(entries, 0), places(place, width))
     write_messages(out_ref, got, pack, blocks)
-    for copy in copies[2:]:
+    message = pltpu.make_async_copy(out_ref, message_hbm, message_sem)
+    message.start()
+    sides_ref[0:1, :] = route[:, 0:side]
+    sides_ref[1:2, :] = route[:, side : 2 * side]
+    for c in range(3):
+        ydn[c] = u_ref[c, :, 0, :]
+    copies[2].wait()
+    for c in range(3):
+        ydn[3 + c] = v_ref[c, :, 0, :]
+    for copy in copies[3:]:
         copy.wait()
-    for c in range(13):
-        ref = component(u_ref, v_ref, stress_ref, hour_ref, c)
-        yup[c] = ref[:, columns - 1, :]
-        if c < 6:
-            ydn[c] = ref[:, 0, :]
+    message.wait()
 
 
 def component(u_ref, v_ref, stress_ref, hour_ref, c):
@@ -146,41 +147,20 @@
     return hour_ref
 
 
-def second_body(u_ref, v_ref, stress_ref, hour_ref, yu, yd, xdn, xup):
+def second_body(u_ref, v_ref, stress_ref, hour_ref, yu, xdn, xup):
     planes, columns = u_ref.shape[1:3]
-    base = 13 * columns
     for c in range(13):
         ref = component(u_ref, v_ref, stress_ref, hour_ref, c)
         xup[c * columns : (c + 1) * columns, :] = ref[planes - 1]
-        xup[base + c : base + c + 1, :] = yd[c, planes - 1 : planes, :]
-    for c in range(6):
-        ref = component(u_ref, v_ref, stress_ref, hour_ref, c)
-        xup[base + 13 + c : base + 14 + c, :] = yu[c, planes - 1 : planes, :]
-        xdn[c * columns : (c + 1) * columns, :] = ref[0]
-        at = 6 * columns + c
-        xdn[at : at + 1, :] = yd[c, 0:1, :]
-        xdn[at + 6 : at + 7, :] = yu[c, 0:1, :]
-
-
-def places_body(
-    width, blocks, nodes_hbm, diag_hbm, gap_hbm, stiff_hbm,
-    place_ref, block_ref, lines_ref, diag_lines_ref, gap_ref, stiff_ref, nodes_ref, diag_ref, sems,
-):
-    copies = [
-        pltpu.make_async_copy(source, target, sems.at[at])
-        for at, (source, target) in enumerate(
-            (
-                (nodes_hbm, nodes_ref),
-                (diag_hbm, diag_ref),
-                (gap_hbm, gap_ref),
-                (stiff_hbm, stiff_ref),
-            )
-        )
-    ]
-    for copy in copies:
-        copy.start()
-    for copy in copies:
-        copy.wait()
+        if c < 6:
+            at = 13 * columns + c
+            xup[at : at + 1, :] = yu[c, planes - 1 : planes, :]
+            xdn[c * columns : (c + 1) * columns, :] = ref[0]
+            at = 6 * columns + c
+            xdn[at : at + 1, :] = yu[c, 0:1, :]
+
+
+def places_body(width, blocks, nodes_ref, diag_ref, place_ref, block_ref, lines_ref, diag_lines_ref):
     pairs = nodes_ref.shape[1]
     for j in range(5):
         nodes = nodes_ref[j : j + 1, :]
@@ -328,12 +308,11 @@
 
 
 def element_body(
-    u_ref, v_ref, stress_ref, hour_ref, mass_ref, ydn, yu, yd, xu, xd,
-    out_ref, row_ref, halo_s, halo_d, edge_ref, node_ref, elem_ref,
+    u_ref, v_ref, stress_ref, hour_ref, mass_ref, yu, xu, xd,
+    out_ref, beyond_ref, row_ref, halo_s, halo_d, last_ref, node_ref, elem_ref,
 ):
     planes, columns, depth = u_ref.shape[1:]
     nb = depth // LANES
-    rows = row_ref.shape[0]
 
     def below(c):
         return xd[c * columns : (c + 1) * columns, :]
@@ -341,43 +320,14 @@
     def above(c):
         return xu[c * columns : (c + 1) * columns, :]
 
-    def assembled(first, middle, last):
-        row_ref[0:1, :] = first
-        row_ref[1 : planes + 1, :] = middle
-        if last is not None:
-            row_ref[planes + 1 : planes + 2, :] = last
-        return split(row_ref[...])
-
-    def line(ref, at):
-        return ref[at : at + 1, :]
-
     row_ref[...] = jnp.zeros(row_ref.shape, jnp.float32)
-    base = 13 * columns
-    left_s, left_d, mid_s, mid_d = [], [], [], []
     for c in range(6):
-        right = assembled(line(xd, base + 13 + c), yu[c], line(xu, 6 * columns + 6 + c))
-        s, d = z_pair(right)
-        halo_s[c] = s
-        halo_d[c] = d
-        s, d = z_pair(assembled(line(xd, base + c), yd[c], line(xu, 6 * columns + c)))
-        left_s.append(s)
-        left_d.append(d)
-        s, d = z_pair(assembled(line(xd, c * columns), ydn[c], line(xu, c * columns)))
-        mid_s.append(s)
-        mid_d.append(d)
-    side = node_terms(left_s, left_d, mid_s, mid_d)
-    stress = [assembled(line(xd, base + 6 + c), yd[6 + c], None) for c in range(6)]
-    hour = assembled(line(xd, base + 12), yd[12], None)
-    next_side = [tuple(pltpu.roll(q, rows - 1, 1) for q in terms) for terms in side]
-    factors = element_terms(side, next_side, stress, hour)
-    upper = [[pltpu.roll(q, rows - 1, 1) for q in terms] for terms in factors]
-    for m, (a, b, c, e) in enumerate(gathered_x(factors, upper)):
-        edge_ref[m, 0] = a + b
-        edge_ref[m, 1] = c + e
+        row_ref[0:1, :] = xd[13 * columns + c : 13 * columns + c + 1, :]
+        row_ref[1 : planes + 1, :] = yu[c]
+        row_ref[planes + 1 : planes + 2, :] = xu[6 * columns + c : 6 * columns + c + 1, :]
+        halo_s[c], halo_d[c] = z_pair(split(row_ref[...]))
 
     row = lax.broadcasted_iota(jnp.int32, (nb, columns, LANES), 1)
-    lane = lax.broadcasted_iota(jnp.int32, (nb, columns, LANES), 2)
-    block = lax.broadcasted_iota(jnp.int32, (nb, columns, LANES), 0)
 
     def node_plane(values, at):
         sums, diffs, sums_next, diffs_next = [], [], [], []
@@ -407,19 +357,23 @@
     def kept_elements():
         return [[elem_ref[m, t] for t in range(7)] for m in range(3)]
 
+    def along_z(p, r):
+        lane = lax.broadcasted_iota(jnp.int32, p.shape, 2)
+        block = lax.broadcasted_iota(jnp.int32, p.shape, 0)
+        up = pltpu.roll(p + r, 1, 2)
+        before_up = jnp.concatenate([jnp.zeros_like(up[:1]), up[:-1]], 0)
+        last = (lane == LANES - 1) & (block == nb - 1)
+        return jnp.where(lane == 0, before_up, up) + jnp.where(last, 0.0, p - r)
+
     def write_plane(before, after, i):
         weight = (time_step / 64.0) / split(mass_ref[i])
         for m, (a, b, c, e) in enumerate(gathered_x(before, after)):
-            ab = edge_ref[m, 0, :, pl.ds(i, 1), :]
-            ce = edge_ref[m, 1, :, pl.ds(i, 1), :]
-            p = (a - b) + jnp.where(row == 0, ab, pltpu.roll(a + b, 1, 1))
-            r = (c - e) + jnp.where(row == 0, ce, pltpu.roll(c + e, 1, 1))
-            up = pltpu.roll(p + r, 1, 2)
-            before_up = jnp.concatenate([jnp.zeros_like(up[:1]), up[:-1]], 0)
-            force = jnp.where(lane == 0, before_up, up)
-            last = (lane == LANES - 1) & (block == nb - 1)
-            force = force + jnp.where(last, 0.0, p - r)
-            result = split(v_ref[m, i]) - force * weight
+            ab, ce = a + b, c + e
+            last_ref[m, 0, :, pl.ds(i, 1), :] = ab[:, columns - 1 : columns]
+            last_ref[m, 1, :, pl.ds(i, 1), :] = ce[:, columns - 1 : columns]
+            p = (a - b) + jnp.where(row == 0, 0.0, pltpu.roll(ab, 1, 1))
+            r = (c - e) + jnp.where(row == 0, 0.0, pltpu.roll(ce, 1, 1))
+            result = split(v_ref[m, i]) - along_z(p, r) * weight
             for k in range(nb):
                 out_ref[m, i, :, k * LANES : (k + 1) * LANES] = result[k]
 
@@ -449,27 +403,38 @@
 
     lax.fori_loop(1, planes, loop, 0)
     step(planes, node_plane([split(above(c)) for c in range(6)], planes + 1))
+    for m in range(3):
+        force = along_z(last_ref[m, 0], last_ref[m, 1])
+        for k in range(nb):
+            beyond_ref[m, :, k * LANES : (k + 1) * LANES] = force[k]
 
 
 def final_body(
-    nspace, capacity, pack, base_ref, mass_ref, table_ref, route_ref, out_hbm, rows_ref, out_ref, sems
+    nspace, capacity, pack,
+    base_ref, mass_ref, table_ref, route_ref, left_ref, out_hbm, rows_ref, out_ref, sems,
 ):
     planes, columns, depth = base_ref.shape[1:]
     offset = (lax.axis_index("space") % pack) * capacity
     (contact,) = looked_up(table_ref, [route_ref[...]], capacity, offset, nspace)
     rows_ref[...] = jnp.zeros(rows_ref.shape, jnp.float32)
     lane = lax.broadcasted_iota(jnp.int32, (planes, columns, LANES), 2)
-    low_weight = jnp.where(lane == 0, time_step / mass_ref[:, :, 0:LANES], 0.0)
-    high_weight = jnp.where(
-        lane == LANES - 1, time_step / mass_ref[:, :, depth - LANES : depth], 0.0
-    )
+    row = lax.broadcasted_iota(jnp.int32, (columns, LANES), 0)
+    weights = [time_step / mass_ref[:, :, k : k + LANES] for k in range(0, depth, LANES)]
+    low_weight = jnp.where(lane == 0, weights[0], 0.0)
+    high_weight = jnp.where(lane == LANES - 1, weights[-1], 0.0)
     copies = []
     for m in range(3):
         rows_ref[m, 0:1, :] = contact[m][0:1]
         rows_ref[m, LANES - 1 : LANES, :] = contact[m][1:2]
         turned = rows_ref[m].T.reshape(planes, columns, LANES)
         for k in range(0, depth, LANES):
-            value = base_ref[m, :, :, k : k + LANES]
+            left = jnp.stack(
+                [
+                    jnp.where(row == 0, left_ref[m, i : i + 1, k : k + LANES] * (1.0 / 64.0), 0.0)
+                    for i in range(planes)
+                ]
+            )
+            value = base_ref[m, :, :, k : k + LANES] - left * weights[k // LANES]
             if k == 0:
                 value = value + low_weight * turned
             if k == depth - LANES:
@@ -506,72 +471,53 @@
 
     message = sized(nspace, 8, LANES)
     width = pack * capacity
-    whole = jax.ShapeDtypeStruct((5, pairs), jnp.int32)
-    place, block, nodes, diagonals, gap, stiffness = kernel_call(
-        functools.partial(places_body, width, blocks),
+    small = (pair_nodes, pair_diagonals, pair_gap.reshape(lines, LANES))
+    small += (pair_stiffness.reshape(lines, LANES),)
+    kept = (displacement, velocity, stress, hourglass, mass) + small
+    outgoing, ydn, sides, *kept = kernel_call(
+        functools.partial(first_body, capacity, pack, blocks),
+        (displacement, contact_route.reshape(1, surf_count)) + kept[1:],
         (
-            pair_nodes,
-            pair_diagonals,
-            pair_gap.reshape(lines, LANES),
-            pair_stiffness.reshape(lines, LANES),
-        ),
-        (
-            jax.ShapeDtypeStruct(((width + 15) // 16 * 16, 5 * pairs), jnp.bfloat16),
-            whole,
-            jax.ShapeDtypeStruct((5, lines, LANES), jnp.int32),
-            sized(6, lines, LANES),
-            sized(lines, LANES),
-            sized(lines, LANES),
+            pltpu.HBM(message.shape, f32),
+            sized(6, planes, depth),
+            jax.ShapeDtypeStruct((2, surf_count // 2), jnp.int32),
+            *(jax.ShapeDtypeStruct(one.shape, one.dtype) for one in kept),
         ),
         [
-            pltpu.VMEM(whole.shape, jnp.int32),
-            pltpu.VMEM((6, pairs), f32),
-            pltpu.SemaphoreType.DMA((4,)),
-        ],
-        hbm_inputs=4,
-    )
-    fields = (displacement, velocity, stress, hourglass, mass)
-    outgoing, ydn, yup, sides, *fields = kernel_call(
-        functools.partial(first_body, capacity, pack, blocks),
-        (*fields, contact_route.reshape(1, surf_count)),
-        (
-            message,
-            sized(6, planes, depth),
-            sized(13, planes, depth),
-            jax.ShapeDtypeStruct((2, surf_count // 2), jnp.int32),
-            *(sized(*field.shape) for field in fields),
-        ),
-        [
+            pltpu.VMEM(message.shape, f32),
             pltpu.VMEM((8, surf_count), f32),
             pltpu.VMEM((1, surf_count), jnp.int32),
-            pltpu.SemaphoreType.DMA((6,)),
+            pltpu.SemaphoreType.DMA((len(kept) + 1,)),
+            pltpu.SemaphoreType.DMA,
         ],
-        hbm_inputs=6,
-    )
+        hbm_inputs=len(kept) + 1,
+    )
+    fields, (pair_nodes, pair_diagonals, gap, stiffness) = kept[:5], kept[5:]
     yu = shifted(ydn, "slab", -1)
-    yd = shifted(yup, "slab", 1)
     received = exchanged(outgoing)
     xdn, xup = kernel_call(
         second_body,
-        (*fields[:4], yu, yd),
+        (*fields[:4], yu),
         (
-            sized((6 * columns + 12 + 7) // 8 * 8, depth),
-            sized((13 * columns + 19 + 7) // 8 * 8, depth),
+            sized((6 * columns + 6 + 7) // 8 * 8, depth),
+            sized((13 * columns + 6 + 7) // 8 * 8, depth),
         ),
     )
     xu = shifted(xdn, "space", -1)
     xd = shifted(xup, "space", 1)
+    place, block, nodes, diagonals = kernel_call(
+        functools.partial(places_body, width, blocks),
+        (pair_nodes, pair_diagonals),
+        (
+            jax.ShapeDtypeStruct(((width + 15) // 16 * 16, 5 * pairs), jnp.bfloat16),
+            jax.ShapeDtypeStruct((5, pairs), jnp.int32),
+            jax.ShapeDtypeStruct((5, lines, LANES), jnp.int32),
+            sized(6, lines, LANES),
+        ),
+    )
     slot_force = kernel_call(
         functools.partial(pair_body, nspace, capacity, pack, blocks),
-        (
-            received,
-            nodes,
-            diagonals,
-            gap,
-            stiffness,
-            place,
-            block,
-        ),
+        (received, nodes, diagonals, gap, stiffness, place, block),
         message,
         [pltpu.VMEM((8, pairs), f32), pltpu.VMEM((24 * blocks, 5 * pairs), jnp.bfloat16)],
     )
@@ -579,30 +525,30 @@
 
     nb = depth // LANES
     rows = (planes + 2 + 7) // 8 * 8
-    base = kernel_call(
+    base, beyond = kernel_call(
         element_body,
-        (*fields, ydn, yu, yd, xu, xd),
-        sized(*displacement.shape),
+        (*fields, yu, xu, xd),
+        (sized(*displacement.shape), sized(3, planes, depth)),
         [
             pltpu.VMEM((rows, depth), f32),
             pltpu.VMEM((6, nb, rows, LANES), f32),
             pltpu.VMEM((6, nb, rows, LANES), f32),
-            pltpu.VMEM((3, 2, nb, rows, LANES), f32),
+            pltpu.VMEM((3, 2, nb, planes, LANES), f32),
             pltpu.VMEM((6, 3, nb, columns, LANES), f32),
             pltpu.VMEM((3, 7, nb, columns, LANES), f32),
         ],
     )
+    left = shifted(beyond, "slab", 1)
 
     return kernel_call(
         functools.partial(final_body, nspace, capacity, pack),
-        (base, fields[4], returned, sides),
-        sized(*displacement.shape),
+        (base, fields[4], returned, sides, left),
+        pltpu.HBM(displacement.shape, f32),
         [
             pltpu.VMEM((3, LANES, LANES), f32),
             pltpu.VMEM(displacement.shape, f32),
             pltpu.SemaphoreType.DMA((3,)),
         ],
-        final=True,
     )
 
 

time: 36 us -> 33.7 us (0.936)
  starting transfers between devices: 18.3 us -> 17 us
  Pallas kernels: 10 us -> 8.8 us
    ppermute x4, starting transfers between devices: 10.1 us -> 8.81 us  [shifted(): lax.ppermute(value, axis, [(at, (at + steps) % count) for at in range(cou...]
    pallas_call x6, Pallas kernels: 10 us -> 8.8 us  [kernel_call(): pl.pallas_call(body, out_shape=outs, in_specs=[pl.BlockSpec(memory_space=...]
    all_to_all x2, waiting for transfers between devices: 3.74 us -> 4.72 us  [exchanged(): lax.all_to_all(value, 'space', split_axis=0, concat_axis=0, tiled=True)]
    ppermute x4, waiting for transfers between devices: 3.47 us -> 2.84 us  [shifted(): lax.ppermute(value, axis, [(at, (at + steps) % count) for at in range(cou...]
  transfers between devices with their start and end apart: 6 -> 6, of which waited for: 4 -> 4; matrix products, arithmetic and copies ran while one was open for 0% -> 0% of each run, Pallas kernels for 19% -> 17%
where the time goes in v1:
time: 33.7 us; the launch traced here: 33.5 us
  starting transfers between devices  17 us (50%)
  Pallas kernels  8.8 us (26%)
  waiting for transfers between devices  7.56 us (22%)
    ppermute x4, starting transfers between devices, shifted(): lax.ppermute(value, axis, [(at, (at + steps) % count) for at in range(cou...  8.81 us
    pallas_call x6, Pallas kernels, kernel_call(): pl.pallas_call(body, out_shape=outs, in_specs=[pl.BlockSpec(memory_space=...  8.8 us
    all_to_all x2, starting transfers between devices, exchanged(): lax.all_to_all(value, 'space', split_axis=0, concat_axis=0, tiled=True)  8.22 us
    all_to_all x2, waiting for transfers between devices, exchanged(): lax.all_to_all(value, 'space', split_axis=0, concat_axis=0, tiled=True)  4.72 us
    ppermute x4, waiting for transfers between devices, shifted(): lax.ppermute(value, axis, [(at, (at + steps) % count) for at in range(cou...  2.84 us
  transfers between devices with their start and end apart: 6, of which 4 were waited for; matrix products, arithmetic and copies ran while one was open for 0% of the time, Pallas kernels for 17%

profile of v1, /device:TPU:0, one launch (start us, length us, event | category | flops | bytes accessed | tf_op | source)
XLA Modules:
  0.0 33.5 jit_solution(15457191303597850054)
XLA Ops:
  0.0 2.0 %shard_map.100 = (f32[8,8,128]{2,1,0:T(8,128)}, f32[6,16,256]{2,1,0:T(8,128)S(1)}, s32[2,128]{1,0:T(2,128)S(1)}, f32[3,16,8,256]{3,2,1,0:T(8,128)S(1)}, f32[3,16...) custom-call(f32[3,16,8,256]{3,2,1,0:T(8,128)} %u_hbm.1, ...), custom_call_target="tpu_custom_call" | custom-call | tf_op jit(solution)/shard_map/pallas_call | solution.py:35
  2.0 2.5 %collective-permute-start = (f32[6,16,256]{2,1,0:T(8,128)S(1)}, f32[6,16,256]{2,1,0:T(8,128)S(1)}, u32[]{:S(2)}, u32[]{:S(2)}) collective-permute-start(f32[6,16,256]{2,1,0:T(8,128)S(1)} %get-tuple-element.30), channel_id=1, source_target_pairs={{0,3},{1,0},{2,1},{3,2},{4,7},{5,4},{6,5},{7,6},{8,11},{9,8},{10,9... | collective-permute-start | bytes 294920 | tf_op jit(solution)/shard_map/ppermute | solution.py:18
  4.5 2.2 %collective-permute-done.yu = f32[6,16,256]{2,1,0:T(8,128)S(1)} collective-permute-done((f32[6,16,256]{2,1,0:T(8,128)S(1)}, f32[6,16,256]{2,1,0:T(8,128)S(1)}, u32[]{:S(2)}, u32[]{:S(2)}) %collective-permute-start) | collective-permute-done | bytes 98336 | tf_op jit(solution)/shard_map/ppermute | solution.py:18
  6.7 1.6 %collective-permute-start.2 = (f32[112,256]{1,0:T(8,128)S(1)}, f32[112,256]{1,0:T(8,128)S(1)}, u32[]{:S(2)}, u32[]{:S(2)}) collective-permute-start(f32[112,256]{1,0:T(8,128)S(1)} %get-tuple-element.32), channel_id=1, source_target_pairs={{0,4},{4,8},{8,12},{12,16},{16,20},{20,24},{24,28},{28,0},{1,5},{5... | collective-permute-start | bytes 344072 | tf_op jit(solution)/shard_map/ppermute | solution.py:18
  8.3 4.9 %all-to-all-start = ((f32[8,8,128]{2,1,0:T(8,128)}), f32[8,8,128]{2,1,0:T(8,128)S(1)}, u32[]{:S(2)}, u32[]{:S(2)}) async-start(f32[8,8,128]{2,1,0:T(8,128)} %get-tuple-element.34), calls=%async_computation | async-start | bytes 65536 | tf_op jit(solution)/shard_map/all_to_all | solution.py:22
  13.2 4.7 %collective-permute-start.1 = (f32[56,256]{1,0:T(8,128)S(1)}, f32[56,256]{1,0:T(8,128)S(1)}, u32[]{:S(2)}, u32[]{:S(2)}) collective-permute-start(f32[56,256]{1,0:T(8,128)S(1)} %get-tuple-element.31), channel_id=1, source_target_pairs={{0,28},{4,0},{8,4},{12,8},{16,12},{20,16},{24,20},{28,24},{1,29},{... | collective-permute-start | bytes 172040 | tf_op jit(solution)/shard_map/ppermute | solution.py:18
  17.9 0.1 shard_map.103
  18.0 1.8 %all-to-all-done.table_ref = f32[8,8,128]{2,1,0:T(8,128)S(1)} async-done(((f32[8,8,128]{2,1,0:T(8,128)}), f32[8,8,128]{2,1,0:T(8,128)S(1)}, u32[]{:S(2)}, u32[]{:S(2)}) %all-to-all-start) | async-done | bytes 32800 | tf_op jit(solution)/shard_map/all_to_all | solution.py:22
  19.8 2.0 %shard_map.104 = f32[8,8,128]{2,1,0:T(8,128)} custom-call(f32[8,8,128]{2,1,0:T(8,128)S(1)} %all-to-all-done.table_ref, s32[5,8,128]{2,1,0:T(8,128)S(1)} %get-tuple-element.37.nodes_ref, f32[6,8,128]{2,1,0:T(8,128)S(1)} %get-tuple-element.38.diag_ref, f32[8,128]{1,0:T(8,128)S(1)} %get-tuple-element.39.gap_ref, f32[8,128]{1,0:T(8,128)S(1)} %get-tuple-element.40.stiff_ref, ...), custom_call_target="tpu_custom_call" | custom-call | tf_op jit(solution)/shard_map/pallas_call | solution.py:35
  21.9 3.3 %all-to-all-start.1 = ((f32[8,8,128]{2,1,0:T(8,128)}), f32[8,8,128]{2,1,0:T(8,128)S(1)}, u32[]{:S(2)}, u32[]{:S(2)}) async-start(f32[8,8,128]{2,1,0:T(8,128)} %shard_map.104), calls=%async_computation.1 | async-start | bytes 65536 | tf_op jit(solution)/shard_map/all_to_all | solution.py:22
  25.2 0.0 collective-permute-done.1.xu
  25.2 0.0 collective-permute-done.2.xd
  25.2 3.6 %shard_map.102 = (f32[3,16,8,256]{3,2,1,0:T(8,128)S(1)}, f32[3,16,256]{2,1,0:T(8,128)S(1)}) custom-call(f32[3,16,8,256]{3,2,1,0:T(8,128)S(1)} %get-tuple-element.25.u_ref, f32[3,16,8,256]{3,2,1,0:T(8,128)S(1)} %get-tuple-element.26.v_ref, f32[6,16,8,256]{3,2,1,0:T(8,128)S(1)} %get-tuple-element.27.stress_ref, f32[16,8,256]{2,1,0:T(8,128)S(1)} %get-tuple-element.28.hour_ref, ...), custom_call_target="tpu_custom_call" | custom-call | tf_op jit(solution)/shard_map/pallas_call | solution.py:35
  28.9 0.1 collective-permute-start.3
  28.9 2.9 %all-to-all-done.1.table_ref = f32[8,8,128]{2,1,0:T(8,128)S(1)} async-done(((f32[8,8,128]{2,1,0:T(8,128)}), f32[8,8,128]{2,1,0:T(8,128)S(1)}, u32[]{:S(2)}, u32[]{:S(2)}) %all-to-all-start.1) | async-done | bytes 32800 | tf_op jit(solution)/shard_map/all_to_all | solution.py:22
  31.8 0.6 %collective-permute-done.3.left_ref = f32[3,16,256]{2,1,0:T(8,128)S(1)} collective-permute-done((f32[3,16,256]{2,1,0:T(8,128)S(1)}, f32[3,16,256]{2,1,0:T(8,128)S(1)}, u32[]{:S(2)}, u32[]{:S(2)}) %collective-permute-start.3) | collective-permute-done | bytes 49184 | tf_op jit(solution)/shard_map/ppermute | solution.py:18
  32.4 1.0 %shard_map.105 = f32[3,16,8,256]{3,2,1,0:T(8,128)} custom-call(f32[3,16,8,256]{3,2,1,0:T(8,128)S(1)} %get-tuple-element.33.base_ref, f32[16,8,256]{2,1,0:T(8,128)S(1)} %get-tuple-element.29.mass_ref, f32[8,8,128]{2,1,0:T(8,128)S(1)} %all-to-all-done.1.table_ref, s32[2,128]{1,0:T(2,128)S(1)} %get-tuple-element.43.route_ref, ...), custom_call_target="tpu_custom_call" | custom-call | tf_op jit(solution)/shard_map/pallas_call | solution.py:35
  (1 shorter events, 0.0 us)
Async XLA Ops:
  2.0 4.7 %collective-permute-start = (f32[6,16,256]{2,1,0:T(8,128)S(1)}, f32[6,16,256]{2,1,0:T(8,128)S(1)}, u32[]{:S(2)}, u32[]{:S(2)}) collective-permute-start(f32[6,16,256]{2,1,0:T(8,128)S(1)} %get-tuple-element.30), channel_id=1, source_target_pairs={{0,3},{1,0},{2,1},{3,2},{4,7},{5,4},{6,5},{7,6},{8,11},{9,8},{10,9... | collective-permute-start | bytes 294920 | tf_op jit(solution)/shard_map/ppermute | solution.py:18
  6.7 18.5 %collective-permute-start.2 = (f32[112,256]{1,0:T(8,128)S(1)}, f32[112,256]{1,0:T(8,128)S(1)}, u32[]{:S(2)}, u32[]{:S(2)}) collective-permute-start(f32[112,256]{1,0:T(8,128)S(1)} %get-tuple-element.32), channel_id=1, source_target_pairs={{0,4},{4,8},{8,12},{12,16},{16,20},{20,24},{24,28},{28,0},{1,5},{5... | collective-permute-start | bytes 344072 | tf_op jit(solution)/shard_map/ppermute | solution.py:18
  8.3 11.6 %all-to-all-start = ((f32[8,8,128]{2,1,0:T(8,128)}), f32[8,8,128]{2,1,0:T(8,128)S(1)}, u32[]{:S(2)}, u32[]{:S(2)}) async-start(f32[8,8,128]{2,1,0:T(8,128)} %get-tuple-element.34), calls=%async_computation | async-start | bytes 65536 | tf_op jit(solution)/shard_map/all_to_all | solution.py:22
  13.2 12.0 %collective-permute-start.1 = (f32[56,256]{1,0:T(8,128)S(1)}, f32[56,256]{1,0:T(8,128)S(1)}, u32[]{:S(2)}, u32[]{:S(2)}) collective-permute-start(f32[56,256]{1,0:T(8,128)S(1)} %get-tuple-element.31), channel_id=1, source_target_pairs={{0,28},{4,0},{8,4},{12,8},{16,12},{20,16},{24,20},{28,24},{1,29},{... | collective-permute-start | bytes 172040 | tf_op jit(solution)/shard_map/ppermute | solution.py:18
  21.9 10.0 %all-to-all-start.1 = ((f32[8,8,128]{2,1,0:T(8,128)}), f32[8,8,128]{2,1,0:T(8,128)S(1)}, u32[]{:S(2)}, u32[]{:S(2)}) async-start(f32[8,8,128]{2,1,0:T(8,128)} %shard_map.104), calls=%async_computation.1 | async-start | bytes 65536 | tf_op jit(solution)/shard_map/all_to_all | solution.py:22
  28.9 3.6 %collective-permute-start.3 = (f32[3,16,256]{2,1,0:T(8,128)S(1)}, f32[3,16,256]{2,1,0:T(8,128)S(1)}, u32[]{:S(2)}, u32[]{:S(2)}) collective-permute-start(f32[3,16,256]{2,1,0:T(8,128)S(1)} %get-tuple-element.44), channel_id=1, source_target_pairs={{0,1},{1,2},{2,3},{3,0},{4,5},{5,6},{6,7},{7,4},{8,9},{9,10},{10,1... | collective-permute-start | bytes 147464 | tf_op jit(solution)/shard_map/ppermute | solution.py:18

commit v2 on v1

--- a/solution.py
+++ b/solution.py
@@ -160,17 +160,24 @@
             xdn[at : at + 1, :] = yu[c, 0:1, :]
 
 
-def places_body(width, blocks, nodes_ref, diag_ref, place_ref, block_ref, lines_ref, diag_lines_ref):
+def matrix_body(nodes_ref, diag_ref, matrix_ref, lines_ref, diag_lines_ref):
     pairs = nodes_ref.shape[1]
-    for j in range(5):
-        nodes = nodes_ref[j : j + 1, :]
-        block, place = block_of(nodes, width, blocks)
-        block_ref[j : j + 1, :] = block
-        place_ref[:, j * pairs : (j + 1) * pairs] = places(place, width)
-        for r in range(pairs // LANES):
-            lines_ref[j, r : r + 1, :] = nodes[:, r * LANES : (r + 1) * LANES]
-    for c in range(6):
-        for r in range(pairs // LANES):
+    group = 16
+
+    def rows(g, carry):
+        start = pl.multiple_of(g * group, group)
+        slot = lax.broadcasted_iota(jnp.int32, (group, pairs), 0) + start
+        total = jnp.where(nodes_ref[0:1, :] == slot, 1.0, 0.0)
+        for j in range(1, 5):
+            total = total - jnp.where(nodes_ref[j : j + 1, :] == slot, 0.25, 0.0)
+        matrix_ref[pl.ds(start, group), :] = total.astype(jnp.bfloat16)
+        return carry
+
+    lax.fori_loop(0, matrix_ref.shape[0] // group, rows, 0)
+    for r in range(pairs // LANES):
+        for j in range(5):
+            lines_ref[j, r : r + 1, :] = nodes_ref[j : j + 1, r * LANES : (r + 1) * LANES]
+        for c in range(6):
             diag_lines_ref[c, r : r + 1, :] = diag_ref[c : c + 1, r * LANES : (r + 1) * LANES]
 
 
@@ -200,8 +207,8 @@
 
 
 def pair_body(
-    nspace, capacity, pack, blocks, table_ref, nodes_ref, diag_ref, gap_ref, stiff_ref, place_ref,
-    block_ref, out_ref, rows_ref, entry_ref,
+    nspace, capacity, pack, blocks,
+    table_ref, nodes_ref, diag_ref, gap_ref, stiff_ref, matrix_ref, out_hbm, rows_ref, out_ref, sem,
 ):
     offset = (lax.axis_index("space") % pack) * capacity
     picked = looked_up(table_ref, [nodes_ref[j] for j in range(5)], capacity, offset, nspace)
@@ -217,20 +224,22 @@
         centre = (picked[1][c] + picked[2][c] + picked[3][c] + picked[4][c]) * 0.25
         gap = gap + (slave[c] - centre) * normal[c]
     push = stiff_ref[...] * jnp.maximum(-gap, 0.0)
-    pairs = rows_ref.shape[1]
+    out_ref[...] = jnp.zeros(out_ref.shape, jnp.float32)
     rows_ref[...] = jnp.zeros(rows_ref.shape, jnp.float32)
     for c in range(3):
         force = push * normal[c]
         for r in range(force.shape[0]):
             rows_ref[c : c + 1, r * LANES : (r + 1) * LANES] = force[r : r + 1]
-    parts = parts_of(rows_ref[...])
-    fourth = [part * -0.25 for part in parts]
-    for j in range(5):
-        entries = spread(fourth if j else parts, block_ref[j : j + 1, :], blocks)
-        entry_ref[:, j * pairs : (j + 1) * pairs] = jnp.concatenate(entries, 0)
-    out_ref[...] = jnp.zeros(out_ref.shape, jnp.float32)
-    got = contract_lanes(entry_ref[...], place_ref[...])
-    write_messages(out_ref, got, pack, blocks)
+    parts = [part.astype(jnp.bfloat16) for part in parts_of(rows_ref[...])]
+    got = contract_lanes(jnp.concatenate(parts, 0), matrix_ref[...])
+    total = got[0:8] + got[8:16] + got[16:24]
+    width = pack * capacity
+    for b in range(blocks):
+        for q in range(pack):
+            out_ref[b * pack + q, :, 0:width] = total[:, b * width : (b + 1) * width]
+    copy = pltpu.make_async_copy(out_ref, out_hbm, sem)
+    copy.start()
+    copy.wait()
 
 
 def split(value):
@@ -307,9 +316,61 @@
     return result
 
 
+def along_z(p, r):
+    lane = lax.broadcasted_iota(jnp.int32, p.shape, 2)
+    block = lax.broadcasted_iota(jnp.int32, p.shape, 0)
+    nb = p.shape[0]
+    up = pltpu.roll(p + r, 1, 2)
+    before_up = jnp.concatenate([jnp.zeros_like(up[:1]), up[:-1]], 0)
+    last = (lane == LANES - 1) & (block == nb - 1)
+    return jnp.where(lane == 0, before_up, up) + jnp.where(last, 0.0, p - r)
+
+
+def edge_body(u_ref, v_ref, stress_ref, hour_ref, yu, xu, xd, beyond_ref, row_ref):
+    planes, columns, _ = u_ref.shape[1:]
+    rows = row_ref.shape[0]
+    row_ref[...] = jnp.zeros(row_ref.shape, jnp.float32)
+
+    def assembled(first, middle, last):
+        row_ref[0:1, :] = first
+        row_ref[1 : planes + 1, :] = middle
+        if last is not None:
+            row_ref[planes + 1 : planes + 2, :] = last
+        return split(row_ref[...])
+
+    def line(ref, at):
+        return ref[at : at + 1, :]
+
+    def following(q):
+        return pltpu.roll(q, rows - 1, 1)
+
+    def own(c):
+        middle = component(u_ref, v_ref, stress_ref, hour_ref, c)[:, columns - 1, :]
+        at = c * columns + columns - 1
+        return assembled(line(xd, at), middle, line(xu, at) if c < 6 else None)
+
+    own_s, own_d, next_s, next_d = [], [], [], []
+    for c in range(6):
+        s, d = z_pair(own(c))
+        own_s.append(s)
+        own_d.append(d)
+        last = line(xu, 6 * columns + c)
+        s, d = z_pair(assembled(line(xd, 13 * columns + c), yu[c], last))
+        next_s.append(s)
+        next_d.append(d)
+    lower = node_terms(own_s, own_d, next_s, next_d)
+    upper = [tuple(following(q) for q in terms) for terms in lower]
+    factors = element_terms(lower, upper, [own(6 + c) for c in range(6)], own(12))
+    after = [[following(q) for q in terms] for terms in factors]
+    for m, (a, b, c, e) in enumerate(gathered_x(factors, after)):
+        force = along_z(a + b, c + e)[:, 0:planes]
+        for k in range(force.shape[0]):
+            beyond_ref[m, :, k * LANES : (k + 1) * LANES] = force[k]
+
+
 def element_body(
     u_ref, v_ref, stress_ref, hour_ref, mass_ref, yu, xu, xd,
-    out_ref, beyond_ref, row_ref, halo_s, halo_d, last_ref, node_ref, elem_ref,
+    out_ref, row_ref, halo_s, halo_d, node_ref, elem_ref,
 ):
     planes, columns, depth = u_ref.shape[1:]
     nb = depth // LANES
@@ -357,20 +418,10 @@
     def kept_elements():
         return [[elem_ref[m, t] for t in range(7)] for m in range(3)]
 
-    def along_z(p, r):
-        lane = lax.broadcasted_iota(jnp.int32, p.shape, 2)
-        block = lax.broadcasted_iota(jnp.int32, p.shape, 0)
-        up = pltpu.roll(p + r, 1, 2)
-        before_up = jnp.concatenate([jnp.zeros_like(up[:1]), up[:-1]], 0)
-        last = (lane == LANES - 1) & (block == nb - 1)
-        return jnp.where(lane == 0, before_up, up) + jnp.where(last, 0.0, p - r)
-
     def write_plane(before, after, i):
         weight = (time_step / 64.0) / split(mass_ref[i])
         for m, (a, b, c, e) in enumerate(gathered_x(before, after)):
             ab, ce = a + b, c + e
-            last_ref[m, 0, :, pl.ds(i, 1), :] = ab[:, columns - 1 : columns]
-            last_ref[m, 1, :, pl.ds(i, 1), :] = ce[:, columns - 1 : columns]
             p = (a - b) + jnp.where(row == 0, 0.0, pltpu.roll(ab, 1, 1))
             r = (c - e) + jnp.where(row == 0, 0.0, pltpu.roll(ce, 1, 1))
             result = split(v_ref[m, i]) - along_z(p, r) * weight
@@ -403,10 +454,6 @@
 
     lax.fori_loop(1, planes, loop, 0)
     step(planes, node_plane([split(above(c)) for c in range(6)], planes + 1))
-    for m in range(3):
-        force = along_z(last_ref[m, 0], last_ref[m, 1])
-        for k in range(nb):
-            beyond_ref[m, :, k * LANES : (k + 1) * LANES] = force[k]
 
 
 def final_body(
@@ -470,7 +517,6 @@
         return jax.ShapeDtypeStruct(shape, f32)
 
     message = sized(nspace, 8, LANES)
-    width = pack * capacity
     small = (pair_nodes, pair_diagonals, pair_gap.reshape(lines, LANES))
     small += (pair_stiffness.reshape(lines, LANES),)
     kept = (displacement, velocity, stress, hourglass, mass) + small
@@ -505,40 +551,49 @@
     )
     xu = shifted(xdn, "space", -1)
     xd = shifted(xup, "space", 1)
-    place, block, nodes, diagonals = kernel_call(
-        functools.partial(places_body, width, blocks),
+    slots = (nspace * capacity + 15) // 16 * 16
+    matrix, nodes, diagonals = kernel_call(
+        matrix_body,
         (pair_nodes, pair_diagonals),
         (
-            jax.ShapeDtypeStruct(((width + 15) // 16 * 16, 5 * pairs), jnp.bfloat16),
-            jax.ShapeDtypeStruct((5, pairs), jnp.int32),
+            jax.ShapeDtypeStruct((slots, pairs), jnp.bfloat16),
             jax.ShapeDtypeStruct((5, lines, LANES), jnp.int32),
             sized(6, lines, LANES),
         ),
     )
     slot_force = kernel_call(
         functools.partial(pair_body, nspace, capacity, pack, blocks),
-        (received, nodes, diagonals, gap, stiffness, place, block),
-        message,
-        [pltpu.VMEM((8, pairs), f32), pltpu.VMEM((24 * blocks, 5 * pairs), jnp.bfloat16)],
+        (received, nodes, diagonals, gap, stiffness, matrix),
+        pltpu.HBM(message.shape, f32),
+        [
+            pltpu.VMEM((8, pairs), f32),
+            pltpu.VMEM(message.shape, f32),
+            pltpu.SemaphoreType.DMA,
+        ],
     )
     returned = exchanged(slot_force)
 
     nb = depth // LANES
     rows = (planes + 2 + 7) // 8 * 8
-    base, beyond = kernel_call(
+    beyond = kernel_call(
+        edge_body,
+        (*fields[:4], yu, xu, xd),
+        sized(3, planes, depth),
+        [pltpu.VMEM((rows, depth), f32)],
+    )
+    left = shifted(beyond, "slab", 1)
+    base = kernel_call(
         element_body,
         (*fields, yu, xu, xd),
-        (sized(*displacement.shape), sized(3, planes, depth)),
+        sized(*displacement.shape),
         [
             pltpu.VMEM((rows, depth), f32),
             pltpu.VMEM((6, nb, rows, LANES), f32),
             pltpu.VMEM((6, nb, rows, LANES), f32),
-            pltpu.VMEM((3, 2, nb, planes, LANES), f32),
             pltpu.VMEM((6, 3, nb, columns, LANES), f32),
             pltpu.VMEM((3, 7, nb, columns, LANES), f32),
         ],
     )
-    left = shifted(beyond, "slab", 1)
 
     return kernel_call(
         functools.partial(final_body, nspace, capacity, pack),

time: 33.7 us -> 32.5 us (0.964)
  waiting for transfers between devices: 7.56 us -> 5.59 us
  Pallas kernels: 8.8 us -> 9.57 us
    all_to_all x2, waiting for transfers between devices: 4.72 us -> 3.36 us  [exchanged(): lax.all_to_all(value, 'space', split_axis=0, concat_axis=0, tiled=True)]
    pallas_call x6 -> x7, Pallas kernels: 8.8 us -> 9.57 us  [kernel_call(): pl.pallas_call(body, out_shape=outs, in_specs=[pl.BlockSpec(memory_space=...]
    ppermute x4, waiting for transfers between devices: 2.84 us -> 2.22 us  [shifted(): lax.ppermute(value, axis, [(at, (at + steps) % count) for at in range(cou...]
  transfers between devices with their start and end apart: 6 -> 6, of which waited for: 4 -> 3; matrix products, arithmetic and copies ran while one was open for 0% -> 0% of each run, Pallas kernels for 17% -> 20%
where the time goes in v2:
time: 32.5 us; the launch traced here: 32.2 us
  starting transfers between devices  17 us (52%)
  Pallas kernels  9.57 us (29%)
  waiting for transfers between devices  5.59 us (17%)
    pallas_call x7, Pallas kernels, kernel_call(): pl.pallas_call(body, out_shape=outs, in_specs=[pl.BlockSpec(memory_space=...  9.57 us
    ppermute x4, starting transfers between devices, shifted(): lax.ppermute(value, axis, [(at, (at + steps) % count) for at in range(cou...  8.79 us
    all_to_all x2, starting transfers between devices, exchanged(): lax.all_to_all(value, 'space', split_axis=0, concat_axis=0, tiled=True)  8.23 us
    all_to_all x2, waiting for transfers between devices, exchanged(): lax.all_to_all(value, 'space', split_axis=0, concat_axis=0, tiled=True)  3.36 us
    ppermute x4, waiting for transfers between devices, shifted(): lax.ppermute(value, axis, [(at, (at + steps) % count) for at in range(cou...  2.22 us
  transfers between devices with their start and end apart: 6, of which 3 were waited for; matrix products, arithmetic and copies ran while one was open for 0% of the time, Pallas kernels for 20%

profile of v2, /device:TPU:0, one launch (start us, length us, event | category | flops | bytes accessed | tf_op | source)
XLA Modules:
  0.0 32.2 jit_solution(12663369063890740645)
XLA Ops:
  0.0 2.0 %shard_map.100 = (f32[8,8,128]{2,1,0:T(8,128)}, f32[6,16,256]{2,1,0:T(8,128)S(1)}, s32[2,128]{1,0:T(2,128)S(1)}, f32[3,16,8,256]{3,2,1,0:T(8,128)S(1)}, f32[3,16...) custom-call(f32[3,16,8,256]{3,2,1,0:T(8,128)} %u_hbm.1, ...), custom_call_target="tpu_custom_call" | custom-call | tf_op jit(solution)/shard_map/pallas_call | solution.py:35
  2.0 2.5 %collective-permute-start = (f32[6,16,256]{2,1,0:T(8,128)S(1)}, f32[6,16,256]{2,1,0:T(8,128)S(1)}, u32[]{:S(2)}, u32[]{:S(2)}) collective-permute-start(f32[6,16,256]{2,1,0:T(8,128)S(1)} %get-tuple-element.27), channel_id=1, source_target_pairs={{0,3},{1,0},{2,1},{3,2},{4,7},{5,4},{6,5},{7,6},{8,11},{9,8},{10,9... | collective-permute-start | bytes 294920 | tf_op jit(solution)/shard_map/ppermute | solution.py:18
  4.5 2.2 %collective-permute-done.yu = f32[6,16,256]{2,1,0:T(8,128)S(1)} collective-permute-done((f32[6,16,256]{2,1,0:T(8,128)S(1)}, f32[6,16,256]{2,1,0:T(8,128)S(1)}, u32[]{:S(2)}, u32[]{:S(2)}) %collective-permute-start) | collective-permute-done | bytes 98336 | tf_op jit(solution)/shard_map/ppermute | solution.py:18
  6.7 1.6 %collective-permute-start.2 = (f32[112,256]{1,0:T(8,128)S(1)}, f32[112,256]{1,0:T(8,128)S(1)}, u32[]{:S(2)}, u32[]{:S(2)}) collective-permute-start(f32[112,256]{1,0:T(8,128)S(1)} %get-tuple-element.29), channel_id=1, source_target_pairs={{0,4},{4,8},{8,12},{12,16},{16,20},{20,24},{24,28},{28,0},{1,5},{5... | collective-permute-start | bytes 344072 | tf_op jit(solution)/shard_map/ppermute | solution.py:18
  8.3 4.9 %all-to-all-start = ((f32[8,8,128]{2,1,0:T(8,128)}), f32[8,8,128]{2,1,0:T(8,128)S(1)}, u32[]{:S(2)}, u32[]{:S(2)}) async-start(f32[8,8,128]{2,1,0:T(8,128)} %get-tuple-element.30), calls=%async_computation | async-start | bytes 65536 | tf_op jit(solution)/shard_map/all_to_all | solution.py:22
  13.2 4.7 %collective-permute-start.1 = (f32[56,256]{1,0:T(8,128)S(1)}, f32[56,256]{1,0:T(8,128)S(1)}, u32[]{:S(2)}, u32[]{:S(2)}) collective-permute-start(f32[56,256]{1,0:T(8,128)S(1)} %get-tuple-element.28), channel_id=1, source_target_pairs={{0,28},{4,0},{8,4},{12,8},{16,12},{20,16},{24,20},{28,24},{1,29},{... | collective-permute-start | bytes 172040 | tf_op jit(solution)/shard_map/ppermute | solution.py:18
  17.9 1.0 %shard_map.103 = (bf16[384,1024]{1,0:T(8,128)(2,1)S(1)}, s32[5,8,128]{2,1,0:T(8,128)S(1)}, f32[6,8,128]{2,1,0:T(8,128)S(1)}) custom-call(s32[5,1024]{1,0:T(8,128)S(1)} %get-tuple-element.31.nodes_ref, f32[6,1024]{1,0:T(8,128)S(1)} %get-tuple-element.32.diag_ref), custom_call_target="tpu_custom_call" | custom-call | tf_op jit(solution)/shard_map/pallas_call | solution.py:35
  18.9 0.9 %all-to-all-done.table_ref = f32[8,8,128]{2,1,0:T(8,128)S(1)} async-done(((f32[8,8,128]{2,1,0:T(8,128)}), f32[8,8,128]{2,1,0:T(8,128)S(1)}, u32[]{:S(2)}, u32[]{:S(2)}) %all-to-all-start) | async-done | bytes 32800 | tf_op jit(solution)/shard_map/all_to_all | solution.py:22
  19.8 1.4 %shard_map.104 = f32[8,8,128]{2,1,0:T(8,128)} custom-call(f32[8,8,128]{2,1,0:T(8,128)S(1)} %all-to-all-done.table_ref, s32[5,8,128]{2,1,0:T(8,128)S(1)} %get-tuple-element.33.nodes_ref, f32[6,8,128]{2,1,0:T(8,128)S(1)} %get-tuple-element.34.diag_ref, f32[8,128]{1,0:T(8,128)S(1)} %get-tuple-element.35.gap_ref, f32[8,128]{1,0:T(8,128)S(1)} %get-tuple-element.36.stiff_ref, ...), custom_call_target="tpu_custom_call" | custom-call | tf_op jit(solution)/shard_map/pallas_call | solution.py:35
  21.2 3.4 %all-to-all-start.1 = ((f32[8,8,128]{2,1,0:T(8,128)}), f32[8,8,128]{2,1,0:T(8,128)S(1)}, u32[]{:S(2)}, u32[]{:S(2)}) async-start(f32[8,8,128]{2,1,0:T(8,128)} %shard_map.104), calls=%async_computation.1 | async-start | bytes 65536 | tf_op jit(solution)/shard_map/all_to_all | solution.py:22
  24.6 0.0 collective-permute-done.1.xu
  24.6 0.0 collective-permute-done.2.xd
  24.6 0.5 %shard_map.105 = f32[3,16,256]{2,1,0:T(8,128)S(1)} custom-call(f32[3,16,8,256]{3,2,1,0:T(8,128)S(1)} %get-tuple-element.22.u_ref, f32[3,16,8,256]{3,2,1,0:T(8,128)S(1)} %get-tuple-element.23.v_ref, f32[6,16,8,256]{3,2,1,0:T(8,128)S(1)} %get-tuple-element.24.stress_ref, f32[16,8,256]{2,1,0:T(8,128)S(1)} %get-tuple-element.25.hour_ref, ...), custom_call_target="tpu_custom_call" | custom-call | tf_op jit(solution)/shard_map/pallas_call | solution.py:35
  25.1 0.0 collective-permute-start.3
  25.1 3.6 %shard_map.102.base_ref = f32[3,16,8,256]{3,2,1,0:T(8,128)S(1)} custom-call(f32[3,16,8,256]{3,2,1,0:T(8,128)S(1)} %get-tuple-element.22.u_ref, f32[3,16,8,256]{3,2,1,0:T(8,128)S(1)} %get-tuple-element.23.v_ref, f32[6,16,8,256]{3,2,1,0:T(8,128)S(1)} %get-tuple-element.24.stress_ref, f32[16,8,256]{2,1,0:T(8,128)S(1)} %get-tuple-element.25.hour_ref, ...), custom_call_target="tpu_custom_call" | custom-call | tf_op jit(solution)/shard_map/pallas_call | solution.py:35
  28.8 2.4 %all-to-all-done.1.table_ref = f32[8,8,128]{2,1,0:T(8,128)S(1)} async-done(((f32[8,8,128]{2,1,0:T(8,128)}), f32[8,8,128]{2,1,0:T(8,128)S(1)}, u32[]{:S(2)}, u32[]{:S(2)}) %all-to-all-start.1) | async-done | bytes 32800 | tf_op jit(solution)/shard_map/all_to_all | solution.py:22
  31.2 0.0 collective-permute-done.3.left_ref
  31.2 1.0 %shard_map.106 = f32[3,16,8,256]{3,2,1,0:T(8,128)} custom-call(f32[3,16,8,256]{3,2,1,0:T(8,128)S(1)} %shard_map.102.base_ref, f32[16,8,256]{2,1,0:T(8,128)S(1)} %get-tuple-element.26.mass_ref, f32[8,8,128]{2,1,0:T(8,128)S(1)} %all-to-all-done.1.table_ref, s32[2,128]{1,0:T(2,128)S(1)} %get-tuple-element.38.route_ref, ...), custom_call_target="tpu_custom_call" | custom-call | tf_op jit(solution)/shard_map/pallas_call | solution.py:35
  (1 shorter events, 0.0 us)
Async XLA Ops:
  2.0 4.7 %collective-permute-start = (f32[6,16,256]{2,1,0:T(8,128)S(1)}, f32[6,16,256]{2,1,0:T(8,128)S(1)}, u32[]{:S(2)}, u32[]{:S(2)}) collective-permute-start(f32[6,16,256]{2,1,0:T(8,128)S(1)} %get-tuple-element.27), channel_id=1, source_target_pairs={{0,3},{1,0},{2,1},{3,2},{4,7},{5,4},{6,5},{7,6},{8,11},{9,8},{10,9... | collective-permute-start | bytes 294920 | tf_op jit(solution)/shard_map/ppermute | solution.py:18
  6.7 17.9 %collective-permute-start.2 = (f32[112,256]{1,0:T(8,128)S(1)}, f32[112,256]{1,0:T(8,128)S(1)}, u32[]{:S(2)}, u32[]{:S(2)}) collective-permute-start(f32[112,256]{1,0:T(8,128)S(1)} %get-tuple-element.29), channel_id=1, source_target_pairs={{0,4},{4,8},{8,12},{12,16},{16,20},{20,24},{24,28},{28,0},{1,5},{5... | collective-permute-start | bytes 344072 | tf_op jit(solution)/shard_map/ppermute | solution.py:18
  8.3 11.6 %all-to-all-start = ((f32[8,8,128]{2,1,0:T(8,128)}), f32[8,8,128]{2,1,0:T(8,128)S(1)}, u32[]{:S(2)}, u32[]{:S(2)}) async-start(f32[8,8,128]{2,1,0:T(8,128)} %get-tuple-element.30), calls=%async_computation | async-start | bytes 65536 | tf_op jit(solution)/shard_map/all_to_all | solution.py:22
  13.2 11.4 %collective-permute-start.1 = (f32[56,256]{1,0:T(8,128)S(1)}, f32[56,256]{1,0:T(8,128)S(1)}, u32[]{:S(2)}, u32[]{:S(2)}) collective-permute-start(f32[56,256]{1,0:T(8,128)S(1)} %get-tuple-element.28), channel_id=1, source_target_pairs={{0,28},{4,0},{8,4},{12,8},{16,12},{20,16},{24,20},{28,24},{1,29},{... | collective-permute-start | bytes 172040 | tf_op jit(solution)/shard_map/ppermute | solution.py:18
  21.2 10.0 %all-to-all-start.1 = ((f32[8,8,128]{2,1,0:T(8,128)}), f32[8,8,128]{2,1,0:T(8,128)S(1)}, u32[]{:S(2)}, u32[]{:S(2)}) async-start(f32[8,8,128]{2,1,0:T(8,128)} %shard_map.104), calls=%async_computation.1 | async-start | bytes 65536 | tf_op jit(solution)/shard_map/all_to_all | solution.py:22
  25.1 6.1 %collective-permute-start.3 = (f32[3,16,256]{2,1,0:T(8,128)S(1)}, f32[3,16,256]{2,1,0:T(8,128)S(1)}, u32[]{:S(2)}, u32[]{:S(2)}) collective-permute-start(f32[3,16,256]{2,1,0:T(8,128)S(1)} %shard_map.105), channel_id=1, source_target_pairs={{0,1},{1,2},{2,3},{3,0},{4,5},{5,6},{6,7},{7,4},{8,9},{9,10},{10,1... | collective-permute-start | bytes 147464 | tf_op jit(solution)/shard_map/ppermute | solution.py:18

commit v3 on v2

--- a/solution.py
+++ b/solution.py
@@ -95,9 +95,9 @@
     capacity, pack, blocks, u_hbm, route_hbm, v_hbm, *rest,
 ):
     hbm, rest = (u_hbm, route_hbm, v_hbm) + rest[:7], rest[7:]
-    message_hbm, ydn, sides_ref, u_ref, v_ref = rest[:5]
+    message_hbm, ydn, xdn, xup, sides_ref, u_ref, v_ref, stress_ref, hour_ref = rest[:9]
     out_ref, rows_ref, route_ref, sems, message_sem = rest[-5:]
-    targets = (u_ref, route_ref, v_ref) + rest[5:-5]
+    targets = (u_ref, route_ref, v_ref, stress_ref, hour_ref) + rest[9:-5]
     copies = [
         pltpu.make_async_copy(source, target, sems.at[at])
         for at, (source, target) in enumerate(zip(hbm, targets))
@@ -127,12 +127,15 @@
     message.start()
     sides_ref[0:1, :] = route[:, 0:side]
     sides_ref[1:2, :] = route[:, side : 2 * side]
-    for c in range(3):
-        ydn[c] = u_ref[c, :, 0, :]
-    copies[2].wait()
-    for c in range(3):
-        ydn[3 + c] = v_ref[c, :, 0, :]
-    for copy in copies[3:]:
+    for copy in copies[2:5]:
+        copy.wait()
+    for c in range(13):
+        ref = component(u_ref, v_ref, stress_ref, hour_ref, c)
+        xup[c * columns : (c + 1) * columns, :] = ref[planes - 1]
+        if c < 6:
+            xdn[c * columns : (c + 1) * columns, :] = ref[0]
+            ydn[c] = ref[:, 0, :]
+    for copy in copies[5:]:
         copy.wait()
     message.wait()
 
@@ -147,17 +150,11 @@
     return hour_ref
 
 
-def second_body(u_ref, v_ref, stress_ref, hour_ref, yu, xdn, xup):
-    planes, columns = u_ref.shape[1:3]
-    for c in range(13):
-        ref = component(u_ref, v_ref, stress_ref, hour_ref, c)
-        xup[c * columns : (c + 1) * columns, :] = ref[planes - 1]
-        if c < 6:
-            at = 13 * columns + c
-            xup[at : at + 1, :] = yu[c, planes - 1 : planes, :]
-            xdn[c * columns : (c + 1) * columns, :] = ref[0]
-            at = 6 * columns + c
-            xdn[at : at + 1, :] = yu[c, 0:1, :]
+def corner_body(columns, xu, xd, out_ref):
+    out_ref[...] = jnp.zeros(out_ref.shape, jnp.float32)
+    for c in range(6):
+        out_ref[c : c + 1, :] = xd[c * columns : c * columns + 1, :]
+        out_ref[8 + c : 9 + c, :] = xu[c * columns : c * columns + 1, :]
 
 
 def matrix_body(nodes_ref, diag_ref, matrix_ref, lines_ref, diag_lines_ref):
@@ -326,7 +323,7 @@
     return jnp.where(lane == 0, before_up, up) + jnp.where(last, 0.0, p - r)
 
 
-def edge_body(u_ref, v_ref, stress_ref, hour_ref, yu, xu, xd, beyond_ref, row_ref):
+def edge_body(u_ref, v_ref, stress_ref, hour_ref, yu, xu, xd, corner, beyond_ref, row_ref):
     planes, columns, _ = u_ref.shape[1:]
     rows = row_ref.shape[0]
     row_ref[...] = jnp.zeros(row_ref.shape, jnp.float32)
@@ -354,8 +351,7 @@
         s, d = z_pair(own(c))
         own_s.append(s)
         own_d.append(d)
-        last = line(xu, 6 * columns + c)
-        s, d = z_pair(assembled(line(xd, 13 * columns + c), yu[c], last))
+        s, d = z_pair(assembled(line(corner, c), yu[c], line(corner, 8 + c)))
         next_s.append(s)
         next_d.append(d)
     lower = node_terms(own_s, own_d, next_s, next_d)
@@ -368,97 +364,141 @@
             beyond_ref[m, :, k * LANES : (k + 1) * LANES] = force[k]
 
 
-def element_body(
-    u_ref, v_ref, stress_ref, hour_ref, mass_ref, yu, xu, xd,
-    out_ref, row_ref, halo_s, halo_d, node_ref, elem_ref,
+def node_plane(values, halo_s, halo_d):
+    row = lax.broadcasted_iota(jnp.int32, values[0].shape, 1)
+    end = values[0].shape[1] - 1
+    sums, diffs, sums_next, diffs_next = [], [], [], []
+    for c in range(6):
+        s, d = z_pair(values[c])
+        sums.append(s)
+        diffs.append(d)
+        sums_next.append(jnp.where(row == end, halo_s[c], pltpu.roll(s, end, 1)))
+        diffs_next.append(jnp.where(row == end, halo_d[c], pltpu.roll(d, end, 1)))
+    return node_terms(sums, diffs, sums_next, diffs_next)
+
+
+def kept_nodes(node_ref, i):
+    return [tuple(node_ref[i, c, t] for t in range(3)) for c in range(6)]
+
+
+def kept_elements(elem_ref, i):
+    return [[elem_ref[i, m, t] for t in range(7)] for m in range(3)]
+
+
+def new_velocity(before, after, velocity, mass):
+    row = lax.broadcasted_iota(jnp.int32, mass.shape, 1)
+    weight = (time_step / 64.0) / mass
+    result = []
+    for m, (a, b, c, e) in enumerate(gathered_x(before, after)):
+        p = (a - b) + jnp.where(row == 0, 0.0, pltpu.roll(a + b, 1, 1))
+        r = (c - e) + jnp.where(row == 0, 0.0, pltpu.roll(c + e, 1, 1))
+        result.append(velocity[m] - along_z(p, r) * weight)
+    return result
+
+
+def steps(start, stop, unroll, body):
+    count = (stop - start) // unroll
+
+    def several(t, carry):
+        for k in range(unroll):
+            body(start + t * unroll + k)
+        return carry
+
+    lax.fori_loop(0, count, several, 0)
+    for i in range(start + count * unroll, stop):
+        body(i)
+
+
+def inner_body(
+    unroll, u_ref, v_ref, stress_ref, hour_ref, mass_ref, yu, out_ref, node_ref, elem_ref, halo_s, halo_d
 ):
-    planes, columns, depth = u_ref.shape[1:]
+    planes, _, depth = u_ref.shape[1:]
     nb = depth // LANES
-
-    def below(c):
-        return xd[c * columns : (c + 1) * columns, :]
-
-    def above(c):
-        return xu[c * columns : (c + 1) * columns, :]
-
-    row_ref[...] = jnp.zeros(row_ref.shape, jnp.float32)
     for c in range(6):
-        row_ref[0:1, :] = xd[13 * columns + c : 13 * columns + c + 1, :]
-        row_ref[1 : planes + 1, :] = yu[c]
-        row_ref[planes + 1 : planes + 2, :] = xu[6 * columns + c : 6 * columns + c + 1, :]
-        halo_s[c], halo_d[c] = z_pair(split(row_ref[...]))
-
-    row = lax.broadcasted_iota(jnp.int32, (nb, columns, LANES), 1)
-
-    def node_plane(values, at):
-        sums, diffs, sums_next, diffs_next = [], [], [], []
-        for c in range(6):
-            s, d = z_pair(values[c])
-            sums.append(s)
-            diffs.append(d)
-            hs = halo_s[c, :, pl.ds(at, 1), :]
-            hd = halo_d[c, :, pl.ds(at, 1), :]
-            sums_next.append(jnp.where(row == columns - 1, hs, pltpu.roll(s, columns - 1, 1)))
-            diffs_next.append(jnp.where(row == columns - 1, hd, pltpu.roll(d, columns - 1, 1)))
-        return node_terms(sums, diffs, sums_next, diffs_next)
-
-    def keep_nodes(terms):
+        halo_s[c], halo_d[c] = z_pair(split(yu[c]))
+
+    def nodes(i):
+        values = [split(u_ref[c, i]) for c in range(3)] + [split(v_ref[c, i]) for c in range(3)]
+        terms = node_plane(
+            values,
+            [halo_s[c, :, pl.ds(i, 1), :] for c in range(6)],
+            [halo_d[c, :, pl.ds(i, 1), :] for c in range(6)],
+        )
         for c in range(6):
             for t in range(3):
-                node_ref[c, t] = terms[c][t]
-
-    def kept_nodes():
-        return [tuple(node_ref[c, t] for t in range(3)) for c in range(6)]
-
-    def keep_elements(factors):
+                node_ref[i, c, t] = terms[c][t]
+
+    def elements(i):
+        factors = element_terms(
+            kept_nodes(node_ref, i),
+            kept_nodes(node_ref, i + 1),
+            [split(stress_ref[c, i]) for c in range(6)],
+            split(hour_ref[i]),
+        )
         for m in range(3):
             for t in range(7):
-                elem_ref[m, t] = factors[m][t]
-
-    def kept_elements():
-        return [[elem_ref[m, t] for t in range(7)] for m in range(3)]
-
-    def write_plane(before, after, i):
-        weight = (time_step / 64.0) / split(mass_ref[i])
-        for m, (a, b, c, e) in enumerate(gathered_x(before, after)):
-            ab, ce = a + b, c + e
-            p = (a - b) + jnp.where(row == 0, 0.0, pltpu.roll(ab, 1, 1))
-            r = (c - e) + jnp.where(row == 0, 0.0, pltpu.roll(ce, 1, 1))
-            result = split(v_ref[m, i]) - along_z(p, r) * weight
+                elem_ref[i, m, t] = factors[m][t]
+
+    def forces(i):
+        result = new_velocity(
+            kept_elements(elem_ref, i - 1),
+            kept_elements(elem_ref, i),
+            [split(v_ref[m, i]) for m in range(3)],
+            split(mass_ref[i]),
+        )
+        for m in range(3):
             for k in range(nb):
-                out_ref[m, i, :, k * LANES : (k + 1) * LANES] = result[k]
-
-    def own_nodes(i):
-        return [split(u_ref[c, i]) for c in range(3)] + [split(v_ref[c, i]) for c in range(3)]
-
-    keep_nodes(node_plane([split(below(c)) for c in range(6)], 0))
-    current = node_plane(own_nodes(0), 1)
-    keep_elements(
-        element_terms(
-            kept_nodes(), current, [split(below(6 + c)) for c in range(6)], split(below(12))
+                out_ref[m, i, :, k * LANES : (k + 1) * LANES] = result[m][k]
+
+    steps(0, planes, unroll, nodes)
+    steps(0, planes - 1, unroll, elements)
+    steps(1, planes - 1, unroll, forces)
+
+
+def outer_body(
+    v_ref, stress_ref, hour_ref, mass_ref, node_ref, elem_ref, xu, xd, corner, out_ref
+):
+    planes, columns, depth = v_ref.shape[1:]
+    last = planes - 1
+
+    def part(ref, c):
+        return split(ref[c * columns : (c + 1) * columns, :])
+
+    def plane_terms(ref, at):
+        halo_s, halo_d = z_pair(split(corner[at : at + 8, :]))
+        return node_plane(
+            [part(ref, c) for c in range(6)],
+            [halo_s[:, c : c + 1] for c in range(6)],
+            [halo_d[:, c : c + 1] for c in range(6)],
         )
-    )
-    keep_nodes(current)
-
-    def step(i, upper):
-        factors = element_terms(
-            kept_nodes(), upper, [split(stress_ref[c, i - 1]) for c in range(6)], split(hour_ref[i - 1])
-        )
-        write_plane(kept_elements(), factors, i - 1)
-        keep_elements(factors)
-        keep_nodes(upper)
-
-    def loop(i, carry):
-        step(i, node_plane(own_nodes(i), i + 1))
-        return carry
-
-    lax.fori_loop(1, planes, loop, 0)
-    step(planes, node_plane([split(above(c)) for c in range(6)], planes + 1))
+
+    below = element_terms(
+        plane_terms(xd, 0),
+        kept_nodes(node_ref, 0),
+        [part(xd, 6 + c) for c in range(6)],
+        part(xd, 12),
+    )
+    above = element_terms(
+        kept_nodes(node_ref, last),
+        plane_terms(xu, 8),
+        [split(stress_ref[c, last]) for c in range(6)],
+        split(hour_ref[last]),
+    )
+    ends = (
+        (0, below, kept_elements(elem_ref, 0)),
+        (last, kept_elements(elem_ref, last - 1), above),
+    )
+    for at, (i, before, after) in enumerate(ends):
+        velocity = [split(v_ref[m, i]) for m in range(3)]
+        result = new_velocity(before, after, velocity, split(mass_ref[i]))
+        for m in range(3):
+            for k in range(depth // LANES):
+                out_ref[m, at, :, k * LANES : (k + 1) * LANES] = result[m][k]
 
 
 def final_body(
     nspace, capacity, pack,
-    base_ref, mass_ref, table_ref, route_ref, left_ref, out_hbm, rows_ref, out_ref, sems,
+    base_ref, outer_ref, mass_ref, table_ref, route_ref, left_ref, out_hbm, rows_ref, out_ref, sems,
 ):
     planes, columns, depth = base_ref.shape[1:]
     offset = (lax.axis_index("space") % pack) * capacity
@@ -481,7 +521,14 @@
                     for i in range(planes)
                 ]
             )
-            value = base_ref[m, :, :, k : k + LANES] - left * weights[k // LANES]
+            value = jnp.concatenate(
+                [
+                    outer_ref[m, 0:1, :, k : k + LANES],
+                    base_ref[m, 1 : planes - 1, :, k : k + LANES],
+                    outer_ref[m, 1:2, :, k : k + LANES],
+                ]
+            )
+            value = value - left * weights[k // LANES]
             if k == 0:
                 value = value + low_weight * turned
             if k == depth - LANES:
@@ -520,12 +567,14 @@
     small = (pair_nodes, pair_diagonals, pair_gap.reshape(lines, LANES))
     small += (pair_stiffness.reshape(lines, LANES),)
     kept = (displacement, velocity, stress, hourglass, mass) + small
-    outgoing, ydn, sides, *kept = kernel_call(
+    outgoing, ydn, xdn, xup, sides, *kept = kernel_call(
         functools.partial(first_body, capacity, pack, blocks),
         (displacement, contact_route.reshape(1, surf_count)) + kept[1:],
         (
             pltpu.HBM(message.shape, f32),
             sized(6, planes, depth),
+            sized(6 * columns, depth),
+            sized(13 * columns, depth),
             jax.ShapeDtypeStruct((2, surf_count // 2), jnp.int32),
             *(jax.ShapeDtypeStruct(one.shape, one.dtype) for one in kept),
         ),
@@ -539,16 +588,8 @@
         hbm_inputs=len(kept) + 1,
     )
     fields, (pair_nodes, pair_diagonals, gap, stiffness) = kept[:5], kept[5:]
+    received = exchanged(outgoing)
     yu = shifted(ydn, "slab", -1)
-    received = exchanged(outgoing)
-    xdn, xup = kernel_call(
-        second_body,
-        (*fields[:4], yu),
-        (
-            sized((6 * columns + 6 + 7) // 8 * 8, depth),
-            sized((13 * columns + 6 + 7) // 8 * 8, depth),
-        ),
-    )
     xu = shifted(xdn, "space", -1)
     xd = shifted(xup, "space", 1)
     slots = (nspace * capacity + 15) // 16 * 16
@@ -573,31 +614,37 @@
     )
     returned = exchanged(slot_force)
 
+    corner = kernel_call(functools.partial(corner_body, columns), (xu, xd), sized(16, depth))
+    corner = shifted(corner, "slab", -1)
     nb = depth // LANES
+    base, node, elem = kernel_call(
+        functools.partial(inner_body, 2),
+        (*fields, yu),
+        (
+            sized(*displacement.shape),
+            sized(planes, 6, 3, nb, columns, LANES),
+            sized(planes - 1, 3, 7, nb, columns, LANES),
+        ),
+        [
+            pltpu.VMEM((6, nb, planes, LANES), f32),
+            pltpu.VMEM((6, nb, planes, LANES), f32),
+        ],
+    )
     rows = (planes + 2 + 7) // 8 * 8
     beyond = kernel_call(
         edge_body,
-        (*fields[:4], yu, xu, xd),
+        (*fields[:4], yu, xu, xd, corner),
         sized(3, planes, depth),
         [pltpu.VMEM((rows, depth), f32)],
     )
     left = shifted(beyond, "slab", 1)
-    base = kernel_call(
-        element_body,
-        (*fields, yu, xu, xd),
-        sized(*displacement.shape),
-        [
-            pltpu.VMEM((rows, depth), f32),
-            pltpu.VMEM((6, nb, rows, LANES), f32),
-            pltpu.VMEM((6, nb, rows, LANES), f32),
-            pltpu.VMEM((6, 3, nb, columns, LANES), f32),
-            pltpu.VMEM((3, 7, nb, columns, LANES), f32),
-        ],
+    outer = kernel_call(
+        outer_body, (*fields[1:], node, elem, xu, xd, corner), sized(3, 2, columns, depth)
     )
 
     return kernel_call(
         functools.partial(final_body, nspace, capacity, pack),
-        (base, fields[4], returned, sides, left),
+        (base, outer, fields[4], returned, sides, left),
         pltpu.HBM(displacement.shape, f32),
         [
             pltpu.VMEM((3, LANES, LANES), f32),

time: 32.5 us -> 31.7 us (0.975)
  waiting for transfers between devices: 5.59 us -> 8.49 us
  starting transfers between devices: 17 us -> 14.4 us
  Pallas kernels: 9.57 us -> 8.51 us
    all_to_all x2, waiting for transfers between devices: 3.36 us -> 8.48 us  [exchanged(): lax.all_to_all(value, 'space', split_axis=0, concat_axis=0, tiled=True)]
    ppermute x4 -> x5, waiting for transfers between devices: 2.22 us -> 0.01 us  [shifted(): lax.ppermute(value, axis, [(at, (at + steps) % count) for at in range(cou...]
    all_to_all x2, starting transfers between devices: 8.23 us -> 6.7 us  [exchanged(): lax.all_to_all(value, 'space', split_axis=0, concat_axis=0, tiled=True)]
    ppermute x4 -> x5, starting transfers between devices: 8.79 us -> 7.67 us  [shifted(): lax.ppermute(value, axis, [(at, (at + steps) % count) for at in range(cou...]
    pallas_call x7 -> x8, Pallas kernels: 9.57 us -> 8.51 us  [kernel_call(): pl.pallas_call(body, out_shape=outs, in_specs=[pl.BlockSpec(memory_space=...]
  transfers between devices with their start and end apart: 6 -> 7, of which waited for: 3 -> 2; matrix products, arithmetic and copies ran while one was open for 0% -> 0% of each run, Pallas kernels for 20% -> 17%
where the time goes in v3:
time: 31.7 us; the launch traced here: 31.5 us
  starting transfers between devices  14.4 us (45%)
  Pallas kernels  8.51 us (27%)
  waiting for transfers between devices  8.49 us (27%)
    pallas_call x8, Pallas kernels, kernel_call(): pl.pallas_call(body, out_shape=outs, in_specs=[pl.BlockSpec(memory_space=...  8.51 us
    all_to_all x2, waiting for transfers between devices, exchanged(): lax.all_to_all(value, 'space', split_axis=0, concat_axis=0, tiled=True)  8.48 us
    ppermute x5, starting transfers between devices, shifted(): lax.ppermute(value, axis, [(at, (at + steps) % count) for at in range(cou...  7.67 us
    all_to_all x2, starting transfers between devices, exchanged(): lax.all_to_all(value, 'space', split_axis=0, concat_axis=0, tiled=True)  6.7 us
  transfers between devices with their start and end apart: 7, of which 2 were waited for; matrix products, arithmetic and copies ran while one was open for 0% of the time, Pallas kernels for 17%

profile of v3, /device:TPU:0, one launch (start us, length us, event | category | flops | bytes accessed | tf_op | source)
XLA Modules:
  0.0 31.5 jit_solution(11317309567831495149)
XLA Ops:
  0.0 2.0 %shard_map.100 = (f32[8,8,128]{2,1,0:T(8,128)}, f32[6,16,256]{2,1,0:T(8,128)S(1)}, f32[48,256]{1,0:T(8,128)S(1)}, f32[104,256]{1,0:T(8,128)S(1)}, s32[2,128]{1,0...) custom-call(f32[3,16,8,256]{3,2,1,0:T(8,128)} %u_hbm.1, ...), custom_call_target="tpu_custom_call" | custom-call | tf_op jit(solution)/shard_map/pallas_call | solution.py:35
  2.0 3.0 %collective-permute-start.2 = (f32[104,256]{1,0:T(8,128)S(1)}, f32[104,256]{1,0:T(8,128)S(1)}, u32[]{:S(2)}, u32[]{:S(2)}) collective-permute-start(f32[104,256]{1,0:T(8,128)S(1)} %get-tuple-element.35), channel_id=1, source_target_pairs={{0,4},{4,8},{8,12},{12,16},{16,20},{20,24},{24,28},{28,0},{1,5},{5... | collective-permute-start | bytes 319496 | tf_op jit(solution)/shard_map/ppermute | solution.py:18
  5.1 0.7 %collective-permute-start = (f32[6,16,256]{2,1,0:T(8,128)S(1)}, f32[6,16,256]{2,1,0:T(8,128)S(1)}, u32[]{:S(2)}, u32[]{:S(2)}) collective-permute-start(f32[6,16,256]{2,1,0:T(8,128)S(1)} %get-tuple-element.30), channel_id=1, source_target_pairs={{0,3},{1,0},{2,1},{3,2},{4,7},{5,4},{6,5},{7,6},{8,11},{9,8},{10,9... | collective-permute-start | bytes 294920 | tf_op jit(solution)/shard_map/ppermute | solution.py:18
  5.7 3.4 %collective-permute-start.1 = (f32[48,256]{1,0:T(8,128)S(1)}, f32[48,256]{1,0:T(8,128)S(1)}, u32[]{:S(2)}, u32[]{:S(2)}) collective-permute-start(f32[48,256]{1,0:T(8,128)S(1)} %get-tuple-element.34), channel_id=1, source_target_pairs={{0,28},{4,0},{8,4},{12,8},{16,12},{20,16},{24,20},{28,24},{1,29},{... | collective-permute-start | bytes 147464 | tf_op jit(solution)/shard_map/ppermute | solution.py:18
  9.1 3.3 %all-to-all-start = ((f32[8,8,128]{2,1,0:T(8,128)}), f32[8,8,128]{2,1,0:T(8,128)S(1)}, u32[]{:S(2)}, u32[]{:S(2)}) async-start(f32[8,8,128]{2,1,0:T(8,128)} %get-tuple-element.36), calls=%async_computation | async-start | bytes 65536 | tf_op jit(solution)/shard_map/all_to_all | solution.py:22
  12.5 0.0 collective-permute-done.1.xu
  12.5 0.0 collective-permute-done.2.xd
  12.5 0.5 %collective-permute-start.3 = (f32[16,256]{1,0:T(8,128)S(1)}, f32[16,256]{1,0:T(8,128)S(1)}, u32[]{:S(2)}, u32[]{:S(2)}) collective-permute-start(f32[16,256]{1,0:T(8,128)S(1)} %shard_map.102), channel_id=1, source_target_pairs={{0,3},{1,0},{2,1},{3,2},{4,7},{5,4},{6,5},{7,6},{8,11},{9,8},{10,9... | collective-permute-start | bytes 49160 | tf_op jit(solution)/shard_map/ppermute | solution.py:18
  13.0 1.0 %shard_map.104 = (bf16[384,1024]{1,0:T(8,128)(2,1)S(1)}, s32[5,8,128]{2,1,0:T(8,128)S(1)}, f32[6,8,128]{2,1,0:T(8,128)S(1)}) custom-call(s32[5,1024]{1,0:T(8,128)S(1)} %get-tuple-element.37.nodes_ref, f32[6,1024]{1,0:T(8,128)S(1)} %get-tuple-element.38.diag_ref), custom_call_target="tpu_custom_call" | custom-call | tf_op jit(solution)/shard_map/pallas_call | solution.py:35
  14.1 5.0 %all-to-all-done.table_ref = f32[8,8,128]{2,1,0:T(8,128)S(1)} async-done(((f32[8,8,128]{2,1,0:T(8,128)}), f32[8,8,128]{2,1,0:T(8,128)S(1)}, u32[]{:S(2)}, u32[]{:S(2)}) %all-to-all-start) | async-done | bytes 32800 | tf_op jit(solution)/shard_map/all_to_all | solution.py:22
  19.1 1.4 %shard_map.105 = f32[8,8,128]{2,1,0:T(8,128)} custom-call(f32[8,8,128]{2,1,0:T(8,128)S(1)} %all-to-all-done.table_ref, s32[5,8,128]{2,1,0:T(8,128)S(1)} %get-tuple-element.39.nodes_ref, f32[6,8,128]{2,1,0:T(8,128)S(1)} %get-tuple-element.40.diag_ref, f32[8,128]{1,0:T(8,128)S(1)} %get-tuple-element.41.gap_ref, f32[8,128]{1,0:T(8,128)S(1)} %get-tuple-element.42.stiff_ref, ...), custom_call_target="tpu_custom_call" | custom-call | tf_op jit(solution)/shard_map/pallas_call | solution.py:35
  20.5 3.4 %all-to-all-start.1 = ((f32[8,8,128]{2,1,0:T(8,128)}), f32[8,8,128]{2,1,0:T(8,128)S(1)}, u32[]{:S(2)}, u32[]{:S(2)}) async-start(f32[8,8,128]{2,1,0:T(8,128)} %shard_map.105), calls=%async_computation.1 | async-start | bytes 65536 | tf_op jit(solution)/shard_map/all_to_all | solution.py:22
  23.8 0.0 collective-permute-done.yu
  23.8 0.0 collective-permute-done.3.corner
  23.9 0.5 %shard_map.106 = f32[3,16,256]{2,1,0:T(8,128)S(1)} custom-call(f32[3,16,8,256]{3,2,1,0:T(8,128)S(1)} %get-tuple-element.25.u_ref, f32[3,16,8,256]{3,2,1,0:T(8,128)S(1)} %get-tuple-element.26.v_ref, f32[6,16,8,256]{3,2,1,0:T(8,128)S(1)} %get-tuple-element.27.stress_ref, f32[16,8,256]{2,1,0:T(8,128)S(1)} %get-tuple-element.28.hour_ref, ...), custom_call_target="tpu_custom_call" | custom-call | tf_op jit(solution)/shard_map/pallas_call | solution.py:35
  24.3 0.0 collective-permute-start.4
  24.4 2.3 %shard_map.101 = (f32[3,16,8,256]{3,2,1,0:T(8,128)S(1)}, f32[16,6,3,2,8,128]{5,4,3,2,1,0:T(8,128)S(1)}, f32[15,3,7,2,8,128]{5,4,3,2,1,0:T(8,128)S(1)}) custom-call(f32[3,16,8,256]{3,2,1,0:T(8,128)S(1)} %get-tuple-element.25.u_ref, f32[3,16,8,256]{3,2,1,0:T(8,128)S(1)} %get-tuple-element.26.v_ref, f32[6,16,8,256]{3,2,1,0:T(8,128)S(1)} %get-tuple-element.27.stress_ref, ...), custom_call_target="tpu_custom_call" | custom-call | tf_op jit(solution)/shard_map/pallas_call | solution.py:35
  26.7 0.3 shard_map.103.outer_ref
  27.0 3.5 %all-to-all-done.1.table_ref = f32[8,8,128]{2,1,0:T(8,128)S(1)} async-done(((f32[8,8,128]{2,1,0:T(8,128)}), f32[8,8,128]{2,1,0:T(8,128)S(1)}, u32[]{:S(2)}, u32[]{:S(2)}) %all-to-all-start.1) | async-done | bytes 32800 | tf_op jit(solution)/shard_map/all_to_all | solution.py:22
  30.5 0.0 collective-permute-done.4.left_ref
  30.5 1.0 %shard_map.107 = f32[3,16,8,256]{3,2,1,0:T(8,128)} custom-call(f32[3,16,8,256]{3,2,1,0:T(8,128)S(1)} %get-tuple-element.31.base_ref, f32[3,2,8,256]{3,2,1,0:T(8,128)S(1)} %shard_map.103.outer_ref, f32[16,8,256]{2,1,0:T(8,128)S(1)} %get-tuple-element.29.mass_ref, f32[8,8,128]{2,1,0:T(8,128)S(1)} %all-to-all-done.1.table_ref, ...), custom_call_target="tpu_custom_call" | custom-call | tf_op jit(solution)/shard_map/pallas_call | solution.py:35
  (1 shorter events, 0.0 us)
Async XLA Ops:
  2.0 10.4 %collective-permute-start.2 = (f32[104,256]{1,0:T(8,128)S(1)}, f32[104,256]{1,0:T(8,128)S(1)}, u32[]{:S(2)}, u32[]{:S(2)}) collective-permute-start(f32[104,256]{1,0:T(8,128)S(1)} %get-tuple-element.35), channel_id=1, source_target_pairs={{0,4},{4,8},{8,12},{12,16},{16,20},{20,24},{24,28},{28,0},{1,5},{5... | collective-permute-start | bytes 319496 | tf_op jit(solution)/shard_map/ppermute | solution.py:18
  5.1 18.8 %collective-permute-start = (f32[6,16,256]{2,1,0:T(8,128)S(1)}, f32[6,16,256]{2,1,0:T(8,128)S(1)}, u32[]{:S(2)}, u32[]{:S(2)}) collective-permute-start(f32[6,16,256]{2,1,0:T(8,128)S(1)} %get-tuple-element.30), channel_id=1, source_target_pairs={{0,3},{1,0},{2,1},{3,2},{4,7},{5,4},{6,5},{7,6},{8,11},{9,8},{10,9... | collective-permute-start | bytes 294920 | tf_op jit(solution)/shard_map/ppermute | solution.py:18
  5.7 6.7 %collective-permute-start.1 = (f32[48,256]{1,0:T(8,128)S(1)}, f32[48,256]{1,0:T(8,128)S(1)}, u32[]{:S(2)}, u32[]{:S(2)}) collective-permute-start(f32[48,256]{1,0:T(8,128)S(1)} %get-tuple-element.34), channel_id=1, source_target_pairs={{0,28},{4,0},{8,4},{12,8},{16,12},{20,16},{24,20},{28,24},{1,29},{... | collective-permute-start | bytes 147464 | tf_op jit(solution)/shard_map/ppermute | solution.py:18
  9.1 10.0 %all-to-all-start = ((f32[8,8,128]{2,1,0:T(8,128)}), f32[8,8,128]{2,1,0:T(8,128)S(1)}, u32[]{:S(2)}, u32[]{:S(2)}) async-start(f32[8,8,128]{2,1,0:T(8,128)} %get-tuple-element.36), calls=%async_computation | async-start | bytes 65536 | tf_op jit(solution)/shard_map/all_to_all | solution.py:22
  12.5 11.4 %collective-permute-start.3 = (f32[16,256]{1,0:T(8,128)S(1)}, f32[16,256]{1,0:T(8,128)S(1)}, u32[]{:S(2)}, u32[]{:S(2)}) collective-permute-start(f32[16,256]{1,0:T(8,128)S(1)} %shard_map.102), channel_id=1, source_target_pairs={{0,3},{1,0},{2,1},{3,2},{4,7},{5,4},{6,5},{7,6},{8,11},{9,8},{10,9... | collective-permute-start | bytes 49160 | tf_op jit(solution)/shard_map/ppermute | solution.py:18
  20.5 10.0 %all-to-all-start.1 = ((f32[8,8,128]{2,1,0:T(8,128)}), f32[8,8,128]{2,1,0:T(8,128)S(1)}, u32[]{:S(2)}, u32[]{:S(2)}) async-start(f32[8,8,128]{2,1,0:T(8,128)} %shard_map.105), calls=%async_computation.1 | async-start | bytes 65536 | tf_op jit(solution)/shard_map/all_to_all | solution.py:22
  24.3 6.1 %collective-permute-start.4 = (f32[3,16,256]{2,1,0:T(8,128)S(1)}, f32[3,16,256]{2,1,0:T(8,128)S(1)}, u32[]{:S(2)}, u32[]{:S(2)}) collective-permute-start(f32[3,16,256]{2,1,0:T(8,128)S(1)} %shard_map.106), channel_id=1, source_target_pairs={{0,1},{1,2},{2,3},{3,0},{4,5},{5,6},{6,7},{7,4},{8,9},{9,10},{10,1... | collective-permute-start | bytes 147464 | tf_op jit(solution)/shard_map/ppermute | solution.py:18

commit v4 on v3

--- a/solution.py
+++ b/solution.py
@@ -157,58 +157,69 @@
         out_ref[8 + c : 9 + c, :] = xu[c * columns : c * columns + 1, :]
 
 
-def matrix_body(nodes_ref, diag_ref, matrix_ref, lines_ref, diag_lines_ref):
-    pairs = nodes_ref.shape[1]
+def matrix_body(nodes_ref, diag_ref, matrix_ref, lines_ref, diag_lines_ref, square_ref, column_ref):
+    pairs, slots = matrix_ref.shape
     group = 16
-
-    def rows(g, carry):
-        start = pl.multiple_of(g * group, group)
-        slot = lax.broadcasted_iota(jnp.int32, (group, pairs), 0) + start
-        total = jnp.where(nodes_ref[0:1, :] == slot, 1.0, 0.0)
-        for j in range(1, 5):
-            total = total - jnp.where(nodes_ref[j : j + 1, :] == slot, 0.25, 0.0)
-        matrix_ref[pl.ds(start, group), :] = total.astype(jnp.bfloat16)
-        return carry
-
-    lax.fori_loop(0, matrix_ref.shape[0] // group, rows, 0)
+    square_ref[...] = jnp.zeros(square_ref.shape, jnp.int32)
     for r in range(pairs // LANES):
+        chunk = nodes_ref[:, r * LANES : (r + 1) * LANES]
         for j in range(5):
-            lines_ref[j, r : r + 1, :] = nodes_ref[j : j + 1, r * LANES : (r + 1) * LANES]
+            lines_ref[j, r : r + 1, :] = chunk[j : j + 1]
+        square_ref[0:5, :] = chunk
+        column_ref[r * LANES : (r + 1) * LANES, :] = square_ref[...].T
         for c in range(6):
             diag_lines_ref[c, r : r + 1, :] = diag_ref[c : c + 1, r * LANES : (r + 1) * LANES]
 
-
-def looked_up(table_ref, slots, capacity, offset, count):
+    def rows(start):
+        columns = column_ref[pl.ds(start, group), :]
+        slot = lax.broadcasted_iota(jnp.int32, (group, slots), 1)
+        total = jnp.where(columns[:, 0:1] == slot, 1.0, 0.0)
+        for j in range(1, 5):
+            total = total - jnp.where(columns[:, j : j + 1] == slot, 0.25, 0.0)
+        matrix_ref[pl.ds(start, group), :] = total.astype(jnp.bfloat16)
+
+    steps(0, pairs // group, 4, lambda g: rows(pl.multiple_of(g * group, group)))
+
+
+def dense_rows(table_ref, rows_ref, capacity, pack, offset):
+    together = LANES // capacity
+    lane = lax.broadcasted_iota(jnp.int32, (8, LANES), 1)
+    for b in range(rows_ref.shape[0]):
+        total = None
+        for q in range(min(together, table_ref.shape[0] - b * together)):
+            tile = table_ref[b * together + q]
+            if pack > 1:
+                tile = jnp.where((lane >= offset) & (lane < offset + capacity), tile, 0.0)
+                tile = pltpu.roll(tile, (q * capacity - offset) & (LANES - 1), 1)
+            elif q:
+                tile = pltpu.roll(tile, q * capacity, 1)
+            total = tile if total is None else total + tile
+        rows_ref[b] = total
+    return together * capacity
+
+
+def looked_up(rows_ref, slots, width):
     shape = slots[0].shape
-
-    def step(s, found):
-        shift = s * capacity - offset
-        result = []
+    found = [[None] * 3 for _ in slots]
+    for b in range(rows_ref.shape[0]):
+        rows = [jnp.broadcast_to(rows_ref[b, c : c + 1, :], shape) for c in range(3)]
         for slot, old in zip(slots, found):
-            here = (slot >= s * capacity) & (slot < (s + 1) * capacity)
-            index = (slot - shift) & (LANES - 1)
-            new = []
+            place = slot - b * width
+            here = place >= 0
             for c in range(3):
-                row = jnp.broadcast_to(table_ref[s, c : c + 1, :], shape)
-                new.append(jnp.where(here, jnp.take_along_axis(row, index, axis=1), old[c]))
-            result.append(tuple(new))
-        return tuple(result)
-
-    zero = jnp.zeros(shape, jnp.float32)
-    found = tuple((zero, zero, zero) for _ in slots)
-    if count <= 16:
-        for s in range(count):
-            found = step(s, found)
-        return found
-    return lax.fori_loop(0, count, step, found)
+                new = jnp.take_along_axis(rows[c], place & (LANES - 1), axis=1)
+                old[c] = jnp.where(here, new, old[c]) if b else new
+    return found
 
 
 def pair_body(
-    nspace, capacity, pack, blocks,
-    table_ref, nodes_ref, diag_ref, gap_ref, stiff_ref, matrix_ref, out_hbm, rows_ref, out_ref, sem,
+    capacity, pack, blocks,
+    table_ref, nodes_ref, diag_ref, gap_ref, stiff_ref, matrix_ref,
+    out_hbm, rows_ref, out_ref, dense_ref, sem,
 ):
     offset = (lax.axis_index("space") % pack) * capacity
-    picked = looked_up(table_ref, [nodes_ref[j] for j in range(5)], capacity, offset, nspace)
+    dense = dense_rows(table_ref, dense_ref, capacity, pack, offset)
+    picked = looked_up(dense_ref, [nodes_ref[j] for j in range(5)], dense)
     slave = picked[0]
     first = [diag_ref[c] + picked[3][c] - picked[1][c] for c in range(3)]
     second = [diag_ref[3 + c] + picked[4][c] - picked[2][c] for c in range(3)]
@@ -228,7 +239,9 @@
         for r in range(force.shape[0]):
             rows_ref[c : c + 1, r * LANES : (r + 1) * LANES] = force[r : r + 1]
     parts = [part.astype(jnp.bfloat16) for part in parts_of(rows_ref[...])]
-    got = contract_lanes(jnp.concatenate(parts, 0), matrix_ref[...])
+    got = jnp.dot(
+        jnp.concatenate(parts, 0), matrix_ref[...], preferred_element_type=jnp.float32
+    )
     total = got[0:8] + got[8:16] + got[16:24]
     width = pack * capacity
     for b in range(blocks):
@@ -406,7 +419,7 @@
 
     lax.fori_loop(0, count, several, 0)
     for i in range(start + count * unroll, stop):
-        body(i)
+        body(jnp.int32(i))
 
 
 def inner_body(
@@ -497,12 +510,14 @@
 
 
 def final_body(
-    nspace, capacity, pack,
-    base_ref, outer_ref, mass_ref, table_ref, route_ref, left_ref, out_hbm, rows_ref, out_ref, sems,
+    capacity, pack,
+    base_ref, outer_ref, mass_ref, table_ref, route_ref, left_ref,
+    out_hbm, rows_ref, out_ref, dense_ref, sems,
 ):
     planes, columns, depth = base_ref.shape[1:]
     offset = (lax.axis_index("space") % pack) * capacity
-    (contact,) = looked_up(table_ref, [route_ref[...]], capacity, offset, nspace)
+    dense = dense_rows(table_ref, dense_ref, capacity, pack, offset)
+    (contact,) = looked_up(dense_ref, [route_ref[...]], dense)
     rows_ref[...] = jnp.zeros(rows_ref.shape, jnp.float32)
     lane = lax.broadcasted_iota(jnp.int32, (planes, columns, LANES), 2)
     row = lax.broadcasted_iota(jnp.int32, (columns, LANES), 0)
@@ -592,23 +607,26 @@
     yu = shifted(ydn, "slab", -1)
     xu = shifted(xdn, "space", -1)
     xd = shifted(xup, "space", 1)
-    slots = (nspace * capacity + 15) // 16 * 16
+    slots = nspace * capacity
     matrix, nodes, diagonals = kernel_call(
         matrix_body,
         (pair_nodes, pair_diagonals),
         (
-            jax.ShapeDtypeStruct((slots, pairs), jnp.bfloat16),
+            jax.ShapeDtypeStruct((pairs, slots), jnp.bfloat16),
             jax.ShapeDtypeStruct((5, lines, LANES), jnp.int32),
             sized(6, lines, LANES),
         ),
-    )
+        [pltpu.VMEM((LANES, LANES), jnp.int32), pltpu.VMEM((pairs, LANES), jnp.int32)],
+    )
+    dense = pltpu.VMEM((pl.cdiv(nspace, LANES // capacity), 8, LANES), f32)
     slot_force = kernel_call(
-        functools.partial(pair_body, nspace, capacity, pack, blocks),
+        functools.partial(pair_body, capacity, pack, blocks),
         (received, nodes, diagonals, gap, stiffness, matrix),
         pltpu.HBM(message.shape, f32),
         [
             pltpu.VMEM((8, pairs), f32),
             pltpu.VMEM(message.shape, f32),
+            dense,
             pltpu.SemaphoreType.DMA,
         ],
     )
@@ -643,12 +661,13 @@
     )
 
     return kernel_call(
-        functools.partial(final_body, nspace, capacity, pack),
+        functools.partial(final_body, capacity, pack),
         (base, outer, fields[4], returned, sides, left),
         pltpu.HBM(displacement.shape, f32),
         [
             pltpu.VMEM((3, LANES, LANES), f32),
             pltpu.VMEM(displacement.shape, f32),
+            dense,
             pltpu.SemaphoreType.DMA((3,)),
         ],
     )

time: 31.7 us -> 31.6 us (level)
  waiting for transfers between devices: 8.49 us -> 7.17 us
  Pallas kernels: 8.51 us -> 9.7 us
    all_to_all x2, waiting for transfers between devices: 8.48 us -> 7.15 us  [exchanged(): lax.all_to_all(value, 'space', split_axis=0, concat_axis=0, tiled=True)]
    pallas_call x8, Pallas kernels: 8.51 us -> 9.7 us  [kernel_call(): pl.pallas_call(body, out_shape=outs, in_specs=[pl.BlockSpec(memory_space=...]
  transfers between devices with their start and end apart: 7 -> 7, of which waited for: 2 -> 2; matrix products, arithmetic and copies ran while one was open for 0% -> 0% of each run, Pallas kernels for 17% -> 21%
where the time goes in v4:
time: 31.6 us; the launch traced here: 31.3 us
  starting transfers between devices  14.4 us (46%)
  Pallas kernels  9.7 us (31%)
  waiting for transfers between devices  7.17 us (23%)
    pallas_call x8, Pallas kernels, kernel_call(): pl.pallas_call(body, out_shape=outs, in_specs=[pl.BlockSpec(memory_space=...  9.7 us
    ppermute x5, starting transfers between devices, shifted(): lax.ppermute(value, axis, [(at, (at + steps) % count) for at in range(cou...  7.67 us
    all_to_all x2, waiting for transfers between devices, exchanged(): lax.all_to_all(value, 'space', split_axis=0, concat_axis=0, tiled=True)  7.15 us
    all_to_all x2, starting transfers between devices, exchanged(): lax.all_to_all(value, 'space', split_axis=0, concat_axis=0, tiled=True)  6.7 us
  transfers between devices with their start and end apart: 7, of which 2 were waited for; matrix products, arithmetic and copies ran while one was open for 0% of the time, Pallas kernels for 21%

profile of v4, /device:TPU:0, one launch (start us, length us, event | category | flops | bytes accessed | tf_op | source)
XLA Modules:
  0.0 31.3 jit_solution(6929625141726240299)
XLA Ops:
  0.0 2.0 %shard_map.100 = (f32[8,8,128]{2,1,0:T(8,128)}, f32[6,16,256]{2,1,0:T(8,128)S(1)}, f32[48,256]{1,0:T(8,128)S(1)}, f32[104,256]{1,0:T(8,128)S(1)}, s32[2,128]{1,0...) custom-call(f32[3,16,8,256]{3,2,1,0:T(8,128)} %u_hbm.1, ...), custom_call_target="tpu_custom_call" | custom-call | tf_op jit(solution)/shard_map/pallas_call | solution.py:35
  2.0 3.0 %collective-permute-start.2 = (f32[104,256]{1,0:T(8,128)S(1)}, f32[104,256]{1,0:T(8,128)S(1)}, u32[]{:S(2)}, u32[]{:S(2)}) collective-permute-start(f32[104,256]{1,0:T(8,128)S(1)} %get-tuple-element.35), channel_id=1, source_target_pairs={{0,4},{4,8},{8,12},{12,16},{16,20},{20,24},{24,28},{28,0},{1,5},{5... | collective-permute-start | bytes 319496 | tf_op jit(solution)/shard_map/ppermute | solution.py:18
  5.1 0.7 %collective-permute-start = (f32[6,16,256]{2,1,0:T(8,128)S(1)}, f32[6,16,256]{2,1,0:T(8,128)S(1)}, u32[]{:S(2)}, u32[]{:S(2)}) collective-permute-start(f32[6,16,256]{2,1,0:T(8,128)S(1)} %get-tuple-element.30), channel_id=1, source_target_pairs={{0,3},{1,0},{2,1},{3,2},{4,7},{5,4},{6,5},{7,6},{8,11},{9,8},{10,9... | collective-permute-start | bytes 294920 | tf_op jit(solution)/shard_map/ppermute | solution.py:18
  5.7 3.4 %collective-permute-start.1 = (f32[48,256]{1,0:T(8,128)S(1)}, f32[48,256]{1,0:T(8,128)S(1)}, u32[]{:S(2)}, u32[]{:S(2)}) collective-permute-start(f32[48,256]{1,0:T(8,128)S(1)} %get-tuple-element.34), channel_id=1, source_target_pairs={{0,28},{4,0},{8,4},{12,8},{16,12},{20,16},{24,20},{28,24},{1,29},{... | collective-permute-start | bytes 147464 | tf_op jit(solution)/shard_map/ppermute | solution.py:18
  9.1 3.3 %all-to-all-start = ((f32[8,8,128]{2,1,0:T(8,128)}), f32[8,8,128]{2,1,0:T(8,128)S(1)}, u32[]{:S(2)}, u32[]{:S(2)}) async-start(f32[8,8,128]{2,1,0:T(8,128)} %get-tuple-element.36), calls=%async_computation | async-start | bytes 65536 | tf_op jit(solution)/shard_map/all_to_all | solution.py:22
  12.5 0.0 collective-permute-done.1.xu
  12.5 0.0 collective-permute-done.2.xd
  12.5 0.5 %collective-permute-start.3 = (f32[16,256]{1,0:T(8,128)S(1)}, f32[16,256]{1,0:T(8,128)S(1)}, u32[]{:S(2)}, u32[]{:S(2)}) collective-permute-start(f32[16,256]{1,0:T(8,128)S(1)} %shard_map.102), channel_id=1, source_target_pairs={{0,3},{1,0},{2,1},{3,2},{4,7},{5,4},{6,5},{7,6},{8,11},{9,8},{10,9... | collective-permute-start | bytes 49160 | tf_op jit(solution)/shard_map/ppermute | solution.py:18
  13.0 2.4 %shard_map.104 = (bf16[1024,384]{1,0:T(8,128)(2,1)S(1)}, s32[5,8,128]{2,1,0:T(8,128)S(1)}, f32[6,8,128]{2,1,0:T(8,128)S(1)}) custom-call(s32[5,1024]{1,0:T(8,128)S(1)} %get-tuple-element.37.nodes_ref, f32[6,1024]{1,0:T(8,128)S(1)} %get-tuple-element.38.diag_ref), custom_call_target="tpu_custom_call" | custom-call | tf_op jit(solution)/shard_map/pallas_call | solution.py:35
  15.4 3.7 %all-to-all-done.table_ref = f32[8,8,128]{2,1,0:T(8,128)S(1)} async-done(((f32[8,8,128]{2,1,0:T(8,128)}), f32[8,8,128]{2,1,0:T(8,128)S(1)}, u32[]{:S(2)}, u32[]{:S(2)}) %all-to-all-start) | async-done | bytes 32800 | tf_op jit(solution)/shard_map/all_to_all | solution.py:22
  19.1 1.2 %shard_map.105 = f32[8,8,128]{2,1,0:T(8,128)} custom-call(f32[8,8,128]{2,1,0:T(8,128)S(1)} %all-to-all-done.table_ref, s32[5,8,128]{2,1,0:T(8,128)S(1)} %get-tuple-element.39.nodes_ref, f32[6,8,128]{2,1,0:T(8,128)S(1)} %get-tuple-element.40.diag_ref, f32[8,128]{1,0:T(8,128)S(1)} %get-tuple-element.41.gap_ref, f32[8,128]{1,0:T(8,128)S(1)} %get-tuple-element.42.stiff_ref, ...), custom_call_target="tpu_custom_call" | custom-call | tf_op jit(solution)/shard_map/pallas_call | solution.py:35
  20.3 3.4 %all-to-all-start.1 = ((f32[8,8,128]{2,1,0:T(8,128)}), f32[8,8,128]{2,1,0:T(8,128)S(1)}, u32[]{:S(2)}, u32[]{:S(2)}) async-start(f32[8,8,128]{2,1,0:T(8,128)} %shard_map.105), calls=%async_computation.1 | async-start | bytes 65536 | tf_op jit(solution)/shard_map/all_to_all | solution.py:22
  23.7 0.0 collective-permute-done.yu
  23.7 0.0 collective-permute-done.3.corner
  23.7 0.5 %shard_map.106 = f32[3,16,256]{2,1,0:T(8,128)S(1)} custom-call(f32[3,16,8,256]{3,2,1,0:T(8,128)S(1)} %get-tuple-element.25.u_ref, f32[3,16,8,256]{3,2,1,0:T(8,128)S(1)} %get-tuple-element.26.v_ref, f32[6,16,8,256]{3,2,1,0:T(8,128)S(1)} %get-tuple-element.27.stress_ref, f32[16,8,256]{2,1,0:T(8,128)S(1)} %get-tuple-element.28.hour_ref, ...), custom_call_target="tpu_custom_call" | custom-call | tf_op jit(solution)/shard_map/pallas_call | solution.py:35
  24.2 0.0 collective-permute-start.4
  24.2 2.3 %shard_map.101 = (f32[3,16,8,256]{3,2,1,0:T(8,128)S(1)}, f32[16,6,3,2,8,128]{5,4,3,2,1,0:T(8,128)S(1)}, f32[15,3,7,2,8,128]{5,4,3,2,1,0:T(8,128)S(1)}) custom-call(f32[3,16,8,256]{3,2,1,0:T(8,128)S(1)} %get-tuple-element.25.u_ref, f32[3,16,8,256]{3,2,1,0:T(8,128)S(1)} %get-tuple-element.26.v_ref, f32[6,16,8,256]{3,2,1,0:T(8,128)S(1)} %get-tuple-element.27.stress_ref, ...), custom_call_target="tpu_custom_call" | custom-call | tf_op jit(solution)/shard_map/pallas_call | solution.py:35
  26.5 0.3 shard_map.103.outer_ref
  26.8 3.5 %all-to-all-done.1.table_ref = f32[8,8,128]{2,1,0:T(8,128)S(1)} async-done(((f32[8,8,128]{2,1,0:T(8,128)}), f32[8,8,128]{2,1,0:T(8,128)S(1)}, u32[]{:S(2)}, u32[]{:S(2)}) %all-to-all-start.1) | async-done | bytes 32800 | tf_op jit(solution)/shard_map/all_to_all | solution.py:22
  30.3 0.0 collective-permute-done.4.left_ref
  30.3 1.0 %shard_map.107 = f32[3,16,8,256]{3,2,1,0:T(8,128)} custom-call(f32[3,16,8,256]{3,2,1,0:T(8,128)S(1)} %get-tuple-element.31.base_ref, f32[3,2,8,256]{3,2,1,0:T(8,128)S(1)} %shard_map.103.outer_ref, f32[16,8,256]{2,1,0:T(8,128)S(1)} %get-tuple-element.29.mass_ref, f32[8,8,128]{2,1,0:T(8,128)S(1)} %all-to-all-done.1.table_ref, ...), custom_call_target="tpu_custom_call" | custom-call | tf_op jit(solution)/shard_map/pallas_call | solution.py:35
  (1 shorter events, 0.0 us)
Async XLA Ops:
  2.0 10.4 %collective-permute-start.2 = (f32[104,256]{1,0:T(8,128)S(1)}, f32[104,256]{1,0:T(8,128)S(1)}, u32[]{:S(2)}, u32[]{:S(2)}) collective-permute-start(f32[104,256]{1,0:T(8,128)S(1)} %get-tuple-element.35), channel_id=1, source_target_pairs={{0,4},{4,8},{8,12},{12,16},{16,20},{20,24},{24,28},{28,0},{1,5},{5... | collective-permute-start | bytes 319496 | tf_op jit(solution)/shard_map/ppermute | solution.py:18
  5.1 18.6 %collective-permute-start = (f32[6,16,256]{2,1,0:T(8,128)S(1)}, f32[6,16,256]{2,1,0:T(8,128)S(1)}, u32[]{:S(2)}, u32[]{:S(2)}) collective-permute-start(f32[6,16,256]{2,1,0:T(8,128)S(1)} %get-tuple-element.30), channel_id=1, source_target_pairs={{0,3},{1,0},{2,1},{3,2},{4,7},{5,4},{6,5},{7,6},{8,11},{9,8},{10,9... | collective-permute-start | bytes 294920 | tf_op jit(solution)/shard_map/ppermute | solution.py:18
  5.7 6.7 %collective-permute-start.1 = (f32[48,256]{1,0:T(8,128)S(1)}, f32[48,256]{1,0:T(8,128)S(1)}, u32[]{:S(2)}, u32[]{:S(2)}) collective-permute-start(f32[48,256]{1,0:T(8,128)S(1)} %get-tuple-element.34), channel_id=1, source_target_pairs={{0,28},{4,0},{8,4},{12,8},{16,12},{20,16},{24,20},{28,24},{1,29},{... | collective-permute-start | bytes 147464 | tf_op jit(solution)/shard_map/ppermute | solution.py:18
  9.1 10.0 %all-to-all-start = ((f32[8,8,128]{2,1,0:T(8,128)}), f32[8,8,128]{2,1,0:T(8,128)S(1)}, u32[]{:S(2)}, u32[]{:S(2)}) async-start(f32[8,8,128]{2,1,0:T(8,128)} %get-tuple-element.36), calls=%async_computation | async-start | bytes 65536 | tf_op jit(solution)/shard_map/all_to_all | solution.py:22
  12.5 11.2 %collective-permute-start.3 = (f32[16,256]{1,0:T(8,128)S(1)}, f32[16,256]{1,0:T(8,128)S(1)}, u32[]{:S(2)}, u32[]{:S(2)}) collective-permute-start(f32[16,256]{1,0:T(8,128)S(1)} %shard_map.102), channel_id=1, source_target_pairs={{0,3},{1,0},{2,1},{3,2},{4,7},{5,4},{6,5},{7,6},{8,11},{9,8},{10,9... | collective-permute-start | bytes 49160 | tf_op jit(solution)/shard_map/ppermute | solution.py:18
  20.3 10.0 %all-to-all-start.1 = ((f32[8,8,128]{2,1,0:T(8,128)}), f32[8,8,128]{2,1,0:T(8,128)S(1)}, u32[]{:S(2)}, u32[]{:S(2)}) async-start(f32[8,8,128]{2,1,0:T(8,128)} %shard_map.105), calls=%async_computation.1 | async-start | bytes 65536 | tf_op jit(solution)/shard_map/all_to_all | solution.py:22
  24.2 6.1 %collective-permute-start.4 = (f32[3,16,256]{2,1,0:T(8,128)S(1)}, f32[3,16,256]{2,1,0:T(8,128)S(1)}, u32[]{:S(2)}, u32[]{:S(2)}) collective-permute-start(f32[3,16,256]{2,1,0:T(8,128)S(1)} %shard_map.106), channel_id=1, source_target_pairs={{0,1},{1,2},{2,3},{3,0},{4,5},{5,6},{6,7},{7,4},{8,9},{9,10},{10,1... | collective-permute-start | bytes 147464 | tf_op jit(solution)/shard_map/ppermute | solution.py:18

commit v5 on v4

--- a/solution.py
+++ b/solution.py
@@ -157,28 +157,25 @@
         out_ref[8 + c : 9 + c, :] = xu[c * columns : c * columns + 1, :]
 
 
-def matrix_body(nodes_ref, diag_ref, matrix_ref, lines_ref, diag_lines_ref, square_ref, column_ref):
-    pairs, slots = matrix_ref.shape
+def matrix_body(nodes_ref, diag_ref, matrix_ref, lines_ref, diag_lines_ref):
+    pairs = nodes_ref.shape[1]
     group = 16
-    square_ref[...] = jnp.zeros(square_ref.shape, jnp.int32)
+
+    def rows(g, carry):
+        start = pl.multiple_of(g * group, group)
+        slot = lax.broadcasted_iota(jnp.int32, (group, pairs), 0) + start
+        total = jnp.where(nodes_ref[0:1, :] == slot, 1.0, 0.0)
+        for j in range(1, 5):
+            total = total - jnp.where(nodes_ref[j : j + 1, :] == slot, 0.25, 0.0)
+        matrix_ref[pl.ds(start, group), :] = total.astype(jnp.bfloat16)
+        return carry
+
+    lax.fori_loop(0, matrix_ref.shape[0] // group, rows, 0)
     for r in range(pairs // LANES):
-        chunk = nodes_ref[:, r * LANES : (r + 1) * LANES]
         for j in range(5):
-            lines_ref[j, r : r + 1, :] = chunk[j : j + 1]
-        square_ref[0:5, :] = chunk
-        column_ref[r * LANES : (r + 1) * LANES, :] = square_ref[...].T
+            lines_ref[j, r : r + 1, :] = nodes_ref[j : j + 1, r * LANES : (r + 1) * LANES]
         for c in range(6):
             diag_lines_ref[c, r : r + 1, :] = diag_ref[c : c + 1, r * LANES : (r + 1) * LANES]
-
-    def rows(start):
-        columns = column_ref[pl.ds(start, group), :]
-        slot = lax.broadcasted_iota(jnp.int32, (group, slots), 1)
-        total = jnp.where(columns[:, 0:1] == slot, 1.0, 0.0)
-        for j in range(1, 5):
-            total = total - jnp.where(columns[:, j : j + 1] == slot, 0.25, 0.0)
-        matrix_ref[pl.ds(start, group), :] = total.astype(jnp.bfloat16)
-
-    steps(0, pairs // group, 4, lambda g: rows(pl.multiple_of(g * group, group)))
 
 
 def dense_rows(table_ref, rows_ref, capacity, pack, offset):
@@ -239,9 +236,7 @@
         for r in range(force.shape[0]):
             rows_ref[c : c + 1, r * LANES : (r + 1) * LANES] = force[r : r + 1]
     parts = [part.astype(jnp.bfloat16) for part in parts_of(rows_ref[...])]
-    got = jnp.dot(
-        jnp.concatenate(parts, 0), matrix_ref[...], preferred_element_type=jnp.float32
-    )
+    got = contract_lanes(jnp.concatenate(parts, 0), matrix_ref[...])
     total = got[0:8] + got[8:16] + got[16:24]
     width = pack * capacity
     for b in range(blocks):
@@ -423,10 +418,9 @@
 
 
 def inner_body(
-    unroll, u_ref, v_ref, stress_ref, hour_ref, mass_ref, yu, out_ref, node_ref, elem_ref, halo_s, halo_d
+    unroll, u_ref, v_ref, stress_ref, hour_ref, yu, node_ref, elem_ref, halo_s, halo_d
 ):
-    planes, _, depth = u_ref.shape[1:]
-    nb = depth // LANES
+    planes = u_ref.shape[1]
     for c in range(6):
         halo_s[c], halo_d[c] = z_pair(split(yu[c]))
 
@@ -452,27 +446,25 @@
             for t in range(7):
                 elem_ref[i, m, t] = factors[m][t]
 
-    def forces(i):
-        result = new_velocity(
-            kept_elements(elem_ref, i - 1),
-            kept_elements(elem_ref, i),
-            [split(v_ref[m, i]) for m in range(3)],
-            split(mass_ref[i]),
-        )
-        for m in range(3):
-            for k in range(nb):
-                out_ref[m, i, :, k * LANES : (k + 1) * LANES] = result[m][k]
-
     steps(0, planes, unroll, nodes)
     steps(0, planes - 1, unroll, elements)
-    steps(1, planes - 1, unroll, forces)
 
 
 def outer_body(
-    v_ref, stress_ref, hour_ref, mass_ref, node_ref, elem_ref, xu, xd, corner, out_ref
+    unroll, v_ref, stress_ref, hour_ref, mass_ref, node_ref, elem_ref, xu, xd, corner, out_ref
 ):
     planes, columns, depth = v_ref.shape[1:]
     last = planes - 1
+
+    def write_plane(i, before, after):
+        velocity = [split(v_ref[m, i]) for m in range(3)]
+        result = new_velocity(before, after, velocity, split(mass_ref[i]))
+        for m in range(3):
+            for k in range(depth // LANES):
+                out_ref[m, i, :, k * LANES : (k + 1) * LANES] = result[m][k]
+
+    def inside(i):
+        write_plane(i, kept_elements(elem_ref, i - 1), kept_elements(elem_ref, i))
 
     def part(ref, c):
         return split(ref[c * columns : (c + 1) * columns, :])
@@ -497,21 +489,14 @@
         [split(stress_ref[c, last]) for c in range(6)],
         split(hour_ref[last]),
     )
-    ends = (
-        (0, below, kept_elements(elem_ref, 0)),
-        (last, kept_elements(elem_ref, last - 1), above),
-    )
-    for at, (i, before, after) in enumerate(ends):
-        velocity = [split(v_ref[m, i]) for m in range(3)]
-        result = new_velocity(before, after, velocity, split(mass_ref[i]))
-        for m in range(3):
-            for k in range(depth // LANES):
-                out_ref[m, at, :, k * LANES : (k + 1) * LANES] = result[m][k]
+    write_plane(0, below, kept_elements(elem_ref, 0))
+    write_plane(last, kept_elements(elem_ref, last - 1), above)
+    steps(1, last, unroll, inside)
 
 
 def final_body(
     capacity, pack,
-    base_ref, outer_ref, mass_ref, table_ref, route_ref, left_ref,
+    base_ref, mass_ref, table_ref, route_ref, left_ref,
     out_hbm, rows_ref, out_ref, dense_ref, sems,
 ):
     planes, columns, depth = base_ref.shape[1:]
@@ -536,14 +521,7 @@
                     for i in range(planes)
                 ]
             )
-            value = jnp.concatenate(
-                [
-                    outer_ref[m, 0:1, :, k : k + LANES],
-                    base_ref[m, 1 : planes - 1, :, k : k + LANES],
-                    outer_ref[m, 1:2, :, k : k + LANES],
-                ]
-            )
-            value = value - left * weights[k // LANES]
+            value = base_ref[m, :, :, k : k + LANES] - left * weights[k // LANES]
             if k == 0:
                 value = value + low_weight * turned
             if k == depth - LANES:
@@ -607,16 +585,15 @@
     yu = shifted(ydn, "slab", -1)
     xu = shifted(xdn, "space", -1)
     xd = shifted(xup, "space", 1)
-    slots = nspace * capacity
+    slots = (nspace * capacity + 15) // 16 * 16
     matrix, nodes, diagonals = kernel_call(
         matrix_body,
         (pair_nodes, pair_diagonals),
         (
-            jax.ShapeDtypeStruct((pairs, slots), jnp.bfloat16),
+            jax.ShapeDtypeStruct((slots, pairs), jnp.bfloat16),
             jax.ShapeDtypeStruct((5, lines, LANES), jnp.int32),
             sized(6, lines, LANES),
         ),
-        [pltpu.VMEM((LANES, LANES), jnp.int32), pltpu.VMEM((pairs, LANES), jnp.int32)],
     )
     dense = pltpu.VMEM((pl.cdiv(nspace, LANES // capacity), 8, LANES), f32)
     slot_force = kernel_call(
@@ -635,11 +612,10 @@
     corner = kernel_call(functools.partial(corner_body, columns), (xu, xd), sized(16, depth))
     corner = shifted(corner, "slab", -1)
     nb = depth // LANES
-    base, node, elem = kernel_call(
+    node, elem = kernel_call(
         functools.partial(inner_body, 2),
-        (*fields, yu),
+        (*fields[:4], yu),
         (
-            sized(*displacement.shape),
             sized(planes, 6, 3, nb, columns, LANES),
             sized(planes - 1, 3, 7, nb, columns, LANES),
         ),
@@ -656,13 +632,15 @@
         [pltpu.VMEM((rows, depth), f32)],
     )
     left = shifted(beyond, "slab", 1)
-    outer = kernel_call(
-        outer_body, (*fields[1:], node, elem, xu, xd, corner), sized(3, 2, columns, depth)
+    base = kernel_call(
+        functools.partial(outer_body, 2),
+        (*fields[1:], node, elem, xu, xd, corner),
+        sized(*displacement.shape),
     )
 
     return kernel_call(
         functools.partial(final_body, capacity, pack),
-        (base, outer, fields[4], returned, sides, left),
+        (base, fields[4], returned, sides, left),
         pltpu.HBM(displacement.shape, f32),
         [
             pltpu.VMEM((3, LANES, LANES), f32),

time: 31.6 us -> 31.7 us (level)
  waiting for transfers between devices: 7.17 us -> 8.48 us
  Pallas kernels: 9.7 us -> 8.46 us
    all_to_all x2, waiting for transfers between devices: 7.15 us -> 8.47 us  [exchanged(): lax.all_to_all(value, 'space', split_axis=0, concat_axis=0, tiled=True)]
    pallas_call x8, Pallas kernels: 9.7 us -> 8.46 us  [kernel_call(): pl.pallas_call(body, out_shape=outs, in_specs=[pl.BlockSpec(memory_space=...]
  transfers between devices with their start and end apart: 7 -> 7, of which waited for: 2 -> 2; matrix products, arithmetic and copies ran while one was open for 0% -> 0% of each run, Pallas kernels for 21% -> 17%
where the time goes in v5:
time: 31.7 us; the launch traced here: 31.4 us
  starting transfers between devices  14.4 us (45%)
  waiting for transfers between devices  8.48 us (27%)
  Pallas kernels  8.46 us (27%)
    all_to_all x2, waiting for transfers between devices, exchanged(): lax.all_to_all(value, 'space', split_axis=0, concat_axis=0, tiled=True)  8.47 us
    pallas_call x8, Pallas kernels, kernel_call(): pl.pallas_call(body, out_shape=outs, in_specs=[pl.BlockSpec(memory_space=...  8.46 us
    ppermute x5, starting transfers between devices, shifted(): lax.ppermute(value, axis, [(at, (at + steps) % count) for at in range(cou...  7.67 us
    all_to_all x2, starting transfers between devices, exchanged(): lax.all_to_all(value, 'space', split_axis=0, concat_axis=0, tiled=True)  6.7 us
  transfers between devices with their start and end apart: 7, of which 2 were waited for; matrix products, arithmetic and copies ran while one was open for 0% of the time, Pallas kernels for 17%

profile of v5, /device:TPU:0, one launch (start us, length us, event | category | flops | bytes accessed | tf_op | source)
XLA Modules:
  0.0 31.4 jit_solution(3457074868603543144)
XLA Ops:
  0.0 2.0 %shard_map.100 = (f32[8,8,128]{2,1,0:T(8,128)}, f32[6,16,256]{2,1,0:T(8,128)S(1)}, f32[48,256]{1,0:T(8,128)S(1)}, f32[104,256]{1,0:T(8,128)S(1)}, s32[2,128]{1,0...) custom-call(f32[3,16,8,256]{3,2,1,0:T(8,128)} %u_hbm.1, ...), custom_call_target="tpu_custom_call" | custom-call | tf_op jit(solution)/shard_map/pallas_call | solution.py:35
  2.0 3.0 %collective-permute-start.2 = (f32[104,256]{1,0:T(8,128)S(1)}, f32[104,256]{1,0:T(8,128)S(1)}, u32[]{:S(2)}, u32[]{:S(2)}) collective-permute-start(f32[104,256]{1,0:T(8,128)S(1)} %get-tuple-element.33), channel_id=1, source_target_pairs={{0,4},{4,8},{8,12},{12,16},{16,20},{20,24},{24,28},{28,0},{1,5},{5... | collective-permute-start | bytes 319496 | tf_op jit(solution)/shard_map/ppermute | solution.py:18
  5.1 0.7 %collective-permute-start = (f32[6,16,256]{2,1,0:T(8,128)S(1)}, f32[6,16,256]{2,1,0:T(8,128)S(1)}, u32[]{:S(2)}, u32[]{:S(2)}) collective-permute-start(f32[6,16,256]{2,1,0:T(8,128)S(1)} %get-tuple-element.29), channel_id=1, source_target_pairs={{0,3},{1,0},{2,1},{3,2},{4,7},{5,4},{6,5},{7,6},{8,11},{9,8},{10,9... | collective-permute-start | bytes 294920 | tf_op jit(solution)/shard_map/ppermute | solution.py:18
  5.7 3.4 %collective-permute-start.1 = (f32[48,256]{1,0:T(8,128)S(1)}, f32[48,256]{1,0:T(8,128)S(1)}, u32[]{:S(2)}, u32[]{:S(2)}) collective-permute-start(f32[48,256]{1,0:T(8,128)S(1)} %get-tuple-element.32), channel_id=1, source_target_pairs={{0,28},{4,0},{8,4},{12,8},{16,12},{20,16},{24,20},{28,24},{1,29},{... | collective-permute-start | bytes 147464 | tf_op jit(solution)/shard_map/ppermute | solution.py:18
  9.1 3.3 %all-to-all-start = ((f32[8,8,128]{2,1,0:T(8,128)}), f32[8,8,128]{2,1,0:T(8,128)S(1)}, u32[]{:S(2)}, u32[]{:S(2)}) async-start(f32[8,8,128]{2,1,0:T(8,128)} %get-tuple-element.34), calls=%async_computation | async-start | bytes 65536 | tf_op jit(solution)/shard_map/all_to_all | solution.py:22
  12.5 0.0 collective-permute-done.1.xu
  12.5 0.0 collective-permute-done.2.xd
  12.5 0.5 %collective-permute-start.3 = (f32[16,256]{1,0:T(8,128)S(1)}, f32[16,256]{1,0:T(8,128)S(1)}, u32[]{:S(2)}, u32[]{:S(2)}) collective-permute-start(f32[16,256]{1,0:T(8,128)S(1)} %shard_map.102), channel_id=1, source_target_pairs={{0,3},{1,0},{2,1},{3,2},{4,7},{5,4},{6,5},{7,6},{8,11},{9,8},{10,9... | collective-permute-start | bytes 49160 | tf_op jit(solution)/shard_map/ppermute | solution.py:18
  13.0 1.0 %shard_map.104 = (bf16[384,1024]{1,0:T(8,128)(2,1)S(1)}, s32[5,8,128]{2,1,0:T(8,128)S(1)}, f32[6,8,128]{2,1,0:T(8,128)S(1)}) custom-call(s32[5,1024]{1,0:T(8,128)S(1)} %get-tuple-element.35.nodes_ref, f32[6,1024]{1,0:T(8,128)S(1)} %get-tuple-element.36.diag_ref), custom_call_target="tpu_custom_call" | custom-call | tf_op jit(solution)/shard_map/pallas_call | solution.py:35
  14.1 5.0 %all-to-all-done.table_ref = f32[8,8,128]{2,1,0:T(8,128)S(1)} async-done(((f32[8,8,128]{2,1,0:T(8,128)}), f32[8,8,128]{2,1,0:T(8,128)S(1)}, u32[]{:S(2)}, u32[]{:S(2)}) %all-to-all-start) | async-done | bytes 32800 | tf_op jit(solution)/shard_map/all_to_all | solution.py:22
  19.1 1.3 %shard_map.105 = f32[8,8,128]{2,1,0:T(8,128)} custom-call(f32[8,8,128]{2,1,0:T(8,128)S(1)} %all-to-all-done.table_ref, s32[5,8,128]{2,1,0:T(8,128)S(1)} %get-tuple-element.37.nodes_ref, f32[6,8,128]{2,1,0:T(8,128)S(1)} %get-tuple-element.38.diag_ref, f32[8,128]{1,0:T(8,128)S(1)} %get-tuple-element.39.gap_ref, f32[8,128]{1,0:T(8,128)S(1)} %get-tuple-element.40.stiff_ref, ...), custom_call_target="tpu_custom_call" | custom-call | tf_op jit(solution)/shard_map/pallas_call | solution.py:35
  20.4 3.4 %all-to-all-start.1 = ((f32[8,8,128]{2,1,0:T(8,128)}), f32[8,8,128]{2,1,0:T(8,128)S(1)}, u32[]{:S(2)}, u32[]{:S(2)}) async-start(f32[8,8,128]{2,1,0:T(8,128)} %shard_map.105), calls=%async_computation.1 | async-start | bytes 65536 | tf_op jit(solution)/shard_map/all_to_all | solution.py:22
  23.7 0.0 collective-permute-done.yu
  23.7 0.0 collective-permute-done.3.corner
  23.8 0.5 %shard_map.106 = f32[3,16,256]{2,1,0:T(8,128)S(1)} custom-call(f32[3,16,8,256]{3,2,1,0:T(8,128)S(1)} %get-tuple-element.28.u_ref, f32[3,16,8,256]{3,2,1,0:T(8,128)S(1)} %get-tuple-element.24.v_ref, f32[6,16,8,256]{3,2,1,0:T(8,128)S(1)} %get-tuple-element.25.stress_ref, f32[16,8,256]{2,1,0:T(8,128)S(1)} %get-tuple-element.26.hour_ref, ...), custom_call_target="tpu_custom_call" | custom-call | tf_op jit(solution)/shard_map/pallas_call | solution.py:35
  24.2 0.0 collective-permute-start.4
  24.3 1.5 %shard_map.101 = (f32[16,6,3,2,8,128]{5,4,3,2,1,0:T(8,128)S(1)}, f32[15,3,7,2,8,128]{5,4,3,2,1,0:T(8,128)S(1)}) custom-call(f32[3,16,8,256]{3,2,1,0:T(8,128)S(1)} %get-tuple-element.28.u_ref, f32[3,16,8,256]{3,2,1,0:T(8,128)S(1)} %get-tuple-element.24.v_ref, f32[6,16,8,256]{3,2,1,0:T(8,128)S(1)} %get-tuple-element.25.stress_ref, ...), custom_call_target="tpu_custom_call" | custom-call | tf_op jit(solution)/shard_map/pallas_call | solution.py:35
  25.8 1.1 %shard_map.103.base_ref = f32[3,16,8,256]{3,2,1,0:T(8,128)S(1)} custom-call(f32[3,16,8,256]{3,2,1,0:T(8,128)S(1)} %get-tuple-element.24.v_ref, f32[6,16,8,256]{3,2,1,0:T(8,128)S(1)} %get-tuple-element.25.stress_ref, f32[16,8,256]{2,1,0:T(8,128)S(1)} %get-tuple-element.26.hour_ref, f32[16,8,256]{2,1,0:T(8,128)S(1)} %get-tuple-element.27.mass_ref, ...), custom_call_target="tpu_custom_call" | custom-call | tf_op jit(solution)/shard_map/pallas_call | solution.py:35
  26.9 3.5 %all-to-all-done.1.table_ref = f32[8,8,128]{2,1,0:T(8,128)S(1)} async-done(((f32[8,8,128]{2,1,0:T(8,128)}), f32[8,8,128]{2,1,0:T(8,128)S(1)}, u32[]{:S(2)}, u32[]{:S(2)}) %all-to-all-start.1) | async-done | bytes 32800 | tf_op jit(solution)/shard_map/all_to_all | solution.py:22
  30.4 0.0 collective-permute-done.4.left_ref
  30.4 1.0 %shard_map.107 = f32[3,16,8,256]{3,2,1,0:T(8,128)} custom-call(f32[3,16,8,256]{3,2,1,0:T(8,128)S(1)} %shard_map.103.base_ref, f32[16,8,256]{2,1,0:T(8,128)S(1)} %get-tuple-element.27.mass_ref, f32[8,8,128]{2,1,0:T(8,128)S(1)} %all-to-all-done.1.table_ref, s32[2,128]{1,0:T(2,128)S(1)} %get-tuple-element.42.route_ref, ...), custom_call_target="tpu_custom_call" | custom-call | tf_op jit(solution)/shard_map/pallas_call | solution.py:35
  (1 shorter events, 0.0 us)
Async XLA Ops:
  2.0 10.4 %collective-permute-start.2 = (f32[104,256]{1,0:T(8,128)S(1)}, f32[104,256]{1,0:T(8,128)S(1)}, u32[]{:S(2)}, u32[]{:S(2)}) collective-permute-start(f32[104,256]{1,0:T(8,128)S(1)} %get-tuple-element.33), channel_id=1, source_target_pairs={{0,4},{4,8},{8,12},{12,16},{16,20},{20,24},{24,28},{28,0},{1,5},{5... | collective-permute-start | bytes 319496 | tf_op jit(solution)/shard_map/ppermute | solution.py:18
  5.1 18.7 %collective-permute-start = (f32[6,16,256]{2,1,0:T(8,128)S(1)}, f32[6,16,256]{2,1,0:T(8,128)S(1)}, u32[]{:S(2)}, u32[]{:S(2)}) collective-permute-start(f32[6,16,256]{2,1,0:T(8,128)S(1)} %get-tuple-element.29), channel_id=1, source_target_pairs={{0,3},{1,0},{2,1},{3,2},{4,7},{5,4},{6,5},{7,6},{8,11},{9,8},{10,9... | collective-permute-start | bytes 294920 | tf_op jit(solution)/shard_map/ppermute | solution.py:18
  5.7 6.7 %collective-permute-start.1 = (f32[48,256]{1,0:T(8,128)S(1)}, f32[48,256]{1,0:T(8,128)S(1)}, u32[]{:S(2)}, u32[]{:S(2)}) collective-permute-start(f32[48,256]{1,0:T(8,128)S(1)} %get-tuple-element.32), channel_id=1, source_target_pairs={{0,28},{4,0},{8,4},{12,8},{16,12},{20,16},{24,20},{28,24},{1,29},{... | collective-permute-start | bytes 147464 | tf_op jit(solution)/shard_map/ppermute | solution.py:18
  9.1 10.0 %all-to-all-start = ((f32[8,8,128]{2,1,0:T(8,128)}), f32[8,8,128]{2,1,0:T(8,128)S(1)}, u32[]{:S(2)}, u32[]{:S(2)}) async-start(f32[8,8,128]{2,1,0:T(8,128)} %get-tuple-element.34), calls=%async_computation | async-start | bytes 65536 | tf_op jit(solution)/shard_map/all_to_all | solution.py:22
  12.5 11.3 %collective-permute-start.3 = (f32[16,256]{1,0:T(8,128)S(1)}, f32[16,256]{1,0:T(8,128)S(1)}, u32[]{:S(2)}, u32[]{:S(2)}) collective-permute-start(f32[16,256]{1,0:T(8,128)S(1)} %shard_map.102), channel_id=1, source_target_pairs={{0,3},{1,0},{2,1},{3,2},{4,7},{5,4},{6,5},{7,6},{8,11},{9,8},{10,9... | collective-permute-start | bytes 49160 | tf_op jit(solution)/shard_map/ppermute | solution.py:18
  20.4 10.0 %all-to-all-start.1 = ((f32[8,8,128]{2,1,0:T(8,128)}), f32[8,8,128]{2,1,0:T(8,128)S(1)}, u32[]{:S(2)}, u32[]{:S(2)}) async-start(f32[8,8,128]{2,1,0:T(8,128)} %shard_map.105), calls=%async_computation.1 | async-start | bytes 65536 | tf_op jit(solution)/shard_map/all_to_all | solution.py:22
  24.2 6.1 %collective-permute-start.4 = (f32[3,16,256]{2,1,0:T(8,128)S(1)}, f32[3,16,256]{2,1,0:T(8,128)S(1)}, u32[]{:S(2)}, u32[]{:S(2)}) collective-permute-start(f32[3,16,256]{2,1,0:T(8,128)S(1)} %shard_map.106), channel_id=1, source_target_pairs={{0,1},{1,2},{2,3},{3,0},{4,5},{5,6},{6,7},{7,4},{8,9},{9,10},{10,1... | collective-permute-start | bytes 147464 | tf_op jit(solution)/shard_map/ppermute | solution.py:18

commit v6 on v5

--- a/solution.py
+++ b/solution.py
@@ -19,7 +19,15 @@
 
 
 def exchanged(value):
-    return lax.all_to_all(value, "space", split_axis=0, concat_axis=0, tiled=True)
+    count = lax.axis_size("space")
+    order = [(at + count // 4) % count for at in range(count)]
+    return lax.all_to_all(
+        value, "space", split_axis=0, concat_axis=0, tiled=True, axis_index_groups=[order]
+    )
+
+
+def seat(at, count):
+    return (at - count // 4) % count
 
 
 def kernel_call(body, inputs, outs, scratch=(), hbm_inputs=0):
@@ -88,7 +96,7 @@
         at = [(part * blocks + b) * 8 for part in range(3)]
         total = got[at[0] : at[0] + 8] + got[at[1] : at[1] + 8] + got[at[2] : at[2] + 8]
         for q in range(pack):
-            out_ref[b * pack + q, :, 0 : total.shape[1]] = total
+            out_ref[seat(b * pack + q, out_ref.shape[0]), :, 0 : total.shape[1]] = total
 
 
 def first_body(
@@ -184,7 +192,7 @@
     for b in range(rows_ref.shape[0]):
         total = None
         for q in range(min(together, table_ref.shape[0] - b * together)):
-            tile = table_ref[b * together + q]
+            tile = table_ref[seat(b * together + q, table_ref.shape[0])]
             if pack > 1:
                 tile = jnp.where((lane >= offset) & (lane < offset + capacity), tile, 0.0)
                 tile = pltpu.roll(tile, (q * capacity - offset) & (LANES - 1), 1)
@@ -241,7 +249,8 @@
     width = pack * capacity
     for b in range(blocks):
         for q in range(pack):
-            out_ref[b * pack + q, :, 0:width] = total[:, b * width : (b + 1) * width]
+            block = total[:, b * width : (b + 1) * width]
+            out_ref[seat(b * pack + q, out_ref.shape[0]), :, 0:width] = block
     copy = pltpu.make_async_copy(out_ref, out_hbm, sem)
     copy.start()
     copy.wait()

time: 31.7 us -> 29.4 us (0.927)
  waiting for transfers between devices: 8.48 us -> 5.91 us
    all_to_all x2, waiting for transfers between devices: 8.47 us -> 5.9 us  [exchanged(): lax.all_to_all(value, 'space', split_axis=0, concat_axis=0, tiled=True, a...]
    all_to_all x2, starting transfers between devices: 6.7 us -> 7.2 us  [exchanged(): lax.all_to_all(value, 'space', split_axis=0, concat_axis=0, tiled=True, a...]
  transfers between devices with their start and end apart: 7 -> 7, of which waited for: 2 -> 2; matrix products, arithmetic and copies ran while one was open for 0% -> 0% of each run, Pallas kernels for 17% -> 19%
where the time goes in v6:
time: 29.4 us; the launch traced here: 29.1 us
  starting transfers between devices  14.7 us (50%)
  Pallas kernels  8.46 us (29%)
  waiting for transfers between devices  5.91 us (20%)
    pallas_call x8, Pallas kernels, kernel_call(): pl.pallas_call(body, out_shape=outs, in_specs=[pl.BlockSpec(memory_space=...  8.46 us
    ppermute x5, starting transfers between devices, shifted(): lax.ppermute(value, axis, [(at, (at + steps) % count) for at in range(cou...  7.46 us
    all_to_all x2, starting transfers between devices, exchanged(): lax.all_to_all(value, 'space', split_axis=0, concat_axis=0, tiled=True, a...  7.2 us
    all_to_all x2, waiting for transfers between devices, exchanged(): lax.all_to_all(value, 'space', split_axis=0, concat_axis=0, tiled=True, a...  5.9 us
  transfers between devices with their start and end apart: 7, of which 2 were waited for; matrix products, arithmetic and copies ran while one was open for 0% of the time, Pallas kernels for 19%

profile of v6, /device:TPU:0, one launch (start us, length us, event | category | flops | bytes accessed | tf_op | source)
XLA Modules:
  0.0 29.1 jit_solution(10755916036929390992)
XLA Ops:
  0.0 2.0 %shard_map.100 = (f32[8,8,128]{2,1,0:T(8,128)}, f32[6,16,256]{2,1,0:T(8,128)S(1)}, f32[48,256]{1,0:T(8,128)S(1)}, f32[104,256]{1,0:T(8,128)S(1)}, s32[2,128]{1,0...) custom-call(f32[3,16,8,256]{3,2,1,0:T(8,128)} %u_hbm.1, ...), custom_call_target="tpu_custom_call" | custom-call | tf_op jit(solution)/shard_map/pallas_call | solution.py:43
  2.0 3.0 %collective-permute-start.2 = (f32[104,256]{1,0:T(8,128)S(1)}, f32[104,256]{1,0:T(8,128)S(1)}, u32[]{:S(2)}, u32[]{:S(2)}) collective-permute-start(f32[104,256]{1,0:T(8,128)S(1)} %get-tuple-element.33), channel_id=1, source_target_pairs={{0,4},{4,8},{8,12},{12,16},{16,20},{20,24},{24,28},{28,0},{1,5},{5... | collective-permute-start | bytes 319496 | tf_op jit(solution)/shard_map/ppermute | solution.py:18
  5.1 0.7 %collective-permute-start = (f32[6,16,256]{2,1,0:T(8,128)S(1)}, f32[6,16,256]{2,1,0:T(8,128)S(1)}, u32[]{:S(2)}, u32[]{:S(2)}) collective-permute-start(f32[6,16,256]{2,1,0:T(8,128)S(1)} %get-tuple-element.29), channel_id=1, source_target_pairs={{0,3},{1,0},{2,1},{3,2},{4,7},{5,4},{6,5},{7,6},{8,11},{9,8},{10,9... | collective-permute-start | bytes 294920 | tf_op jit(solution)/shard_map/ppermute | solution.py:18
  5.7 3.4 %collective-permute-start.1 = (f32[48,256]{1,0:T(8,128)S(1)}, f32[48,256]{1,0:T(8,128)S(1)}, u32[]{:S(2)}, u32[]{:S(2)}) collective-permute-start(f32[48,256]{1,0:T(8,128)S(1)} %get-tuple-element.32), channel_id=1, source_target_pairs={{0,28},{4,0},{8,4},{12,8},{16,12},{20,16},{24,20},{28,24},{1,29},{... | collective-permute-start | bytes 147464 | tf_op jit(solution)/shard_map/ppermute | solution.py:18
  9.1 3.5 %all-to-all-start = ((f32[8,8,128]{2,1,0:T(8,128)}), f32[8,8,128]{2,1,0:T(8,128)S(1)}, u32[]{:S(2)}, u32[]{:S(2)}) async-start(f32[8,8,128]{2,1,0:T(8,128)} %get-tuple-element.34), calls=%async_computation | async-start | bytes 65536 | tf_op jit(solution)/shard_map/all_to_all | solution.py:24
  12.6 0.0 collective-permute-done.1.xu
  12.6 0.0 collective-permute-done.2.xd
  12.6 0.3 %collective-permute-start.3 = (f32[16,256]{1,0:T(8,128)S(1)}, f32[16,256]{1,0:T(8,128)S(1)}, u32[]{:S(2)}, u32[]{:S(2)}) collective-permute-start(f32[16,256]{1,0:T(8,128)S(1)} %shard_map.102), channel_id=1, source_target_pairs={{0,3},{1,0},{2,1},{3,2},{4,7},{5,4},{6,5},{7,6},{8,11},{9,8},{10,9... | collective-permute-start | bytes 49160 | tf_op jit(solution)/shard_map/ppermute | solution.py:18
  13.0 1.0 %shard_map.104 = (bf16[384,1024]{1,0:T(8,128)(2,1)S(1)}, s32[5,8,128]{2,1,0:T(8,128)S(1)}, f32[6,8,128]{2,1,0:T(8,128)S(1)}) custom-call(s32[5,1024]{1,0:T(8,128)S(1)} %get-tuple-element.35.nodes_ref, f32[6,1024]{1,0:T(8,128)S(1)} %get-tuple-element.36.diag_ref), custom_call_target="tpu_custom_call" | custom-call | tf_op jit(solution)/shard_map/pallas_call | solution.py:43
  14.0 3.8 %all-to-all-done.table_ref = f32[8,8,128]{2,1,0:T(8,128)S(1)} async-done(((f32[8,8,128]{2,1,0:T(8,128)}), f32[8,8,128]{2,1,0:T(8,128)S(1)}, u32[]{:S(2)}, u32[]{:S(2)}) %all-to-all-start) | async-done | bytes 32800 | tf_op jit(solution)/shard_map/all_to_all | solution.py:24
  17.8 1.3 %shard_map.105 = f32[8,8,128]{2,1,0:T(8,128)} custom-call(f32[8,8,128]{2,1,0:T(8,128)S(1)} %all-to-all-done.table_ref, s32[5,8,128]{2,1,0:T(8,128)S(1)} %get-tuple-element.37.nodes_ref, f32[6,8,128]{2,1,0:T(8,128)S(1)} %get-tuple-element.38.diag_ref, f32[8,128]{1,0:T(8,128)S(1)} %get-tuple-element.39.gap_ref, f32[8,128]{1,0:T(8,128)S(1)} %get-tuple-element.40.stiff_ref, ...), custom_call_target="tpu_custom_call" | custom-call | tf_op jit(solution)/shard_map/pallas_call | solution.py:43
  19.1 3.7 %all-to-all-start.1 = ((f32[8,8,128]{2,1,0:T(8,128)}), f32[8,8,128]{2,1,0:T(8,128)S(1)}, u32[]{:S(2)}, u32[]{:S(2)}) async-start(f32[8,8,128]{2,1,0:T(8,128)} %shard_map.105), calls=%async_computation.1 | async-start | bytes 65536 | tf_op jit(solution)/shard_map/all_to_all | solution.py:24
  22.8 0.0 collective-permute-done.yu
  22.8 0.0 collective-permute-done.3.corner
  22.8 0.5 %shard_map.106 = f32[3,16,256]{2,1,0:T(8,128)S(1)} custom-call(f32[3,16,8,256]{3,2,1,0:T(8,128)S(1)} %get-tuple-element.28.u_ref, f32[3,16,8,256]{3,2,1,0:T(8,128)S(1)} %get-tuple-element.24.v_ref, f32[6,16,8,256]{3,2,1,0:T(8,128)S(1)} %get-tuple-element.25.stress_ref, f32[16,8,256]{2,1,0:T(8,128)S(1)} %get-tuple-element.26.hour_ref, ...), custom_call_target="tpu_custom_call" | custom-call | tf_op jit(solution)/shard_map/pallas_call | solution.py:43
  23.3 0.0 collective-permute-start.4
  23.3 1.5 %shard_map.101 = (f32[16,6,3,2,8,128]{5,4,3,2,1,0:T(8,128)S(1)}, f32[15,3,7,2,8,128]{5,4,3,2,1,0:T(8,128)S(1)}) custom-call(f32[3,16,8,256]{3,2,1,0:T(8,128)S(1)} %get-tuple-element.28.u_ref, f32[3,16,8,256]{3,2,1,0:T(8,128)S(1)} %get-tuple-element.24.v_ref, f32[6,16,8,256]{3,2,1,0:T(8,128)S(1)} %get-tuple-element.25.stress_ref, ...), custom_call_target="tpu_custom_call" | custom-call | tf_op jit(solution)/shard_map/pallas_call | solution.py:43
  24.9 1.1 %shard_map.103.base_ref = f32[3,16,8,256]{3,2,1,0:T(8,128)S(1)} custom-call(f32[3,16,8,256]{3,2,1,0:T(8,128)S(1)} %get-tuple-element.24.v_ref, f32[6,16,8,256]{3,2,1,0:T(8,128)S(1)} %get-tuple-element.25.stress_ref, f32[16,8,256]{2,1,0:T(8,128)S(1)} %get-tuple-element.26.hour_ref, f32[16,8,256]{2,1,0:T(8,128)S(1)} %get-tuple-element.27.mass_ref, ...), custom_call_target="tpu_custom_call" | custom-call | tf_op jit(solution)/shard_map/pallas_call | solution.py:43
  26.0 2.1 %all-to-all-done.1.table_ref = f32[8,8,128]{2,1,0:T(8,128)S(1)} async-done(((f32[8,8,128]{2,1,0:T(8,128)}), f32[8,8,128]{2,1,0:T(8,128)S(1)}, u32[]{:S(2)}, u32[]{:S(2)}) %all-to-all-start.1) | async-done | bytes 32800 | tf_op jit(solution)/shard_map/all_to_all | solution.py:24
  28.0 0.0 collective-permute-done.4.left_ref
  28.0 1.0 %shard_map.107 = f32[3,16,8,256]{3,2,1,0:T(8,128)} custom-call(f32[3,16,8,256]{3,2,1,0:T(8,128)S(1)} %shard_map.103.base_ref, f32[16,8,256]{2,1,0:T(8,128)S(1)} %get-tuple-element.27.mass_ref, f32[8,8,128]{2,1,0:T(8,128)S(1)} %all-to-all-done.1.table_ref, s32[2,128]{1,0:T(2,128)S(1)} %get-tuple-element.42.route_ref, ...), custom_call_target="tpu_custom_call" | custom-call | tf_op jit(solution)/shard_map/pallas_call | solution.py:43
  (1 shorter events, 0.0 us)
Async XLA Ops:
  2.0 10.6 %collective-permute-start.2 = (f32[104,256]{1,0:T(8,128)S(1)}, f32[104,256]{1,0:T(8,128)S(1)}, u32[]{:S(2)}, u32[]{:S(2)}) collective-permute-start(f32[104,256]{1,0:T(8,128)S(1)} %get-tuple-element.33), channel_id=1, source_target_pairs={{0,4},{4,8},{8,12},{12,16},{16,20},{20,24},{24,28},{28,0},{1,5},{5... | collective-permute-start | bytes 319496 | tf_op jit(solution)/shard_map/ppermute | solution.py:18
  5.1 17.8 %collective-permute-start = (f32[6,16,256]{2,1,0:T(8,128)S(1)}, f32[6,16,256]{2,1,0:T(8,128)S(1)}, u32[]{:S(2)}, u32[]{:S(2)}) collective-permute-start(f32[6,16,256]{2,1,0:T(8,128)S(1)} %get-tuple-element.29), channel_id=1, source_target_pairs={{0,3},{1,0},{2,1},{3,2},{4,7},{5,4},{6,5},{7,6},{8,11},{9,8},{10,9... | collective-permute-start | bytes 294920 | tf_op jit(solution)/shard_map/ppermute | solution.py:18
  5.7 6.9 %collective-permute-start.1 = (f32[48,256]{1,0:T(8,128)S(1)}, f32[48,256]{1,0:T(8,128)S(1)}, u32[]{:S(2)}, u32[]{:S(2)}) collective-permute-start(f32[48,256]{1,0:T(8,128)S(1)} %get-tuple-element.32), channel_id=1, source_target_pairs={{0,28},{4,0},{8,4},{12,8},{16,12},{20,16},{24,20},{28,24},{1,29},{... | collective-permute-start | bytes 147464 | tf_op jit(solution)/shard_map/ppermute | solution.py:18
  9.1 8.7 %all-to-all-start = ((f32[8,8,128]{2,1,0:T(8,128)}), f32[8,8,128]{2,1,0:T(8,128)S(1)}, u32[]{:S(2)}, u32[]{:S(2)}) async-start(f32[8,8,128]{2,1,0:T(8,128)} %get-tuple-element.34), calls=%async_computation | async-start | bytes 65536 | tf_op jit(solution)/shard_map/all_to_all | solution.py:24
  12.6 10.2 %collective-permute-start.3 = (f32[16,256]{1,0:T(8,128)S(1)}, f32[16,256]{1,0:T(8,128)S(1)}, u32[]{:S(2)}, u32[]{:S(2)}) collective-permute-start(f32[16,256]{1,0:T(8,128)S(1)} %shard_map.102), channel_id=1, source_target_pairs={{0,3},{1,0},{2,1},{3,2},{4,7},{5,4},{6,5},{7,6},{8,11},{9,8},{10,9... | collective-permute-start | bytes 49160 | tf_op jit(solution)/shard_map/ppermute | solution.py:18
  19.1 8.9 %all-to-all-start.1 = ((f32[8,8,128]{2,1,0:T(8,128)}), f32[8,8,128]{2,1,0:T(8,128)S(1)}, u32[]{:S(2)}, u32[]{:S(2)}) async-start(f32[8,8,128]{2,1,0:T(8,128)} %shard_map.105), calls=%async_computation.1 | async-start | bytes 65536 | tf_op jit(solution)/shard_map/all_to_all | solution.py:24
  23.3 4.7 %collective-permute-start.4 = (f32[3,16,256]{2,1,0:T(8,128)S(1)}, f32[3,16,256]{2,1,0:T(8,128)S(1)}, u32[]{:S(2)}, u32[]{:S(2)}) collective-permute-start(f32[3,16,256]{2,1,0:T(8,128)S(1)} %shard_map.106), channel_id=1, source_target_pairs={{0,1},{1,2},{2,3},{3,0},{4,5},{5,6},{6,7},{7,4},{8,9},{9,10},{10,1... | collective-permute-start | bytes 147464 | tf_op jit(solution)/shard_map/ppermute | solution.py:18

commit v7 on v6

--- a/solution.py
+++ b/solution.py
@@ -103,9 +103,9 @@
     capacity, pack, blocks, u_hbm, route_hbm, v_hbm, *rest,
 ):
     hbm, rest = (u_hbm, route_hbm, v_hbm) + rest[:7], rest[7:]
-    message_hbm, ydn, xdn, xup, sides_ref, u_ref, v_ref, stress_ref, hour_ref = rest[:9]
+    message_hbm, ydn, yup, xdn, xup, sides_ref, u_ref, v_ref, stress_ref, hour_ref = rest[:10]
     out_ref, rows_ref, route_ref, sems, message_sem = rest[-5:]
-    targets = (u_ref, route_ref, v_ref, stress_ref, hour_ref) + rest[9:-5]
+    targets = (u_ref, route_ref, v_ref, stress_ref, hour_ref) + rest[10:-5]
     copies = [
         pltpu.make_async_copy(source, target, sems.at[at])
         for at, (source, target) in enumerate(zip(hbm, targets))
@@ -140,6 +140,7 @@
     for c in range(13):
         ref = component(u_ref, v_ref, stress_ref, hour_ref, c)
         xup[c * columns : (c + 1) * columns, :] = ref[planes - 1]
+        yup[c] = ref[:, columns - 1, :]
         if c < 6:
             xdn[c * columns : (c + 1) * columns, :] = ref[0]
             ydn[c] = ref[:, 0, :]
@@ -158,11 +159,16 @@
     return hour_ref
 
 
-def corner_body(columns, xu, xd, out_ref):
-    out_ref[...] = jnp.zeros(out_ref.shape, jnp.float32)
-    for c in range(6):
-        out_ref[c : c + 1, :] = xd[c * columns : c * columns + 1, :]
-        out_ref[8 + c : 9 + c, :] = xu[c * columns : c * columns + 1, :]
+def corner_body(columns, xu, xd, left_ref, right_ref):
+    left_ref[...] = jnp.zeros(left_ref.shape, jnp.float32)
+    right_ref[...] = jnp.zeros(right_ref.shape, jnp.float32)
+    for c in range(13):
+        at = c * columns
+        right_ref[c : c + 1, :] = xd[at + columns - 1 : at + columns, :]
+        if c < 6:
+            left_ref[c : c + 1, :] = xd[at : at + 1, :]
+            left_ref[8 + c : 9 + c, :] = xu[at : at + 1, :]
+            right_ref[16 + c : 17 + c, :] = xu[at + columns - 1 : at + columns, :]
 
 
 def matrix_body(nodes_ref, diag_ref, matrix_ref, lines_ref, diag_lines_ref):
@@ -340,8 +346,8 @@
     return jnp.where(lane == 0, before_up, up) + jnp.where(last, 0.0, p - r)
 
 
-def edge_body(u_ref, v_ref, stress_ref, hour_ref, yu, xu, xd, corner, beyond_ref, row_ref):
-    planes, columns, _ = u_ref.shape[1:]
+def edge_body(columns, ydn, yd, xu, xd, corner, out_ref, row_ref):
+    planes = ydn.shape[1]
     rows = row_ref.shape[0]
     row_ref[...] = jnp.zeros(row_ref.shape, jnp.float32)
 
@@ -358,27 +364,23 @@
     def following(q):
         return pltpu.roll(q, rows - 1, 1)
 
-    def own(c):
-        middle = component(u_ref, v_ref, stress_ref, hour_ref, c)[:, columns - 1, :]
-        at = c * columns + columns - 1
-        return assembled(line(xd, at), middle, line(xu, at) if c < 6 else None)
-
-    own_s, own_d, next_s, next_d = [], [], [], []
+    left_s, left_d, own_s, own_d = [], [], [], []
     for c in range(6):
-        s, d = z_pair(own(c))
+        s, d = z_pair(assembled(line(corner, c), yd[c], line(corner, 16 + c)))
+        left_s.append(s)
+        left_d.append(d)
+        s, d = z_pair(assembled(line(xd, c * columns), ydn[c], line(xu, c * columns)))
         own_s.append(s)
         own_d.append(d)
-        s, d = z_pair(assembled(line(corner, c), yu[c], line(corner, 8 + c)))
-        next_s.append(s)
-        next_d.append(d)
-    lower = node_terms(own_s, own_d, next_s, next_d)
+    stress = [assembled(line(corner, 6 + c), yd[6 + c], None) for c in range(6)]
+    hour = assembled(line(corner, 12), yd[12], None)
+    lower = node_terms(left_s, left_d, own_s, own_d)
     upper = [tuple(following(q) for q in terms) for terms in lower]
-    factors = element_terms(lower, upper, [own(6 + c) for c in range(6)], own(12))
+    factors = element_terms(lower, upper, stress, hour)
     after = [[following(q) for q in terms] for terms in factors]
     for m, (a, b, c, e) in enumerate(gathered_x(factors, after)):
-        force = along_z(a + b, c + e)[:, 0:planes]
-        for k in range(force.shape[0]):
-            beyond_ref[m, :, k * LANES : (k + 1) * LANES] = force[k]
+        out_ref[m, 0] = a + b
+        out_ref[m, 1] = c + e
 
 
 def node_plane(values, halo_s, halo_d):
@@ -402,13 +404,13 @@
     return [[elem_ref[i, m, t] for t in range(7)] for m in range(3)]
 
 
-def new_velocity(before, after, velocity, mass):
+def new_velocity(before, after, left, velocity, mass):
     row = lax.broadcasted_iota(jnp.int32, mass.shape, 1)
     weight = (time_step / 64.0) / mass
     result = []
     for m, (a, b, c, e) in enumerate(gathered_x(before, after)):
-        p = (a - b) + jnp.where(row == 0, 0.0, pltpu.roll(a + b, 1, 1))
-        r = (c - e) + jnp.where(row == 0, 0.0, pltpu.roll(c + e, 1, 1))
+        p = (a - b) + jnp.where(row == 0, left[m][0], pltpu.roll(a + b, 1, 1))
+        r = (c - e) + jnp.where(row == 0, left[m][1], pltpu.roll(c + e, 1, 1))
         result.append(velocity[m] - along_z(p, r) * weight)
     return result
 
@@ -460,14 +462,16 @@
 
 
 def outer_body(
-    unroll, v_ref, stress_ref, hour_ref, mass_ref, node_ref, elem_ref, xu, xd, corner, out_ref
+    unroll, v_ref, stress_ref, hour_ref, mass_ref, node_ref, elem_ref, edge_ref, xu, xd, corner,
+    out_ref,
 ):
     planes, columns, depth = v_ref.shape[1:]
     last = planes - 1
 
     def write_plane(i, before, after):
         velocity = [split(v_ref[m, i]) for m in range(3)]
-        result = new_velocity(before, after, velocity, split(mass_ref[i]))
+        left = [[edge_ref[m, t, :, pl.ds(i, 1), :] for t in range(2)] for m in range(3)]
+        result = new_velocity(before, after, left, velocity, split(mass_ref[i]))
         for m in range(3):
             for k in range(depth // LANES):
                 out_ref[m, i, :, k * LANES : (k + 1) * LANES] = result[m][k]
@@ -505,7 +509,7 @@
 
 def final_body(
     capacity, pack,
-    base_ref, mass_ref, table_ref, route_ref, left_ref,
+    base_ref, mass_ref, table_ref, route_ref,
     out_hbm, rows_ref, out_ref, dense_ref, sems,
 ):
     planes, columns, depth = base_ref.shape[1:]
@@ -514,23 +518,17 @@
     (contact,) = looked_up(dense_ref, [route_ref[...]], dense)
     rows_ref[...] = jnp.zeros(rows_ref.shape, jnp.float32)
     lane = lax.broadcasted_iota(jnp.int32, (planes, columns, LANES), 2)
-    row = lax.broadcasted_iota(jnp.int32, (columns, LANES), 0)
-    weights = [time_step / mass_ref[:, :, k : k + LANES] for k in range(0, depth, LANES)]
-    low_weight = jnp.where(lane == 0, weights[0], 0.0)
-    high_weight = jnp.where(lane == LANES - 1, weights[-1], 0.0)
+    low_weight = jnp.where(lane == 0, time_step / mass_ref[:, :, 0:LANES], 0.0)
+    high_weight = jnp.where(
+        lane == LANES - 1, time_step / mass_ref[:, :, depth - LANES : depth], 0.0
+    )
     copies = []
     for m in range(3):
         rows_ref[m, 0:1, :] = contact[m][0:1]
         rows_ref[m, LANES - 1 : LANES, :] = contact[m][1:2]
         turned = rows_ref[m].T.reshape(planes, columns, LANES)
         for k in range(0, depth, LANES):
-            left = jnp.stack(
-                [
-                    jnp.where(row == 0, left_ref[m, i : i + 1, k : k + LANES] * (1.0 / 64.0), 0.0)
-                    for i in range(planes)
-                ]
-            )
-            value = base_ref[m, :, :, k : k + LANES] - left * weights[k // LANES]
+            value = base_ref[m, :, :, k : k + LANES]
             if k == 0:
                 value = value + low_weight * turned
             if k == depth - LANES:
@@ -569,12 +567,13 @@
     small = (pair_nodes, pair_diagonals, pair_gap.reshape(lines, LANES))
     small += (pair_stiffness.reshape(lines, LANES),)
     kept = (displacement, velocity, stress, hourglass, mass) + small
-    outgoing, ydn, xdn, xup, sides, *kept = kernel_call(
+    outgoing, ydn, yup, xdn, xup, sides, *kept = kernel_call(
         functools.partial(first_body, capacity, pack, blocks),
         (displacement, contact_route.reshape(1, surf_count)) + kept[1:],
         (
             pltpu.HBM(message.shape, f32),
             sized(6, planes, depth),
+            sized(13, planes, depth),
             sized(6 * columns, depth),
             sized(13 * columns, depth),
             jax.ShapeDtypeStruct((2, surf_count // 2), jnp.int32),
@@ -592,6 +591,7 @@
     fields, (pair_nodes, pair_diagonals, gap, stiffness) = kept[:5], kept[5:]
     received = exchanged(outgoing)
     yu = shifted(ydn, "slab", -1)
+    yd = shifted(yup, "slab", 1)
     xu = shifted(xdn, "space", -1)
     xd = shifted(xup, "space", 1)
     slots = (nspace * capacity + 15) // 16 * 16
@@ -618,8 +618,11 @@
     )
     returned = exchanged(slot_force)
 
-    corner = kernel_call(functools.partial(corner_body, columns), (xu, xd), sized(16, depth))
-    corner = shifted(corner, "slab", -1)
+    to_left, to_right = kernel_call(
+        functools.partial(corner_body, columns), (xu, xd), (sized(16, depth), sized(24, depth))
+    )
+    right_corner = shifted(to_left, "slab", -1)
+    left_corner = shifted(to_right, "slab", 1)
     nb = depth // LANES
     node, elem = kernel_call(
         functools.partial(inner_body, 2),
@@ -634,22 +637,21 @@
         ],
     )
     rows = (planes + 2 + 7) // 8 * 8
-    beyond = kernel_call(
-        edge_body,
-        (*fields[:4], yu, xu, xd, corner),
-        sized(3, planes, depth),
+    edge = kernel_call(
+        functools.partial(edge_body, columns),
+        (ydn, yd, xu, xd, left_corner),
+        sized(3, 2, nb, rows, LANES),
         [pltpu.VMEM((rows, depth), f32)],
     )
-    left = shifted(beyond, "slab", 1)
     base = kernel_call(
         functools.partial(outer_body, 2),
-        (*fields[1:], node, elem, xu, xd, corner),
+        (*fields[1:], node, elem, edge, xu, xd, right_corner),
         sized(*displacement.shape),
     )
 
     return kernel_call(
         functools.partial(final_body, capacity, pack),
-        (base, fields[4], returned, sides, left),
+        (base, fields[4], returned, sides),
         pltpu.HBM(displacement.shape, f32),
         [
             pltpu.VMEM((3, LANES, LANES), f32),

time: 29.4 us -> 28.5 us (0.969)
  the two profiles are of different devices: /device:TPU:0 before, /device:TPU:1 now
where the time goes in v7:
time: 28.5 us; the launch traced here: 28.3 us
  starting transfers between devices  16.7 us (59%)
  Pallas kernels  9.06 us (32%)
  waiting for transfers between devices  2.37 us (8%)
    pallas_call x8, Pallas kernels, kernel_call(): pl.pallas_call(body, out_shape=outs, in_specs=[pl.BlockSpec(memory_space=...  9.06 us
    ppermute x6, starting transfers between devices, shifted(): lax.ppermute(value, axis, [(at, (at + steps) % count) for at in range(cou...  8.56 us
    all_to_all x2, starting transfers between devices, exchanged(): lax.all_to_all(value, 'space', split_axis=0, concat_axis=0, tiled=True, a...  8.17 us
    ppermute x6, waiting for transfers between devices, shifted(): lax.ppermute(value, axis, [(at, (at + steps) % count) for at in range(cou...  1.54 us
    all_to_all x2, waiting for transfers between devices, exchanged(): lax.all_to_all(value, 'space', split_axis=0, concat_axis=0, tiled=True, a...  0.83 us
  transfers between devices with their start and end apart: 8, of which 2 were waited for; matrix products, arithmetic and copies ran while one was open for 0% of the time, Pallas kernels for 19%

profile of v7, /device:TPU:1, one launch (start us, length us, event | category | flops | bytes accessed | tf_op | source)
XLA Modules:
  0.0 28.3 jit_solution(5398094313403978535)
XLA Ops:
  0.0 2.7 %shard_map.100 = (f32[8,8,128]{2,1,0:T(8,128)}, f32[6,16,256]{2,1,0:T(8,128)S(1)}, f32[13,16,256]{2,1,0:T(8,128)S(1)}, f32[48,256]{1,0:T(8,128)}, f32[104,256]{1...) custom-call(f32[3,16,8,256]{3,2,1,0:T(8,128)} %u_hbm.1, ...), custom_call_target="tpu_custom_call" | custom-call | tf_op jit(solution)/shard_map/pallas_call | solution.py:43
  2.7 2.6 %collective-permute-start.1 = (f32[13,16,256]{2,1,0:T(8,128)S(1)}, f32[13,16,256]{2,1,0:T(8,128)S(1)}, u32[]{:S(2)}, u32[]{:S(2)}) collective-permute-start(f32[13,16,256]{2,1,0:T(8,128)S(1)} %get-tuple-element.35), channel_id=1, source_target_pairs={{0,1},{1,2},{2,3},{3,0},{4,5},{5,6},{6,7},{7,4},{8,9},{9,10},{10,1... | collective-permute-start | bytes 638984 | tf_op jit(solution)/shard_map/ppermute | solution.py:18
  5.3 1.2 %collective-permute-start.3 = (f32[104,256]{1,0:T(8,128)}, f32[104,256]{1,0:T(8,128)S(1)}, u32[]{:S(2)}, u32[]{:S(2)}) collective-permute-start(f32[104,256]{1,0:T(8,128)} %get-tuple-element.37), channel_id=1, source_target_pairs={{0,4},{4,8},{8,12},{12,16},{16,20},{20,24},{24,28},{28,0},{1,5},{5... | collective-permute-start | bytes 319496 | tf_op jit(solution)/shard_map/ppermute | solution.py:18
  6.5 4.9 %all-to-all-start = ((f32[8,8,128]{2,1,0:T(8,128)}), f32[8,8,128]{2,1,0:T(8,128)S(1)}, u32[]{:S(2)}, u32[]{:S(2)}) async-start(f32[8,8,128]{2,1,0:T(8,128)} %get-tuple-element.40), calls=%async_computation | async-start | bytes 65536 | tf_op jit(solution)/shard_map/all_to_all | solution.py:24
  11.4 0.0 collective-permute-start
  11.4 3.0 %collective-permute-start.2 = (f32[48,256]{1,0:T(8,128)}, f32[48,256]{1,0:T(8,128)S(1)}, u32[]{:S(2)}, u32[]{:S(2)}) collective-permute-start(f32[48,256]{1,0:T(8,128)} %get-tuple-element.36), channel_id=1, source_target_pairs={{0,28},{4,0},{8,4},{12,8},{16,12},{20,16},{24,20},{28,24},{1,29},{... | collective-permute-start | bytes 147464 | tf_op jit(solution)/shard_map/ppermute | solution.py:18
  14.4 1.0 %shard_map.105 = (bf16[384,1024]{1,0:T(8,128)(2,1)S(1)}, s32[5,8,128]{2,1,0:T(8,128)S(1)}, f32[6,8,128]{2,1,0:T(8,128)S(1)}) custom-call(s32[5,1024]{1,0:T(8,128)S(1)} %get-tuple-element.41.nodes_ref, f32[6,1024]{1,0:T(8,128)S(1)} %get-tuple-element.42.diag_ref), custom_call_target="tpu_custom_call" | custom-call | tf_op jit(solution)/shard_map/pallas_call | solution.py:43
  15.4 0.8 %all-to-all-done.table_ref = f32[8,8,128]{2,1,0:T(8,128)S(1)} async-done(((f32[8,8,128]{2,1,0:T(8,128)}), f32[8,8,128]{2,1,0:T(8,128)S(1)}, u32[]{:S(2)}, u32[]{:S(2)}) %all-to-all-start) | async-done | bytes 32800 | tf_op jit(solution)/shard_map/all_to_all | solution.py:24
  16.3 1.3 %shard_map.106 = f32[8,8,128]{2,1,0:T(8,128)} custom-call(f32[8,8,128]{2,1,0:T(8,128)S(1)} %all-to-all-done.table_ref, s32[5,8,128]{2,1,0:T(8,128)S(1)} %get-tuple-element.43.nodes_ref, f32[6,8,128]{2,1,0:T(8,128)S(1)} %get-tuple-element.44.diag_ref, f32[8,128]{1,0:T(8,128)S(1)} %get-tuple-element.45.gap_ref, f32[8,128]{1,0:T(8,128)S(1)} %get-tuple-element.46.stiff_ref, ...), custom_call_target="tpu_custom_call" | custom-call | tf_op jit(solution)/shard_map/pallas_call | solution.py:43
  17.6 3.3 %all-to-all-start.1 = ((f32[8,8,128]{2,1,0:T(8,128)}), f32[8,8,128]{2,1,0:T(8,128)S(1)}, u32[]{:S(2)}, u32[]{:S(2)}) async-start(f32[8,8,128]{2,1,0:T(8,128)} %shard_map.106), calls=%async_computation.1 | async-start | bytes 65536 | tf_op jit(solution)/shard_map/all_to_all | solution.py:24
  20.9 0.0 collective-permute-done.2.xu
  20.9 0.0 collective-permute-done.3.xd
  20.9 1.7 %collective-permute-start.4 = (f32[24,256]{1,0:T(8,128)S(1)}, f32[24,256]{1,0:T(8,128)S(1)}, u32[]{:S(2)}, u32[]{:S(2)}) collective-permute-start(f32[24,256]{1,0:T(8,128)S(1)} %get-tuple-element.38), channel_id=1, source_target_pairs={{0,1},{1,2},{2,3},{3,0},{4,5},{5,6},{6,7},{7,4},{8,9},{9,10},{10,1... | collective-permute-start | bytes 73736 | tf_op jit(solution)/shard_map/ppermute | solution.py:18
  22.6 0.0 collective-permute-start.5
  22.6 0.0 collective-permute-done.yu
  22.6 1.5 %shard_map.101 = (f32[16,6,3,2,8,128]{5,4,3,2,1,0:T(8,128)S(1)}, f32[15,3,7,2,8,128]{5,4,3,2,1,0:T(8,128)S(1)}) custom-call(f32[3,16,8,256]{3,2,1,0:T(8,128)S(1)} %get-tuple-element.31.u_ref, f32[3,16,8,256]{3,2,1,0:T(8,128)S(1)} %get-tuple-element.27.v_ref, f32[6,16,8,256]{3,2,1,0:T(8,128)S(1)} %get-tuple-element.28.stress_ref, ...), custom_call_target="tpu_custom_call" | custom-call | tf_op jit(solution)/shard_map/pallas_call | solution.py:43
  24.1 0.0 collective-permute-done.4.corner
  24.2 0.0 collective-permute-done.1.yd
  24.2 0.4 %shard_map.103.edge_ref = f32[3,2,2,24,128]{4,3,2,1,0:T(8,128)S(1)} custom-call(f32[6,16,256]{2,1,0:T(8,128)S(1)} %get-tuple-element.32.ydn, f32[13,16,256]{2,1,0:T(8,128)S(1)} %collective-permute-done.1.yd, f32[48,256]{1,0:T(8,128)S(1)} %collective-permute-done.2.xu, f32[104,256]{1,0:T(8,128)S(1)} %collective-permute-done.3.xd, ...), custom_call_target="tpu_custom_call" | custom-call | tf_op jit(solution)/shard_map/pallas_call | solution.py:43
  24.5 1.5 %collective-permute-done.5.corner = f32[16,256]{1,0:T(8,128)S(1)} collective-permute-done((f32[16,256]{1,0:T(8,128)S(1)}, f32[16,256]{1,0:T(8,128)S(1)}, u32[]{:S(2)}, u32[]{:S(2)}) %collective-permute-start.5) | collective-permute-done | bytes 16416 | tf_op jit(solution)/shard_map/ppermute | solution.py:18
  26.1 1.1 %shard_map.104.base_ref = f32[3,16,8,256]{3,2,1,0:T(8,128)S(1)} custom-call(f32[3,16,8,256]{3,2,1,0:T(8,128)S(1)} %get-tuple-element.27.v_ref, f32[6,16,8,256]{3,2,1,0:T(8,128)S(1)} %get-tuple-element.28.stress_ref, f32[16,8,256]{2,1,0:T(8,128)S(1)} %get-tuple-element.29.hour_ref, f32[16,8,256]{2,1,0:T(8,128)S(1)} %get-tuple-element.30.mass_ref, ...), custom_call_target="tpu_custom_call" | custom-call | tf_op jit(solution)/shard_map/pallas_call | solution.py:43
  27.2 0.0 all-to-all-done.1.table_ref
  27.2 1.0 %shard_map.107 = f32[3,16,8,256]{3,2,1,0:T(8,128)} custom-call(f32[3,16,8,256]{3,2,1,0:T(8,128)S(1)} %shard_map.104.base_ref, f32[16,8,256]{2,1,0:T(8,128)S(1)} %get-tuple-element.30.mass_ref, f32[8,8,128]{2,1,0:T(8,128)S(1)} %all-to-all-done.1.table_ref, s32[2,128]{1,0:T(2,128)S(1)} %get-tuple-element.48.route_ref), custom_call_target="tpu_custom_call" | custom-call | tf_op jit(solution)/shard_map/pallas_call | solution.py:43
  (1 shorter events, 0.0 us)
Async XLA Ops:
  2.7 21.5 %collective-permute-start.1 = (f32[13,16,256]{2,1,0:T(8,128)S(1)}, f32[13,16,256]{2,1,0:T(8,128)S(1)}, u32[]{:S(2)}, u32[]{:S(2)}) collective-permute-start(f32[13,16,256]{2,1,0:T(8,128)S(1)} %get-tuple-element.35), channel_id=1, source_target_pairs={{0,1},{1,2},{2,3},{3,0},{4,5},{5,6},{6,7},{7,4},{8,9},{9,10},{10,1... | collective-permute-start | bytes 638984 | tf_op jit(solution)/shard_map/ppermute | solution.py:18
  5.3 15.6 %collective-permute-start.3 = (f32[104,256]{1,0:T(8,128)}, f32[104,256]{1,0:T(8,128)S(1)}, u32[]{:S(2)}, u32[]{:S(2)}) collective-permute-start(f32[104,256]{1,0:T(8,128)} %get-tuple-element.37), channel_id=1, source_target_pairs={{0,4},{4,8},{8,12},{12,16},{16,20},{20,24},{24,28},{28,0},{1,5},{5... | collective-permute-start | bytes 319496 | tf_op jit(solution)/shard_map/ppermute | solution.py:18
  6.5 9.7 %all-to-all-start = ((f32[8,8,128]{2,1,0:T(8,128)}), f32[8,8,128]{2,1,0:T(8,128)S(1)}, u32[]{:S(2)}, u32[]{:S(2)}) async-start(f32[8,8,128]{2,1,0:T(8,128)} %get-tuple-element.40), calls=%async_computation | async-start | bytes 65536 | tf_op jit(solution)/shard_map/all_to_all | solution.py:24
  11.4 11.2 %collective-permute-start = (f32[6,16,256]{2,1,0:T(8,128)S(1)}, f32[6,16,256]{2,1,0:T(8,128)S(1)}, u32[]{:S(2)}, u32[]{:S(2)}) collective-permute-start(f32[6,16,256]{2,1,0:T(8,128)S(1)} %get-tuple-element.32.ydn), channel_id=1, source_target_pairs={{0,3},{1,0},{2,1},{3,2},{4,7},{5,4},{6,5},{7,6},{8,11},{9,8},{10,9... | collective-permute-start | bytes 294920 | tf_op jit(solution)/shard_map/ppermute | solution.py:18
  11.4 9.4 %collective-permute-start.2 = (f32[48,256]{1,0:T(8,128)}, f32[48,256]{1,0:T(8,128)S(1)}, u32[]{:S(2)}, u32[]{:S(2)}) collective-permute-start(f32[48,256]{1,0:T(8,128)} %get-tuple-element.36), channel_id=1, source_target_pairs={{0,28},{4,0},{8,4},{12,8},{16,12},{20,16},{24,20},{28,24},{1,29},{... | collective-permute-start | bytes 147464 | tf_op jit(solution)/shard_map/ppermute | solution.py:18
  17.6 9.7 %all-to-all-start.1 = ((f32[8,8,128]{2,1,0:T(8,128)}), f32[8,8,128]{2,1,0:T(8,128)S(1)}, u32[]{:S(2)}, u32[]{:S(2)}) async-start(f32[8,8,128]{2,1,0:T(8,128)} %shard_map.106), calls=%async_computation.1 | async-start | bytes 65536 | tf_op jit(solution)/shard_map/all_to_all | solution.py:24
  20.9 3.2 %collective-permute-start.4 = (f32[24,256]{1,0:T(8,128)S(1)}, f32[24,256]{1,0:T(8,128)S(1)}, u32[]{:S(2)}, u32[]{:S(2)}) collective-permute-start(f32[24,256]{1,0:T(8,128)S(1)} %get-tuple-element.38), channel_id=1, source_target_pairs={{0,1},{1,2},{2,3},{3,0},{4,5},{5,6},{6,7},{7,4},{8,9},{9,10},{10,1... | collective-permute-start | bytes 73736 | tf_op jit(solution)/shard_map/ppermute | solution.py:18
  22.6 3.5 %collective-permute-start.5 = (f32[16,256]{1,0:T(8,128)S(1)}, f32[16,256]{1,0:T(8,128)S(1)}, u32[]{:S(2)}, u32[]{:S(2)}) collective-permute-start(f32[16,256]{1,0:T(8,128)S(1)} %get-tuple-element.39), channel_id=1, source_target_pairs={{0,3},{1,0},{2,1},{3,2},{4,7},{5,4},{6,5},{7,6},{8,11},{9,8},{10,9... | collective-permute-start | bytes 49160 | tf_op jit(solution)/shard_map/ppermute | solution.py:18

commit v8 on v7

--- a/solution.py
+++ b/solution.py
@@ -103,9 +103,10 @@
     capacity, pack, blocks, u_hbm, route_hbm, v_hbm, *rest,
 ):
     hbm, rest = (u_hbm, route_hbm, v_hbm) + rest[:7], rest[7:]
-    message_hbm, ydn, yup, xdn, xup, sides_ref, u_ref, v_ref, stress_ref, hour_ref = rest[:10]
-    out_ref, rows_ref, route_ref, sems, message_sem = rest[-5:]
-    targets = (u_ref, route_ref, v_ref, stress_ref, hour_ref) + rest[10:-5]
+    message_hbm, xdn_hbm, xup_hbm, ydn, yup, sides_ref = rest[:6]
+    u_ref, v_ref, stress_ref, hour_ref = rest[6:10]
+    out_ref, xdn, xup, rows_ref, route_ref, sems, out_sems = rest[-7:]
+    targets = (u_ref, route_ref, v_ref, stress_ref, hour_ref) + rest[10:-7]
     copies = [
         pltpu.make_async_copy(source, target, sems.at[at])
         for at, (source, target) in enumerate(zip(hbm, targets))
@@ -131,8 +132,13 @@
     entries = spread(parts_of(rows_ref[...]), block, blocks)
     got = contract_lanes(jnp.concatenate(entries, 0), places(place, width))
     write_messages(out_ref, got, pack, blocks)
-    message = pltpu.make_async_copy(out_ref, message_hbm, message_sem)
-    message.start()
+    leaving = [
+        pltpu.make_async_copy(source, target, out_sems.at[at])
+        for at, (source, target) in enumerate(
+            ((out_ref, message_hbm), (xdn, xdn_hbm), (xup, xup_hbm))
+        )
+    ]
+    leaving[0].start()
     sides_ref[0:1, :] = route[:, 0:side]
     sides_ref[1:2, :] = route[:, side : 2 * side]
     for copy in copies[2:5]:
@@ -140,13 +146,17 @@
     for c in range(13):
         ref = component(u_ref, v_ref, stress_ref, hour_ref, c)
         xup[c * columns : (c + 1) * columns, :] = ref[planes - 1]
+        if c < 6:
+            xdn[c * columns : (c + 1) * columns, :] = ref[0]
+    leaving[1].start()
+    leaving[2].start()
+    for c in range(13):
+        ref = component(u_ref, v_ref, stress_ref, hour_ref, c)
         yup[c] = ref[:, columns - 1, :]
         if c < 6:
-            xdn[c * columns : (c + 1) * columns, :] = ref[0]
             ydn[c] = ref[:, 0, :]
-    for copy in copies[5:]:
+    for copy in copies[5:] + leaving:
         copy.wait()
-    message.wait()
 
 
 def component(u_ref, v_ref, stress_ref, hour_ref, c):
@@ -567,24 +577,26 @@
     small = (pair_nodes, pair_diagonals, pair_gap.reshape(lines, LANES))
     small += (pair_stiffness.reshape(lines, LANES),)
     kept = (displacement, velocity, stress, hourglass, mass) + small
-    outgoing, ydn, yup, xdn, xup, sides, *kept = kernel_call(
+    outgoing, xdn, xup, ydn, yup, sides, *kept = kernel_call(
         functools.partial(first_body, capacity, pack, blocks),
         (displacement, contact_route.reshape(1, surf_count)) + kept[1:],
         (
             pltpu.HBM(message.shape, f32),
+            pltpu.HBM((6 * columns, depth), f32),
+            pltpu.HBM((13 * columns, depth), f32),
             sized(6, planes, depth),
             sized(13, planes, depth),
-            sized(6 * columns, depth),
-            sized(13 * columns, depth),
             jax.ShapeDtypeStruct((2, surf_count // 2), jnp.int32),
             *(jax.ShapeDtypeStruct(one.shape, one.dtype) for one in kept),
         ),
         [
             pltpu.VMEM(message.shape, f32),
+            pltpu.VMEM((6 * columns, depth), f32),
+            pltpu.VMEM((13 * columns, depth), f32),
             pltpu.VMEM((8, surf_count), f32),
             pltpu.VMEM((1, surf_count), jnp.int32),
             pltpu.SemaphoreType.DMA((len(kept) + 1,)),
-            pltpu.SemaphoreType.DMA,
+            pltpu.SemaphoreType.DMA((3,)),
         ],
         hbm_inputs=len(kept) + 1,
     )

time: 28.5 us -> 28 us (0.982)
  Pallas kernels: 9.06 us -> 8.57 us
    pallas_call x8, Pallas kernels: 9.06 us -> 8.57 us  [kernel_call(): pl.pallas_call(body, out_shape=outs, in_specs=[pl.BlockSpec(memory_space=...]
where the time goes in v8:
time: 28 us; the launch traced here: 27.8 us
  starting transfers between devices  16.7 us (60%)
  Pallas kernels  8.57 us (31%)
  waiting for transfers between devices  2.37 us (8%)
    pallas_call x8, Pallas kernels, kernel_call(): pl.pallas_call(body, out_shape=outs, in_specs=[pl.BlockSpec(memory_space=...  8.57 us
    ppermute x6, starting transfers between devices, shifted(): lax.ppermute(value, axis, [(at, (at + steps) % count) for at in range(cou...  8.56 us
    all_to_all x2, starting transfers between devices, exchanged(): lax.all_to_all(value, 'space', split_axis=0, concat_axis=0, tiled=True, a...  8.17 us
    ppermute x6, waiting for transfers between devices, shifted(): lax.ppermute(value, axis, [(at, (at + steps) % count) for at in range(cou...  1.54 us
    all_to_all x2, waiting for transfers between devices, exchanged(): lax.all_to_all(value, 'space', split_axis=0, concat_axis=0, tiled=True, a...  0.83 us
  transfers between devices with their start and end apart: 8, of which 2 were waited for; matrix products, arithmetic and copies ran while one was open for 0% of the time, Pallas kernels for 19%

profile of v8, /device:TPU:1, one launch (start us, length us, event | category | flops | bytes accessed | tf_op | source)
XLA Modules:
  0.0 27.8 jit_solution(3102992141612320318)
XLA Ops:
  0.0 2.2 %shard_map.100 = (f32[8,8,128]{2,1,0:T(8,128)}, f32[48,256]{1,0:T(8,128)}, f32[104,256]{1,0:T(8,128)}, f32[6,16,256]{2,1,0:T(8,128)S(1)}, f32[13,16,256]{2,1,0:T...) custom-call(f32[3,16,8,256]{3,2,1,0:T(8,128)} %u_hbm.1, ...), custom_call_target="tpu_custom_call" | custom-call | tf_op jit(solution)/shard_map/pallas_call | solution.py:43
  2.2 2.6 %collective-permute-start.1 = (f32[13,16,256]{2,1,0:T(8,128)S(1)}, f32[13,16,256]{2,1,0:T(8,128)S(1)}, u32[]{:S(2)}, u32[]{:S(2)}) collective-permute-start(f32[13,16,256]{2,1,0:T(8,128)S(1)} %get-tuple-element.35), channel_id=1, source_target_pairs={{0,1},{1,2},{2,3},{3,0},{4,5},{5,6},{6,7},{7,4},{8,9},{9,10},{10,1... | collective-permute-start | bytes 638984 | tf_op jit(solution)/shard_map/ppermute | solution.py:18
  4.8 1.2 %collective-permute-start.3 = (f32[104,256]{1,0:T(8,128)}, f32[104,256]{1,0:T(8,128)S(1)}, u32[]{:S(2)}, u32[]{:S(2)}) collective-permute-start(f32[104,256]{1,0:T(8,128)} %get-tuple-element.37), channel_id=1, source_target_pairs={{0,4},{4,8},{8,12},{12,16},{16,20},{20,24},{24,28},{28,0},{1,5},{5... | collective-permute-start | bytes 319496 | tf_op jit(solution)/shard_map/ppermute | solution.py:18
  6.1 4.9 %all-to-all-start = ((f32[8,8,128]{2,1,0:T(8,128)}), f32[8,8,128]{2,1,0:T(8,128)S(1)}, u32[]{:S(2)}, u32[]{:S(2)}) async-start(f32[8,8,128]{2,1,0:T(8,128)} %get-tuple-element.40), calls=%async_computation | async-start | bytes 65536 | tf_op jit(solution)/shard_map/all_to_all | solution.py:24
  10.9 0.0 collective-permute-start
  10.9 3.0 %collective-permute-start.2 = (f32[48,256]{1,0:T(8,128)}, f32[48,256]{1,0:T(8,128)S(1)}, u32[]{:S(2)}, u32[]{:S(2)}) collective-permute-start(f32[48,256]{1,0:T(8,128)} %get-tuple-element.36), channel_id=1, source_target_pairs={{0,28},{4,0},{8,4},{12,8},{16,12},{20,16},{24,20},{28,24},{1,29},{... | collective-permute-start | bytes 147464 | tf_op jit(solution)/shard_map/ppermute | solution.py:18
  13.9 1.0 %shard_map.105 = (bf16[384,1024]{1,0:T(8,128)(2,1)S(1)}, s32[5,8,128]{2,1,0:T(8,128)S(1)}, f32[6,8,128]{2,1,0:T(8,128)S(1)}) custom-call(s32[5,1024]{1,0:T(8,128)S(1)} %get-tuple-element.41.nodes_ref, f32[6,1024]{1,0:T(8,128)S(1)} %get-tuple-element.42.diag_ref), custom_call_target="tpu_custom_call" | custom-call | tf_op jit(solution)/shard_map/pallas_call | solution.py:43
  15.0 0.8 %all-to-all-done.table_ref = f32[8,8,128]{2,1,0:T(8,128)S(1)} async-done(((f32[8,8,128]{2,1,0:T(8,128)}), f32[8,8,128]{2,1,0:T(8,128)S(1)}, u32[]{:S(2)}, u32[]{:S(2)}) %all-to-all-start) | async-done | bytes 32800 | tf_op jit(solution)/shard_map/all_to_all | solution.py:24
  15.8 1.3 %shard_map.106 = f32[8,8,128]{2,1,0:T(8,128)} custom-call(f32[8,8,128]{2,1,0:T(8,128)S(1)} %all-to-all-done.table_ref, s32[5,8,128]{2,1,0:T(8,128)S(1)} %get-tuple-element.43.nodes_ref, f32[6,8,128]{2,1,0:T(8,128)S(1)} %get-tuple-element.44.diag_ref, f32[8,128]{1,0:T(8,128)S(1)} %get-tuple-element.45.gap_ref, f32[8,128]{1,0:T(8,128)S(1)} %get-tuple-element.46.stiff_ref, ...), custom_call_target="tpu_custom_call" | custom-call | tf_op jit(solution)/shard_map/pallas_call | solution.py:43
  17.1 3.3 %all-to-all-start.1 = ((f32[8,8,128]{2,1,0:T(8,128)}), f32[8,8,128]{2,1,0:T(8,128)S(1)}, u32[]{:S(2)}, u32[]{:S(2)}) async-start(f32[8,8,128]{2,1,0:T(8,128)} %shard_map.106), calls=%async_computation.1 | async-start | bytes 65536 | tf_op jit(solution)/shard_map/all_to_all | solution.py:24
  20.4 0.0 collective-permute-done.2.xu
  20.4 0.0 collective-permute-done.3.xd
  20.4 1.7 %collective-permute-start.4 = (f32[24,256]{1,0:T(8,128)S(1)}, f32[24,256]{1,0:T(8,128)S(1)}, u32[]{:S(2)}, u32[]{:S(2)}) collective-permute-start(f32[24,256]{1,0:T(8,128)S(1)} %get-tuple-element.38), channel_id=1, source_target_pairs={{0,1},{1,2},{2,3},{3,0},{4,5},{5,6},{6,7},{7,4},{8,9},{9,10},{10,1... | collective-permute-start | bytes 73736 | tf_op jit(solution)/shard_map/ppermute | solution.py:18
  22.1 0.0 collective-permute-start.5
  22.1 0.0 collective-permute-done.yu
  22.1 1.5 %shard_map.101 = (f32[16,6,3,2,8,128]{5,4,3,2,1,0:T(8,128)S(1)}, f32[15,3,7,2,8,128]{5,4,3,2,1,0:T(8,128)S(1)}) custom-call(f32[3,16,8,256]{3,2,1,0:T(8,128)S(1)} %get-tuple-element.31.u_ref, f32[3,16,8,256]{3,2,1,0:T(8,128)S(1)} %get-tuple-element.27.v_ref, f32[6,16,8,256]{3,2,1,0:T(8,128)S(1)} %get-tuple-element.28.stress_ref, ...), custom_call_target="tpu_custom_call" | custom-call | tf_op jit(solution)/shard_map/pallas_call | solution.py:43
  23.7 0.0 collective-permute-done.4.corner
  23.7 0.0 collective-permute-done.1.yd
  23.7 0.4 %shard_map.103.edge_ref = f32[3,2,2,24,128]{4,3,2,1,0:T(8,128)S(1)} custom-call(f32[6,16,256]{2,1,0:T(8,128)S(1)} %get-tuple-element.32.ydn, f32[13,16,256]{2,1,0:T(8,128)S(1)} %collective-permute-done.1.yd, f32[48,256]{1,0:T(8,128)S(1)} %collective-permute-done.2.xu, f32[104,256]{1,0:T(8,128)S(1)} %collective-permute-done.3.xd, ...), custom_call_target="tpu_custom_call" | custom-call | tf_op jit(solution)/shard_map/pallas_call | solution.py:43
  24.1 1.5 %collective-permute-done.5.corner = f32[16,256]{1,0:T(8,128)S(1)} collective-permute-done((f32[16,256]{1,0:T(8,128)S(1)}, f32[16,256]{1,0:T(8,128)S(1)}, u32[]{:S(2)}, u32[]{:S(2)}) %collective-permute-start.5) | collective-permute-done | bytes 16416 | tf_op jit(solution)/shard_map/ppermute | solution.py:18
  25.6 1.1 %shard_map.104.base_ref = f32[3,16,8,256]{3,2,1,0:T(8,128)S(1)} custom-call(f32[3,16,8,256]{3,2,1,0:T(8,128)S(1)} %get-tuple-element.27.v_ref, f32[6,16,8,256]{3,2,1,0:T(8,128)S(1)} %get-tuple-element.28.stress_ref, f32[16,8,256]{2,1,0:T(8,128)S(1)} %get-tuple-element.29.hour_ref, f32[16,8,256]{2,1,0:T(8,128)S(1)} %get-tuple-element.30.mass_ref, ...), custom_call_target="tpu_custom_call" | custom-call | tf_op jit(solution)/shard_map/pallas_call | solution.py:43
  26.7 0.0 all-to-all-done.1.table_ref
  26.7 1.0 %shard_map.107 = f32[3,16,8,256]{3,2,1,0:T(8,128)} custom-call(f32[3,16,8,256]{3,2,1,0:T(8,128)S(1)} %shard_map.104.base_ref, f32[16,8,256]{2,1,0:T(8,128)S(1)} %get-tuple-element.30.mass_ref, f32[8,8,128]{2,1,0:T(8,128)S(1)} %all-to-all-done.1.table_ref, s32[2,128]{1,0:T(2,128)S(1)} %get-tuple-element.48.route_ref), custom_call_target="tpu_custom_call" | custom-call | tf_op jit(solution)/shard_map/pallas_call | solution.py:43
  (1 shorter events, 0.0 us)
Async XLA Ops:
  2.2 21.5 %collective-permute-start.1 = (f32[13,16,256]{2,1,0:T(8,128)S(1)}, f32[13,16,256]{2,1,0:T(8,128)S(1)}, u32[]{:S(2)}, u32[]{:S(2)}) collective-permute-start(f32[13,16,256]{2,1,0:T(8,128)S(1)} %get-tuple-element.35), channel_id=1, source_target_pairs={{0,1},{1,2},{2,3},{3,0},{4,5},{5,6},{6,7},{7,4},{8,9},{9,10},{10,1... | collective-permute-start | bytes 638984 | tf_op jit(solution)/shard_map/ppermute | solution.py:18
  4.8 15.6 %collective-permute-start.3 = (f32[104,256]{1,0:T(8,128)}, f32[104,256]{1,0:T(8,128)S(1)}, u32[]{:S(2)}, u32[]{:S(2)}) collective-permute-start(f32[104,256]{1,0:T(8,128)} %get-tuple-element.37), channel_id=1, source_target_pairs={{0,4},{4,8},{8,12},{12,16},{16,20},{20,24},{24,28},{28,0},{1,5},{5... | collective-permute-start | bytes 319496 | tf_op jit(solution)/shard_map/ppermute | solution.py:18
  6.1 9.7 %all-to-all-start = ((f32[8,8,128]{2,1,0:T(8,128)}), f32[8,8,128]{2,1,0:T(8,128)S(1)}, u32[]{:S(2)}, u32[]{:S(2)}) async-start(f32[8,8,128]{2,1,0:T(8,128)} %get-tuple-element.40), calls=%async_computation | async-start | bytes 65536 | tf_op jit(solution)/shard_map/all_to_all | solution.py:24
  10.9 11.2 %collective-permute-start = (f32[6,16,256]{2,1,0:T(8,128)S(1)}, f32[6,16,256]{2,1,0:T(8,128)S(1)}, u32[]{:S(2)}, u32[]{:S(2)}) collective-permute-start(f32[6,16,256]{2,1,0:T(8,128)S(1)} %get-tuple-element.32.ydn), channel_id=1, source_target_pairs={{0,3},{1,0},{2,1},{3,2},{4,7},{5,4},{6,5},{7,6},{8,11},{9,8},{10,9... | collective-permute-start | bytes 294920 | tf_op jit(solution)/shard_map/ppermute | solution.py:18
  10.9 9.4 %collective-permute-start.2 = (f32[48,256]{1,0:T(8,128)}, f32[48,256]{1,0:T(8,128)S(1)}, u32[]{:S(2)}, u32[]{:S(2)}) collective-permute-start(f32[48,256]{1,0:T(8,128)} %get-tuple-element.36), channel_id=1, source_target_pairs={{0,28},{4,0},{8,4},{12,8},{16,12},{20,16},{24,20},{28,24},{1,29},{... | collective-permute-start | bytes 147464 | tf_op jit(solution)/shard_map/ppermute | solution.py:18
  17.1 9.7 %all-to-all-start.1 = ((f32[8,8,128]{2,1,0:T(8,128)}), f32[8,8,128]{2,1,0:T(8,128)S(1)}, u32[]{:S(2)}, u32[]{:S(2)}) async-start(f32[8,8,128]{2,1,0:T(8,128)} %shard_map.106), calls=%async_computation.1 | async-start | bytes 65536 | tf_op jit(solution)/shard_map/all_to_all | solution.py:24
  20.4 3.2 %collective-permute-start.4 = (f32[24,256]{1,0:T(8,128)S(1)}, f32[24,256]{1,0:T(8,128)S(1)}, u32[]{:S(2)}, u32[]{:S(2)}) collective-permute-start(f32[24,256]{1,0:T(8,128)S(1)} %get-tuple-element.38), channel_id=1, source_target_pairs={{0,1},{1,2},{2,3},{3,0},{4,5},{5,6},{6,7},{7,4},{8,9},{9,10},{10,1... | collective-permute-start | bytes 73736 | tf_op jit(solution)/shard_map/ppermute | solution.py:18
  22.1 3.5 %collective-permute-start.5 = (f32[16,256]{1,0:T(8,128)S(1)}, f32[16,256]{1,0:T(8,128)S(1)}, u32[]{:S(2)}, u32[]{:S(2)}) collective-permute-start(f32[16,256]{1,0:T(8,128)S(1)} %get-tuple-element.39), channel_id=1, source_target_pairs={{0,3},{1,0},{2,1},{3,2},{4,7},{5,4},{6,5},{7,6},{8,11},{9,8},{10,9... | collective-permute-start | bytes 49160 | tf_op jit(solution)/shard_map/ppermute | solution.py:18
